TPU v7x, 32 devices: a whole 2x2x4 slice. The times are simulated.
32 devices in a mesh: expert: 2 (over x), dp: 16 (over z, y, core).
Axes of the slice: x: 2, y: 2, z: 4, core: 2. Of those that a mesh axis runs over, the one named last changes fastest.
Arguments:
- upstream: bfloat16 [4096, 3584], P(('expert', 'dp')), may hold values from -2.5 to 2.5
- combine_weights: bfloat16 [4096, 2], P(('expert', 'dp')), may hold values from 0.099609375 to 1
- expert_ids: int32 [4096, 2], P(('expert', 'dp')), may hold values from 0 to 1, as said below
- saved_hidden: bfloat16 [2, 4096, 2048], P('expert', 'dp'), may hold values from -6 to 6
- down_weight: bfloat16 [2, 1024, 3584], P('expert'), may hold values from -0.1875 to 0.1875
Outputs:
- grad_down: float32 [2, 3584, 1024], P('expert', 'dp')
- grad_hidden: bfloat16 [2, 4096, 2048], P('expert', 'dp')
- grad_probs: float32 [4096, 2], P(('expert', 'dp'))
Inputs may be any that keep to these rules, and one draw needn't show every extreme that they name: `expert_ids`: the 2 ids of a token differ. Among the 128 tokens of one device no expert is named more than 128 times, and in every draw one expert is named exactly 128 times by the tokens of every device.
All inputs are finite; a program needn't handle non-finite values.
Results may differ from a plain program's by a relative error of at most 0.0049.
Values may be sent and summed in bfloat16 or wider, within the bound.
No kernel may reach another device: no remote copies, remote signals or barrier semaphores. Data moves between devices by JAX's collectives and lax.ppermute only.
A program may use at most 128 MiB of HBM per device.

v0:
```python
import jax
import jax.numpy as jnp
from jax import lax
from jax.sharding import PartitionSpec as P


def contract_rows(left_rows, right_rows):
    return lax.dot_general(
        left_rows, right_rows, (((0,), (0,)), ((), ())), preferred_element_type=jnp.float32
    )


def local(upstream, combine_weights, expert_ids, saved_hidden, down_weight):
    tok_rows, features = upstream.shape
    experts = lax.axis_size("expert")
    hidden_units = down_weight.shape[1]
    capacity = saved_hidden.shape[1] // experts
    labels = lax.broadcasted_iota(jnp.int32, (1, 1, experts), 2)
    matched = expert_ids[:, :, None] == labels
    member = jnp.sum(matched.astype(jnp.int32), axis=1)
    slot_rank = jnp.cumsum(member, axis=0) - member
    token_iota = lax.broadcasted_iota(jnp.int32, (tok_rows, experts, capacity), 0)
    slot_iota = lax.broadcasted_iota(jnp.int32, (tok_rows, experts, capacity), 2)
    placed = (member[:, :, None] == 1) & (slot_rank[:, :, None] == slot_iota)
    source = jnp.sum(jnp.where(placed, token_iota, 0), axis=0)
    filled = jnp.any(placed, axis=0)
    token_weight = jnp.sum(
        jnp.where(matched, combine_weights[:, :, None].astype(jnp.float32), 0.0), axis=1
    )
    send_rows = jnp.where(filled[:, :, None], upstream[source], jnp.zeros((), jnp.bfloat16))
    send_weight = jnp.where(
        filled, jnp.take_along_axis(token_weight.T, source, axis=1), 0.0
    ).astype(jnp.bfloat16)
    got_rows, got_weight = (
        lax.all_to_all(send_rows, "expert", split_axis=0, concat_axis=0, tiled=True),
        lax.all_to_all(send_weight, "expert", split_axis=0, concat_axis=0, tiled=True),
    )
    routed = got_rows.reshape(experts * capacity, features)
    row_weight = got_weight.reshape(experts * capacity, 1).astype(jnp.float32)
    stored = saved_hidden[0]
    gate_pre = stored[:, :hidden_units].astype(jnp.float32)
    up_pre = stored[:, hidden_units:].astype(jnp.float32)
    sigmoid_gate = jax.nn.sigmoid(gate_pre)
    activated = (gate_pre * sigmoid_gate * up_pre).astype(jnp.bfloat16)
    scaled = (row_weight * routed.astype(jnp.float32)).astype(jnp.bfloat16)
    weights = down_weight[0]
    backward = lax.dot_general(
        routed, weights, (((1,), (1,)), ((), ())), preferred_element_type=jnp.float32
    )
    grad_act = row_weight * backward
    grad_gate = grad_act * up_pre * sigmoid_gate * (1.0 + gate_pre * (1.0 - sigmoid_gate))
    grad_up = grad_act * gate_pre * sigmoid_gate
    grad_hidden = jnp.concatenate([grad_gate, grad_up], axis=1).astype(jnp.bfloat16)
    outputs = jnp.dot(activated, weights, preferred_element_type=jnp.float32)
    scores = jnp.sum(routed.astype(jnp.float32) * outputs, axis=1)
    returned = lax.all_to_all(
        scores.reshape(experts, capacity), "expert", split_axis=0, concat_axis=0, tiled=True
    )
    slot_of = jnp.sum(jnp.where(matched, slot_rank[:, None, :], 0), axis=2)
    flat_index = expert_ids * capacity + slot_of
    score_table = returned.reshape(experts * capacity)
    cell_ids = lax.broadcasted_iota(jnp.int32, (1, 1, experts * capacity), 2)
    grad_probs = jnp.sum(
        jnp.where(flat_index[:, :, None] == cell_ids, score_table[None, None, :], 0.0), axis=2
    )
    grad_down = lax.psum_scatter(
        contract_rows(scaled, activated), "dp", scatter_dimension=0, tiled=True
    )
    return (grad_down[None], grad_hidden[None], grad_probs)


def solution(mesh):
    return jax.shard_map(
        local,
        mesh=mesh,
        in_specs=(
            P(("expert", "dp"), None),
            P(("expert", "dp"), None),
            P(("expert", "dp"), None),
            P("expert", "dp", None),
            P("expert", None, None),
        ),
        out_specs=(P("expert", "dp", None), P("expert", "dp", None), P(("expert", "dp"), None)),
        check_vma=False,
    )
```

profile of v0, /device:TPU:0, one launch (start us, length us, event | category | flops | bytes accessed | tf_op | source)
XLA Modules:
  0.0 212.7 jit_solution(13656522340395950082)
XLA Ops:
  7.2 0.0 copy-start
  7.2 0.8 convert_reduce_fusion
  8.0 0.1 copy.21
  8.1 0.2 reduce_window_sum.11
  8.3 0.1 copy.23
  8.3 0.2 select_reduce_fusion.1
  8.5 0.1 fusion.30
  8.7 0.7 convert_element_type.53
  9.3 0.7 select_reduce_fusion.3
  10.0 0.1 copy.24
  10.1 2.4 %gather_fusion.1 = bf16[256]{0:T(256)(128)(2,1)S(1)} fusion(bf16[2,128]{0,1:T(8,128)(2,1)S(1)} %bitcast.48, s32[256]{0:T(256)S(1)} %get-tuple-element.5), kind=kCustom, calls=%fused_computation.1 | custom fusion | bytes 3072 | tf_op jit(solution)/shard_map/jit(take_along_axis)/gather | solution.py:32
  12.6 0.6 copy.25
  13.2 4.2 %all-to-all-start = ((bf16[2,1,128]{2,1,0:T(2,128)(2,1)}), bf16[2,1,128]{2,1,0:T(2,128)(2,1)S(1)}, u32[]{:S(2)}, u32[]{:S(2)}) async-start(bf16[2,1,128]{2,1,0:T(2,128)(2,1)} %copy.25), calls=%async_computation | async-start | bytes 2048 | tf_op jit(solution)/shard_map/all_to_all | solution.py:36
  17.4 0.0 copy-done
  17.4 1.7 gather_fusion
  19.1 1.4 broadcast_select_fusion
  20.5 0.5 all-to-all-done
  21.0 3.7 %all-to-all-start.1 = ((bf16[2,128,3584]{2,1,0:T(8,128)(2,1)}), bf16[2,128,3584]{2,1,0:T(8,128)(2,1)S(1)}, u32[]{:S(2)}, u32[]{:S(2)}) async-start(bf16[2,128,3584]{2,1,0:T(8,128)(2,1)} %broadcast_select_fusion), calls=%async_computation.1 | async-start | bytes 3670016 | tf_op jit(solution)/shard_map/all_to_all | solution.py:35
  24.8 0.0 reduce-scatter.2.cloned.1.call-start
  24.8 21.9 %all-to-all-done.1 = bf16[2,128,3584]{2,1,0:T(8,128)(2,1)S(1)} async-done(((bf16[2,128,3584]{2,1,0:T(8,128)(2,1)}), bf16[2,128,3584]{2,1,0:T(8,128)(2,1)S(1)}, u32[]{:S(2)}, u32[]{:S(2)}) %all-to-all-start.1) | async-done | bytes 1835040 | tf_op jit(solution)/shard_map/all_to_all | solution.py:35
  46.8 8.7 %fusion.8 = f32[3584,1024]{1,0:T(8,128)} fusion(bf16[256,3584]{1,0:T(8,128)(2,1)S(1)} %bitcast.49, f32[256]{0:T(256)S(1)} %bitcast.56, bf16[256,2048]{1,0:T(8,128)(2,1)} %bitcast.53), kind=kOutput, calls=%fused_computation.9 | convolution fusion | flops 1883897856 | bytes 17564672 | tf_op jit(solution)/shard_map/dot_general | solution.py:8
  55.5 0.0 copy-start.1
  55.5 0.0 reduce-scatter.2.cloned.1.call-update
  55.5 0.7 copy-done.1
  56.2 6.3 %fusion.11 = f32[256]{0:T(256)} fusion(bf16[1,1024,3584]{2,1,0:T(8,128)(2,1)} %param.9, bf16[256,3584]{1,0:T(8,128)(2,1)S(1)} %bitcast.50, bf16[256,2048]{1,0:T(8,128)(2,1)} %bitcast.54), kind=kOutput, calls=%fused_computation.16 | convolution fusion | flops 1883897600 | bytes 10224640 | tf_op jit(solution)/shard_map/dot_general | solution.py:54
  62.4 3.2 %all-to-all-start.2 = ((f32[2,1,128]{2,1,0:T(1,128)}), f32[2,1,128]{2,1,0:T(1,128)S(1)}, u32[]{:S(2)}, u32[]{:S(2)}) async-start(f32[2,1,128]{2,1,0:T(1,128)} %bitcast.15), calls=%async_computation.3 | async-start | bytes 2048 | tf_op jit(solution)/shard_map/all_to_all | solution.py:56
  65.7 7.0 %fusion.28 = (bf16[1,256,1024]{2,1,0:T(8,128)(2,1)S(1)}, bf16[1,256,1024]{2,1,0:T(8,128)(2,1)S(1)}) fusion(bf16[256,2048]{1,0:T(8,128)(2,1)} %bitcast.55, bf16[256,3584]{1,0:T(8,128)(2,1)S(1)} %bitcast.51, bf16[1,1024,3584]{2,1,0:T(8,128)(2,1)} %param.9, f32[256]{0:T(256)S(1)} %bitcast.57), kind=kOutput, calls=%fused_computation.32 | convolution fusion | flops 1883242496 | bytes 11273216 | tf_op jit(solution)/shard_map/dot_general | solution.py:47
  72.7 1.1 pad_maximum_fusion
  73.7 0.0 all-to-all-done.2
  73.7 0.7 select_reduce_fusion
  74.5 131.4 %reduce-scatter.2.cloned.1.call-done = f32[224,1024]{1,0:T(8,128)} async-done(((f32[3584,1024]{1,0:T(8,128)}), f32[224,1024]{1,0:T(8,128)}) %reduce-scatter.2.cloned.1.call-update) | async-done | bytes 917520 | tf_op jit(solution)/shard_map/reduce_scatter | solution.py:66
  (8 shorter events, 0.1 us)
Async XLA Ops:
  7.2 10.2 %copy-start = (bf16[128,3584]{1,0:T(8,128)(2,1)S(1)}, bf16[128,3584]{1,0:T(8,128)(2,1)}, u32[]{:S(2)}) copy-start(bf16[128,3584]{1,0:T(8,128)(2,1)} %param.5) | copy-start | bytes 2752516
  13.2 7.9 %all-to-all-start = ((bf16[2,1,128]{2,1,0:T(2,128)(2,1)}), bf16[2,1,128]{2,1,0:T(2,128)(2,1)S(1)}, u32[]{:S(2)}, u32[]{:S(2)}) async-start(bf16[2,1,128]{2,1,0:T(2,128)(2,1)} %copy.25), calls=%async_computation | async-start | bytes 2048 | tf_op jit(solution)/shard_map/all_to_all | solution.py:36
  21.0 25.7 %all-to-all-start.1 = ((bf16[2,128,3584]{2,1,0:T(8,128)(2,1)}), bf16[2,128,3584]{2,1,0:T(8,128)(2,1)S(1)}, u32[]{:S(2)}, u32[]{:S(2)}) async-start(bf16[2,128,3584]{2,1,0:T(8,128)(2,1)} %broadcast_select_fusion), calls=%async_computation.1 | async-start | bytes 3670016 | tf_op jit(solution)/shard_map/all_to_all | solution.py:35
  24.8 181.1 %reduce-scatter.2.cloned.1.call-start = ((), (), s32[]{:S(2)}) async-start(), calls=%async_computation.4 | async-start | bytes 15597568 | tf_op jit(solution)/shard_map/reduce_scatter | solution.py:66
  55.5 0.7 copy-start.1
  62.4 11.3 %all-to-all-start.2 = ((f32[2,1,128]{2,1,0:T(1,128)}), f32[2,1,128]{2,1,0:T(1,128)S(1)}, u32[]{:S(2)}, u32[]{:S(2)}) async-start(f32[2,1,128]{2,1,0:T(1,128)} %bitcast.15), calls=%async_computation.3 | async-start | bytes 2048 | tf_op jit(solution)/shard_map/all_to_all | solution.py:56
Sparse Core Ops, SparseCore 0:
  55.6 150.1 reduce-scatter.1
where the time goes:
time: 213 us
  waiting for transfers between devices  154 us (72%)
  matrix products  22 us (10%)
  between operations  14.1 us (7%)
  starting transfers between devices  11.2 us (5%)
  other arithmetic  5.93 us (3%)
  local copies, waits for them, and re-layouts  5.68 us (3%)
    reduce_scatter x1, waiting for transfers between devices, local(): lax.psum_scatter(contract_rows(scaled, activated), 'dp', scatter_dimensio...  131 us
    all_to_all x1, waiting for transfers between devices, local(): lax.all_to_all(send_rows, 'expert', split_axis=0, concat_axis=0, tiled=True)  21.9 us
    dot_general x1, matrix products, contract_rows(): lax.dot_general(left_rows, right_rows, (((0,), (0,)), ((), ())), preferre...  8.72 us
    dot_general x1, matrix products, local(): lax.dot_general(routed, weights, (((1,), (1,)), ((), ())), preferred_elem...  7.01 us
    dot_general x1, matrix products, local(): outputs = jnp.dot(activated, weights, preferred_element_type=jnp.float32)  6.26 us
  transfers between devices with their start and end apart: 4, of which 3 were waited for; matrix products, arithmetic and copies ran while one was open for 9% of the time, Pallas kernels for 0%

commit v1 on v0

--- a/solution.py
+++ b/solution.py
@@ -1,7 +1,15 @@
+import functools
+
 import jax
 import jax.numpy as jnp
 from jax import lax
+from jax.experimental import pallas as pl
+from jax.experimental.pallas import tpu as pltpu
 from jax.sharding import PartitionSpec as P
+
+INNER = 4
+LANES = 128
+VMEM = pl.BlockSpec(memory_space=pltpu.VMEM)
 
 
 def contract_rows(left_rows, right_rows):
@@ -10,7 +18,197 @@
     )
 
 
-def local(upstream, combine_weights, expert_ids, saved_hidden, down_weight):
+def call(kernel, outs, *args, scratch=()):
+    return pl.pallas_call(
+        kernel,
+        out_shape=outs,
+        in_specs=[VMEM] * len(args),
+        out_specs=jax.tree.map(lambda _: VMEM, outs),
+        scratch_shapes=list(scratch),
+        compiler_params=pltpu.CompilerParams(vmem_limit_bytes=48 << 20),
+    )(*args)
+
+
+def token_weight(ids_ref, weights_ref, expert):
+    picked = jnp.where(ids_ref[...] == expert, weights_ref[...].astype(jnp.float32), 0.0)
+    return jnp.sum(picked, axis=1, keepdims=True)
+
+
+def chunk_start(k, chunk):
+    group = lax.axis_index("dp") // INNER
+    return pl.multiple_of((group ^ k) * chunk, LANES)
+
+
+def first_kernel(k, chunk, up_ref, ids_ref, weights_ref, out_ref):
+    out_ref[:, :chunk] = up_ref[:, pl.ds(chunk_start(k, chunk), chunk)]
+    weight = token_weight(ids_ref, weights_ref, 1 - lax.axis_index("expert"))
+    out_ref[:, chunk:] = jnp.broadcast_to(weight, (weight.shape[0], LANES)).astype(jnp.bfloat16)
+
+
+def own_kernel(outer, chunk, up_ref, ids_ref, weights_ref, *outs):
+    own_refs, send_refs = outs[:outer], outs[outer:]
+    weight = token_weight(ids_ref, weights_ref, lax.axis_index("expert"))
+    for k in range(outer):
+        rows = up_ref[:, pl.ds(chunk_start(k, chunk), chunk)]
+        if k < outer - 1:
+            send_refs[k][...] = rows
+        scaled = (weight * rows.astype(jnp.float32)).astype(jnp.bfloat16)
+        own_refs[k][...] = scaled.T
+
+
+def act_kernel(hidden_ref, out_ref):
+    rows, hidden_units = out_ref.shape
+    half = rows // 2
+    expert = lax.axis_index("expert")
+    for part in range(2):
+        source = pl.ds(pl.multiple_of((expert ^ part) * half, half), half)
+        gate = hidden_ref[source, :hidden_units].astype(jnp.float32)
+        up = hidden_ref[source, hidden_units:].astype(jnp.float32)
+        act = gate * jax.nn.sigmoid(gate) * up
+        out_ref[part * half : (part + 1) * half, :] = act.astype(jnp.bfloat16)
+
+
+def split_kernel(chunk, got_ref, first_ref, own_ref, *refs):
+    pays, scaled_ref = refs[:INNER], refs[INNER]
+    weight = first_ref[:, chunk : chunk + 1].astype(jnp.float32)
+    scaled = (weight * got_ref[:, :chunk].astype(jnp.float32)).astype(jnp.bfloat16)
+    scaled_ref[...] = scaled.T
+    piece = chunk // INNER
+    mine = lax.axis_index("dp") % INNER
+    for j in range(INNER):
+        rows = pl.ds(pl.multiple_of((mine ^ j) * piece, 16), piece)
+        pays[j][:, :LANES] = own_ref[rows, :]
+        pays[j][:, LANES:] = scaled_ref[rows, :]
+
+
+def partial_kernel(*refs):
+    pays, acts, adds, out_ref = refs[:INNER], refs[INNER : 2 * INNER], refs[2 * INNER : -1], refs[-1]
+    total = None
+    for pay, act in zip(pays, acts):
+        term = jnp.dot(pay[...], act[...], preferred_element_type=jnp.float32)
+        total = term if total is None else total + term
+    for add in adds:
+        total = total + add[...].astype(jnp.float32)
+    out_ref[...] = total.astype(out_ref.dtype)
+
+
+def hidden_kernel(outer, chunk, up_ref, ids_ref, weights_ref, hidden_ref, w_ref, *refs):
+    got_refs, out_ref, own_score, got_score = refs[:outer], refs[outer], refs[outer + 1], refs[outer + 2]
+    step = pl.program_id(0)
+    half = up_ref.shape[0]
+    width = w_ref.shape[0]
+    hidden_units = hidden_ref.shape[1] // 2
+    expert = lax.axis_index("expert")
+    last = got_refs[outer - 1]
+
+    @pl.when(step == 0)
+    def _():
+        own_score[...] = jnp.zeros_like(own_score)
+        got_score[...] = jnp.zeros_like(got_score)
+
+    def finish(backward, weight, part, score):
+        rows = pl.ds(pl.multiple_of((expert ^ part) * half, half), half)
+        gate_cols = pl.ds(pl.multiple_of(step * width, LANES), width)
+        up_cols = pl.ds(pl.multiple_of(hidden_units + step * width, LANES), width)
+        gate = hidden_ref[rows, gate_cols].astype(jnp.float32)
+        up = hidden_ref[rows, up_cols].astype(jnp.float32)
+        sig = jax.nn.sigmoid(gate)
+        act = (gate * sig * up).astype(jnp.bfloat16).astype(jnp.float32)
+        score[...] += jnp.sum(backward * act, axis=1, keepdims=True)
+        grad = weight * backward
+        out_ref[rows, gate_cols] = (grad * up * sig * (1.0 + gate * (1.0 - sig))).astype(jnp.bfloat16)
+        out_ref[rows, up_cols] = (grad * gate * sig).astype(jnp.bfloat16)
+
+    turned = (((1,), (1,)), ((), ()))
+    own = lax.dot_general(up_ref[...], w_ref[...], turned, preferred_element_type=jnp.float32)
+    finish(own, token_weight(ids_ref, weights_ref, expert), 0, own_score)
+    got = None
+    for k in range(outer):
+        cols = w_ref[:, pl.ds(chunk_start(k, chunk), chunk)]
+        term = lax.dot_general(got_refs[k][:, :chunk], cols, turned, preferred_element_type=jnp.float32)
+        got = term if got is None else got + term
+    finish(got, last[:, chunk : chunk + 1].astype(jnp.float32), 1, got_score)
+
+
+def hidden_call(outer, chunk, upstream, ids, combine, stored, weights, got):
+    tokens, features = upstream.shape
+    hidden_units = weights.shape[0]
+    width = 256
+    whole = lambda a: pl.BlockSpec(a.shape, lambda i: (0, 0))
+    column = jax.ShapeDtypeStruct((tokens, 1), jnp.float32)
+    return pl.pallas_call(
+        functools.partial(hidden_kernel, outer, chunk),
+        grid=(hidden_units // width,),
+        out_shape=(jax.ShapeDtypeStruct(stored.shape, jnp.bfloat16), column, column),
+        in_specs=[whole(upstream), whole(ids), whole(combine), whole(stored)]
+        + [pl.BlockSpec((width, features), lambda i: (i, 0))]
+        + [whole(g) for g in got],
+        out_specs=(whole(stored), whole(column), whole(column)),
+        compiler_params=pltpu.CompilerParams(vmem_limit_bytes=48 << 20),
+    )(upstream, ids, combine, stored, weights, *got)
+
+
+def both_experts(upstream, combine_weights, expert_ids, saved_hidden, down_weight):
+    tokens, features = upstream.shape
+    n = lax.axis_size("dp")
+    outer = n // INNER
+    chunk, piece = features // outer, features // n
+    hidden_units = down_weight.shape[1]
+    stored, weights = saved_hidden[0], down_weight[0]
+    bf16 = lambda *shape: jax.ShapeDtypeStruct(shape, jnp.bfloat16)
+    flip = [(0, 1), (1, 0)]
+    swap = lambda bit: [(i, i ^ bit) for i in range(n)]
+
+    top = outer - 1
+    first = call(
+        functools.partial(first_kernel, top, chunk),
+        bf16(tokens, chunk + LANES), upstream, expert_ids, combine_weights,
+    )
+    got = {top: lax.ppermute(first, "expert", flip)}
+    act = {0: call(act_kernel, bf16(stored.shape[0], hidden_units), stored)}
+    act[2] = lax.ppermute(act[0], "dp", swap(2))
+    own = call(
+        functools.partial(own_kernel, outer, chunk),
+        (bf16(chunk, tokens),) * outer + (bf16(tokens, chunk),) * top,
+        upstream, expert_ids, combine_weights,
+    )
+    own, send = own[:outer], own[outer:]
+    for k in range(top - 1, -1, -1):
+        got[k] = lax.ppermute(send[k], "expert", flip)
+    act[1] = lax.ppermute(act[0], "dp", swap(1))
+    act[3] = lax.ppermute(act[2], "dp", swap(1))
+
+    adds = {k: [] for k in range(outer)}
+    for k in range(top, -1, -1):
+        pays = call(
+            functools.partial(split_kernel, chunk),
+            (bf16(piece, 2 * tokens),) * INNER, got[k], got[top], own[k],
+            scratch=[pltpu.VMEM((chunk, tokens), jnp.bfloat16)],
+        )
+        pays = [pays[0]] + [lax.ppermute(pays[j], "dp", swap(j)) for j in range(1, INNER)]
+        kind = jnp.bfloat16 if k else jnp.float32
+        terms = adds[k] if k else []
+        part = call(
+            partial_kernel, jax.ShapeDtypeStruct((piece, hidden_units), kind),
+            *pays, *[act[j] for j in range(INNER)], *terms,
+        )
+        if k:
+            bit = k & -k
+            adds[k ^ bit].append(lax.ppermute(part, "dp", swap(bit * INNER)))
+    grad_down = part
+    for term in adds[0]:
+        grad_down = grad_down + term.astype(jnp.float32)
+
+    grad_hidden, own_score, got_score = hidden_call(
+        outer, chunk, upstream, expert_ids, combine_weights, stored, weights,
+        [got[k] for k in range(outer)],
+    )
+    back_score = lax.ppermute(got_score, "expert", flip)
+    grad_probs = jnp.where(expert_ids == lax.axis_index("expert"), own_score, back_score)
+    return grad_down[None], grad_hidden[None], grad_probs
+
+
+def any_experts(upstream, combine_weights, expert_ids, saved_hidden, down_weight):
     tok_rows, features = upstream.shape
     experts = lax.axis_size("expert")
     hidden_units = down_weight.shape[1]
@@ -69,6 +267,22 @@
     return (grad_down[None], grad_hidden[None], grad_probs)
 
 
+def local(upstream, combine_weights, expert_ids, saved_hidden, down_weight):
+    tokens, features = upstream.shape
+    n = lax.axis_size("dp")
+    outer = n // INNER
+    every_token_to_both = (
+        lax.axis_size("expert") == 2
+        and expert_ids.shape[1] == 2
+        and saved_hidden.shape[1] == 2 * tokens
+        and tokens == LANES
+    )
+    splits = n % INNER == 0 and outer & (outer - 1) == 0 and features % (n * 16) == 0
+    if every_token_to_both and splits and (features // max(outer, 1)) % LANES == 0:
+        return both_experts(upstream, combine_weights, expert_ids, saved_hidden, down_weight)
+    return any_experts(upstream, combine_weights, expert_ids, saved_hidden, down_weight)
+
+
 def solution(mesh):
     return jax.shard_map(
         local,

time: 213 us -> 94.7 us (0.44)
  waiting for transfers between devices: 154 us -> 40.7 us
  matrix products: 22 us -> 0 us
  Pallas kernels: 0 us -> 15.1 us
  starting transfers between devices: 11.2 us -> 24.6 us
  between operations: 14.1 us -> 0.79 us
  local copies, waits for them, and re-layouts: 5.68 us -> 10.1 us
  other arithmetic: 5.93 us -> 3.06 us
    reduce_scatter x1 -> x0, waiting for transfers between devices: 131 us -> none  [local(): lax.psum_scatter(contract_rows(scaled, activated), 'dp', scatter_dimensio...]
    ppermute x0 -> x23, waiting for transfers between devices: none -> 40.7 us  [the longest x12 13.2 us: both_experts(): lax.ppermute(pays[j], 'dp', swap(j))]
    ppermute x0 -> x23, starting transfers between devices: none -> 24.6 us  [the longest x12 8.74 us: both_experts(): lax.ppermute(pays[j], 'dp', swap(j))]
    all_to_all x3 -> x0, waiting for transfers between devices: 22.4 us -> none  [the longest x1 21.9 us: local(): lax.all_to_all(send_rows, 'expert', split_axis=0, concat_axis=0, tiled=True)]
    dot_general x3 -> x0, matrix products: 22 us -> none  [the longest x1 8.72 us: contract_rows(): lax.dot_general(left_rows, right_rows, (((0,), (0,)), ((), ())), preferre...]
    pallas_call x0 -> x12, Pallas kernels: none -> 15.1 us  [the longest x1 8.05 us: hidden_call(): pl.pallas_call(functools.partial(hidden_kernel, outer, chunk), grid=(hidd...]
    all_to_all x3 -> x0, starting transfers between devices: 11.1 us -> none  [the longest x1 4.21 us: local(): lax.all_to_all(send_weight, 'expert', split_axis=0, concat_axis=0, tiled=...]
    unnamed x4 -> x24, local copies, waits for them, and re-layouts: 0.66 us -> 10.1 us
  transfers between devices with their start and end apart: 4 -> 23, of which waited for: 3 -> 10; matrix products, arithmetic and copies ran while one was open for 9% -> 2% of each run, Pallas kernels for 0% -> 16%
where the time goes in v1:
time: 94.7 us; the launch traced here: 94.3 us
  waiting for transfers between devices  40.7 us (43%)
  starting transfers between devices  24.6 us (26%)
  Pallas kernels  15.1 us (16%)
  local copies, waits for them, and re-layouts  10.1 us (11%)
  other arithmetic  3.06 us (3%)
    ppermute x12, waiting for transfers between devices, both_experts(): lax.ppermute(pays[j], 'dp', swap(j))  13.2 us
    ppermute x1, waiting for transfers between devices, both_experts(): act[2] = lax.ppermute(act[0], 'dp', swap(2))  11.9 us
    unnamed x24, local copies, waits for them, and re-layouts  10.1 us
    ppermute x3, waiting for transfers between devices, both_experts(): got[k] = lax.ppermute(send[k], 'expert', flip)  10 us
    ppermute x12, starting transfers between devices, both_experts(): lax.ppermute(pays[j], 'dp', swap(j))  8.74 us
    pallas_call x1, Pallas kernels, hidden_call(): pl.pallas_call(functools.partial(hidden_kernel, outer, chunk), grid=(hidd...  8.05 us
    pallas_call x11, Pallas kernels, call(): pl.pallas_call(kernel, out_shape=outs, in_specs=[VMEM] * len(args), out_s...  7.08 us
    ppermute x1, waiting for transfers between devices, both_experts(): got = {top: lax.ppermute(first, 'expert', flip)}  5.56 us
  transfers between devices with their start and end apart: 23, of which 10 were waited for; matrix products, arithmetic and copies ran while one was open for 2% of the time, Pallas kernels for 16%

profile of v1, /device:TPU:0, one launch (start us, length us, event | category | flops | bytes accessed | tf_op | source)
XLA Modules:
  0.0 94.3 jit_solution(306873321821645429)
XLA Ops:
  0.6 0.0 copy-start.2
  0.6 1.2 %copy-done.2 = bf16[1,256,2048]{2,1,0:T(8,128)(2,1)S(1)} copy-done((bf16[1,256,2048]{2,1,0:T(8,128)(2,1)S(1)}, bf16[1,256,2048]{2,1,0:T(8,128)(2,1)}, u32[]{:S(2)}) %copy-start.2) | copy-done | bytes 1048600
  1.9 0.2 shard_map.79.refs_4_
  2.1 3.0 %collective-permute-start.6 = (bf16[256,1024]{1,0:T(8,128)(2,1)S(1)}, bf16[256,1024]{1,0:T(8,128)(2,1)S(1)}, u32[]{:S(2)}, u32[]{:S(2)}) collective-permute-start(bf16[256,1024]{1,0:T(8,128)(2,1)S(1)} %shard_map.79.refs_4_), channel_id=1, source_target_pairs={{0,2},{1,3},{2,0},{3,1},{4,6},{5,7},{6,4},{7,5},{8,10},{9,11},{10,... | collective-permute-start | bytes 1572872 | tf_op jit(solution)/shard_map/ppermute | solution.py:169
  5.1 0.0 collective-permute-start.5
  5.1 11.9 %collective-permute-done.6.refs_6_ = bf16[256,1024]{1,0:T(8,128)(2,1)S(1)} collective-permute-done((bf16[256,1024]{1,0:T(8,128)(2,1)S(1)}, bf16[256,1024]{1,0:T(8,128)(2,1)S(1)}, u32[]{:S(2)}, u32[]{:S(2)}) %collective-permute-start.6) | collective-permute-done | bytes 524320 | tf_op jit(solution)/shard_map/ppermute | solution.py:169
  17.0 0.0 collective-permute-start.7
  17.0 0.8 copy.14.ids_ref
  17.8 0.8 copy.15.weights_ref
  18.6 1.2 %copy-done = bf16[128,3584]{1,0:T(8,128)(2,1)S(1)} copy-done((bf16[128,3584]{1,0:T(8,128)(2,1)S(1)}, bf16[128,3584]{1,0:T(8,128)(2,1)}, u32[]{:S(2)}) %copy-start) | copy-done | bytes 917528
  19.8 0.1 shard_map.77
  19.9 1.8 %collective-permute-start.1 = (bf16[128,1024]{1,0:T(8,128)(2,1)S(1)}, bf16[128,1024]{1,0:T(8,128)(2,1)S(1)}, u32[]{:S(2)}, u32[]{:S(2)}) collective-permute-start(bf16[128,1024]{1,0:T(8,128)(2,1)S(1)} %shard_map.77), channel_id=1, source_target_pairs={{0,16},{16,0},{1,17},{17,1},{2,18},{18,2},{3,19},{19,3},{4,20},{20... | collective-permute-start | bytes 786440 | tf_op jit(solution)/shard_map/ppermute | solution.py:167
  21.7 0.8 shard_map.76
  22.4 0.7 copy-done.8
  23.1 5.6 %collective-permute-done.1.first_ref.got_ref.refs_3_ = bf16[128,1024]{1,0:T(8,128)(2,1)S(1)} collective-permute-done((bf16[128,1024]{1,0:T(8,128)(2,1)S(1)}, bf16[128,1024]{1,0:T(8,128)(2,1)S(1)}, u32[]{:S(2)}, u32[]{:S(2)}) %collective-permute-start.1) | collective-permute-done | bytes 262176 | tf_op jit(solution)/shard_map/ppermute | solution.py:167
  28.7 0.2 shard_map.82
  28.9 0.1 collective-permute-start.12
  29.0 1.8 %collective-permute-start.13 = (bf16[224,256]{1,0:T(8,128)(2,1)S(1)}, bf16[224,256]{1,0:T(8,128)(2,1)S(1)}, u32[]{:S(2)}, u32[]{:S(2)}) collective-permute-start(bf16[224,256]{1,0:T(8,128)(2,1)S(1)} %get-tuple-element.44), channel_id=1, source_target_pairs={{0,2},{1,3},{2,0},{3,1},{4,6},{5,7},{6,4},{7,5},{8,10},{9,11},{10,... | collective-permute-start | bytes 344072 | tf_op jit(solution)/shard_map/ppermute | solution.py:188
  30.8 0.1 collective-permute-start.14
  30.9 0.0 collective-permute-done.12.refs_1_
  30.9 1.7 %collective-permute-start.17 = (bf16[128,896]{1,0:T(8,128)(2,1)S(1)}, bf16[128,896]{1,0:T(8,128)(2,1)S(1)}, u32[]{:S(2)}, u32[]{:S(2)}) collective-permute-start(bf16[128,896]{1,0:T(8,128)(2,1)S(1)} %get-tuple-element.46), channel_id=1, source_target_pairs={{0,16},{16,0},{1,17},{17,1},{2,18},{18,2},{3,19},{19,3},{4,20},{20... | collective-permute-start | bytes 688136 | tf_op jit(solution)/shard_map/ppermute | solution.py:177
  32.6 2.4 %collective-permute-done.13.refs_2_ = bf16[224,256]{1,0:T(8,128)(2,1)S(1)} collective-permute-done((bf16[224,256]{1,0:T(8,128)(2,1)S(1)}, bf16[224,256]{1,0:T(8,128)(2,1)S(1)}, u32[]{:S(2)}, u32[]{:S(2)}) %collective-permute-start.13) | collective-permute-done | bytes 114720 | tf_op jit(solution)/shard_map/ppermute | solution.py:188
  35.0 1.6 %collective-permute-done.14.refs_3_ = bf16[224,256]{1,0:T(8,128)(2,1)S(1)} collective-permute-done((bf16[224,256]{1,0:T(8,128)(2,1)S(1)}, bf16[224,256]{1,0:T(8,128)(2,1)S(1)}, u32[]{:S(2)}, u32[]{:S(2)}) %collective-permute-start.14) | collective-permute-done | bytes 114720 | tf_op jit(solution)/shard_map/ppermute | solution.py:188
  36.6 0.0 collective-permute-done.5.refs_5_
  36.6 0.0 collective-permute-done.7.refs_7_
  36.6 0.6 shard_map.83
  37.2 1.9 %collective-permute-start.15 = (bf16[224,1024]{1,0:T(8,128)(2,1)S(1)}, bf16[224,1024]{1,0:T(8,128)(2,1)S(1)}, u32[]{:S(2)}, u32[]{:S(2)}) collective-permute-start(bf16[224,1024]{1,0:T(8,128)(2,1)S(1)} %shard_map.83), channel_id=1, source_target_pairs={{0,4},{1,5},{2,6},{3,7},{4,0},{5,1},{6,2},{7,3},{8,12},{9,13},{10,... | collective-permute-start | bytes 1376264 | tf_op jit(solution)/shard_map/ppermute | solution.py:197
  39.1 1.5 %collective-permute-start.8 = (bf16[128,896]{1,0:T(8,128)(2,1)S(1)}, bf16[128,896]{1,0:T(8,128)(2,1)S(1)}, u32[]{:S(2)}, u32[]{:S(2)}) collective-permute-start(bf16[128,896]{1,0:T(8,128)(2,1)S(1)} %get-tuple-element.35), channel_id=1, source_target_pairs={{0,16},{16,0},{1,17},{17,1},{2,18},{18,2},{3,19},{19,3},{4,20},{20... | collective-permute-start | bytes 688136 | tf_op jit(solution)/shard_map/ppermute | solution.py:177
  40.6 0.0 collective-permute-done.17.got_ref.refs_1_
  40.6 0.2 shard_map.85
  40.8 0.7 copy-done.4
  41.5 0.0 collective-permute-start.18
  41.5 1.5 %collective-permute-start.19 = (bf16[224,256]{1,0:T(8,128)(2,1)S(1)}, bf16[224,256]{1,0:T(8,128)(2,1)S(1)}, u32[]{:S(2)}, u32[]{:S(2)}) collective-permute-start(bf16[224,256]{1,0:T(8,128)(2,1)S(1)} %get-tuple-element.50), channel_id=1, source_target_pairs={{0,2},{1,3},{2,0},{3,1},{4,6},{5,7},{6,4},{7,5},{8,10},{9,11},{10,... | collective-permute-start | bytes 344072 | tf_op jit(solution)/shard_map/ppermute | solution.py:188
  43.1 3.8 %collective-permute-done.8.got_ref.refs_2_ = bf16[128,896]{1,0:T(8,128)(2,1)S(1)} collective-permute-done((bf16[128,896]{1,0:T(8,128)(2,1)S(1)}, bf16[128,896]{1,0:T(8,128)(2,1)S(1)}, u32[]{:S(2)}, u32[]{:S(2)}) %collective-permute-start.8) | collective-permute-done | bytes 229408 | tf_op jit(solution)/shard_map/ppermute | solution.py:177
  46.9 0.2 shard_map.81
  47.1 0.7 copy-done.6
  47.8 1.5 %collective-permute-start.10 = (bf16[224,256]{1,0:T(8,128)(2,1)S(1)}, bf16[224,256]{1,0:T(8,128)(2,1)S(1)}, u32[]{:S(2)}, u32[]{:S(2)}) collective-permute-start(bf16[224,256]{1,0:T(8,128)(2,1)S(1)} %get-tuple-element.39), channel_id=1, source_target_pairs={{0,2},{1,3},{2,0},{3,1},{4,6},{5,7},{6,4},{7,5},{8,10},{9,11},{10,... | collective-permute-start | bytes 344072 | tf_op jit(solution)/shard_map/ppermute | solution.py:188
  49.4 1.7 %collective-permute-start.11 = (bf16[224,256]{1,0:T(8,128)(2,1)S(1)}, bf16[224,256]{1,0:T(8,128)(2,1)S(1)}, u32[]{:S(2)}, u32[]{:S(2)}) collective-permute-start(bf16[224,256]{1,0:T(8,128)(2,1)S(1)} %get-tuple-element.40), channel_id=1, source_target_pairs={{0,3},{1,2},{2,1},{3,0},{4,7},{5,6},{6,5},{7,4},{8,11},{9,10},{10,... | collective-permute-start | bytes 344072 | tf_op jit(solution)/shard_map/ppermute | solution.py:188
  51.1 0.0 collective-permute-done.19.refs_2_
  51.1 4.2 %collective-permute-done.20.refs_3_ = bf16[224,256]{1,0:T(8,128)(2,1)S(1)} collective-permute-done((bf16[224,256]{1,0:T(8,128)(2,1)S(1)}, bf16[224,256]{1,0:T(8,128)(2,1)S(1)}, u32[]{:S(2)}, u32[]{:S(2)}) %collective-permute-start.20) | collective-permute-done | bytes 114720 | tf_op jit(solution)/shard_map/ppermute | solution.py:188
  55.3 1.4 %shard_map.86 = bf16[224,1024]{1,0:T(8,128)(2,1)} custom-call(bf16[224,256]{1,0:T(8,128)(2,1)S(1)} %get-tuple-element.48.refs_0_, bf16[224,256]{1,0:T(8,128)(2,1)S(1)} %collective-permute-done.18.refs_1_, bf16[224,256]{1,0:T(8,128)(2,1)S(1)} %collective-permute-done.19.refs_2_, bf16[224,256]{1,0:T(8,128)(2,1)S(1)} %collective-permute-done.20.refs_3_, ...), custom_call_target="tpu_custom_call" | custom-call | tf_op jit(solution)/shard_map/pallas_call | solution.py:22
  56.7 0.4 collective-permute-start.21
  57.1 0.2 collective-permute-done.11.refs_3_
  57.3 1.4 %shard_map.84 = bf16[224,1024]{1,0:T(8,128)(2,1)} custom-call(bf16[224,256]{1,0:T(8,128)(2,1)S(1)} %get-tuple-element.37.refs_0_, bf16[224,256]{1,0:T(8,128)(2,1)S(1)} %collective-permute-done.9.refs_1_, bf16[224,256]{1,0:T(8,128)(2,1)S(1)} %collective-permute-done.10.refs_2_, bf16[224,256]{1,0:T(8,128)(2,1)S(1)} %collective-permute-done.11.refs_3_, ...), custom_call_target="tpu_custom_call" | custom-call | tf_op jit(solution)/shard_map/pallas_call | solution.py:22
  58.7 2.6 %collective-permute-start.16 = (bf16[224,1024]{1,0:T(8,128)(2,1)}, bf16[224,1024]{1,0:T(8,128)(2,1)}, u32[]{:S(2)}, u32[]{:S(2)}) collective-permute-start(bf16[224,1024]{1,0:T(8,128)(2,1)} %shard_map.84), channel_id=1, source_target_pairs={{0,8},{1,9},{2,10},{3,11},{4,12},{5,13},{6,14},{7,15},{8,0},{9,1},... | collective-permute-start | bytes 1376264 | tf_op jit(solution)/shard_map/ppermute | solution.py:197
  61.3 1.5 %collective-permute-start = (bf16[128,896]{1,0:T(8,128)(2,1)}, bf16[128,896]{1,0:T(8,128)(2,1)}, u32[]{:S(2)}, u32[]{:S(2)}) collective-permute-start(bf16[128,896]{1,0:T(8,128)(2,1)} %get-tuple-element.29), channel_id=1, source_target_pairs={{0,16},{16,0},{1,17},{17,1},{2,18},{18,2},{3,19},{19,3},{4,20},{20... | collective-permute-start | bytes 688136 | tf_op jit(solution)/shard_map/ppermute | solution.py:177
  62.8 6.2 %collective-permute-done.got_ref.refs_0_ = bf16[128,896]{1,0:T(8,128)(2,1)} collective-permute-done((bf16[128,896]{1,0:T(8,128)(2,1)}, bf16[128,896]{1,0:T(8,128)(2,1)}, u32[]{:S(2)}, u32[]{:S(2)}) %collective-permute-start) | collective-permute-done | bytes 229408 | tf_op jit(solution)/shard_map/ppermute | solution.py:177
  68.9 1.2 %copy-done.3 = bf16[1,256,2048]{2,1,0:T(8,128)(2,1)S(1)} copy-done((bf16[1,256,2048]{2,1,0:T(8,128)(2,1)S(1)}, bf16[1,256,2048]{2,1,0:T(8,128)(2,1)}, u32[]{:S(2)}) %copy-start.3) | copy-done | bytes 1048600
  70.2 0.9 copy-done.5
  71.1 0.9 copy-done.7
  72.0 8.0 %shard_map.87 = (bf16[256,2048]{1,0:T(8,128)(2,1)}, f32[128,1]{1,0:T(8,128)S(1)}, f32[128,1]{1,0:T(8,128)S(1)}) custom-call(bf16[128,3584]{1,0:T(8,128)(2,1)S(1)} %copy-done.1, s32[128,2]{1,0:T(8,128)S(1)} %copy.14.ids_ref, bf16[128,2]{1,0:T(8,128)(2,1)S(1)} %copy.15.weights_ref, bf16[256,2048]{1,0:T(8,128)(2,1)S(1)} %bitcast.6, bf16[1024,3584]{1,0:T(8,128)(2,1)} %bitcast.7, ...), custom_call_target="tpu_custom_call" | custom-call | tf_op jit(solution)/shard_map/pallas_call | solution.py:139
  80.1 1.5 %collective-permute-start.22 = (f32[128,1]{1,0:T(8,128)S(1)}, f32[128,1]{1,0:T(8,128)S(1)}, u32[]{:S(2)}, u32[]{:S(2)}) collective-permute-start(f32[128,1]{1,0:T(8,128)S(1)} %get-tuple-element.54), channel_id=1, source_target_pairs={{0,16},{16,0},{1,17},{17,1},{2,18},{18,2},{3,19},{19,3},{4,20},{20... | collective-permute-start | bytes 1544 | tf_op jit(solution)/shard_map/ppermute | solution.py:206
  81.6 0.9 copy-done.9
  82.5 1.2 %shard_map.78 = (bf16[224,256]{1,0:T(8,128)(2,1)S(1)}, bf16[224,256]{1,0:T(8,128)(2,1)S(1)}, bf16[224,256]{1,0:T(8,128)(2,1)S(1)}, bf16[224,256]{1,0:T(8,128)(2,1)S(1)}) custom-call(bf16[128,896]{1,0:T(8,128)(2,1)} %collective-permute-done.got_ref.refs_0_, bf16[128,1024]{1,0:T(8,128)(2,1)S(1)} %collective-permute-done.1.first_ref.got_ref.refs_3_, ...), custom_call_target="tpu_custom_call" | custom-call | tf_op jit(solution)/shard_map/pallas_call | solution.py:22
  83.7 0.1 collective-permute-start.2
  83.8 1.4 %collective-permute-start.3 = (bf16[224,256]{1,0:T(8,128)(2,1)S(1)}, bf16[224,256]{1,0:T(8,128)(2,1)S(1)}, u32[]{:S(2)}, u32[]{:S(2)}) collective-permute-start(bf16[224,256]{1,0:T(8,128)(2,1)S(1)} %get-tuple-element.33), channel_id=1, source_target_pairs={{0,2},{1,3},{2,0},{3,1},{4,6},{5,7},{6,4},{7,5},{8,10},{9,11},{10,... | collective-permute-start | bytes 344072 | tf_op jit(solution)/shard_map/ppermute | solution.py:188
  85.2 0.1 reduce
  85.3 0.5 collective-permute-start.4
  85.8 0.1 reduce.1
  85.9 0.6 compare_select_fusion
  86.5 3.3 %collective-permute-done.3.refs_2_ = bf16[224,256]{1,0:T(8,128)(2,1)S(1)} collective-permute-done((bf16[224,256]{1,0:T(8,128)(2,1)S(1)}, bf16[224,256]{1,0:T(8,128)(2,1)S(1)}, u32[]{:S(2)}, u32[]{:S(2)}) %collective-permute-start.3) | collective-permute-done | bytes 114720 | tf_op jit(solution)/shard_map/ppermute | solution.py:188
  89.8 1.6 %collective-permute-done.4.refs_3_ = bf16[224,256]{1,0:T(8,128)(2,1)S(1)} collective-permute-done((bf16[224,256]{1,0:T(8,128)(2,1)S(1)}, bf16[224,256]{1,0:T(8,128)(2,1)S(1)}, u32[]{:S(2)}, u32[]{:S(2)}) %collective-permute-start.4) | collective-permute-done | bytes 114720 | tf_op jit(solution)/shard_map/ppermute | solution.py:188
  91.3 0.6 shard_map.80
  92.0 2.3 %add_bitcast_fusion = f32[1,224,1024]{2,1,0:T(8,128)} fusion(bf16[224,1024]{1,0:T(8,128)(2,1)} %collective-permute-done.21, f32[224,1024]{1,0:T(8,128)S(1)} %shard_map.80, bf16[224,1024]{1,0:T(8,128)(2,1)} %collective-permute-done.16), kind=kLoop, calls=%fused_computation | loop fusion | flops 917504 | bytes 2752512 | tf_op jit(solution)/shard_map/broadcast_in_dim | solution.py:208
  (22 shorter events, 0.0 us)
Async XLA Ops:
  0.6 1.2 %copy-start.2 = (bf16[1,256,2048]{2,1,0:T(8,128)(2,1)S(1)}, bf16[1,256,2048]{2,1,0:T(8,128)(2,1)}, u32[]{:S(2)}) copy-start(bf16[1,256,2048]{2,1,0:T(8,128)(2,1)} %param.8) | copy-start | bytes 3145732
  1.9 67.1 %copy-start.1 = (bf16[128,3584]{1,0:T(8,128)(2,1)S(1)}, bf16[128,3584]{1,0:T(8,128)(2,1)}, u32[]{:S(2)}) copy-start(bf16[128,3584]{1,0:T(8,128)(2,1)} %up_ref.5) | copy-start | bytes 2752516
  2.1 15.0 %collective-permute-start.6 = (bf16[256,1024]{1,0:T(8,128)(2,1)S(1)}, bf16[256,1024]{1,0:T(8,128)(2,1)S(1)}, u32[]{:S(2)}, u32[]{:S(2)}) collective-permute-start(bf16[256,1024]{1,0:T(8,128)(2,1)S(1)} %shard_map.79.refs_4_), channel_id=1, source_target_pairs={{0,2},{1,3},{2,0},{3,1},{4,6},{5,7},{6,4},{7,5},{8,10},{9,11},{10,... | collective-permute-start | bytes 1572872 | tf_op jit(solution)/shard_map/ppermute | solution.py:169
  5.1 31.5 %collective-permute-start.5 = (bf16[256,1024]{1,0:T(8,128)(2,1)S(1)}, bf16[256,1024]{1,0:T(8,128)(2,1)S(1)}, u32[]{:S(2)}, u32[]{:S(2)}) collective-permute-start(bf16[256,1024]{1,0:T(8,128)(2,1)S(1)} %shard_map.79.refs_4_), channel_id=1, source_target_pairs={{0,1},{1,0},{2,3},{3,2},{4,5},{5,4},{6,7},{7,6},{8,9},{9,8},{10,11... | collective-permute-start | bytes 1572872 | tf_op jit(solution)/shard_map/ppermute | solution.py:178
  17.0 19.5 %collective-permute-start.7 = (bf16[256,1024]{1,0:T(8,128)(2,1)S(1)}, bf16[256,1024]{1,0:T(8,128)(2,1)S(1)}, u32[]{:S(2)}, u32[]{:S(2)}) collective-permute-start(bf16[256,1024]{1,0:T(8,128)(2,1)S(1)} %collective-permute-done.6.refs_6_), channel_id=1, source_target_pairs={{0,1},{1,0},{2,3},{3,2},{4,5},{5,4},{6,7},{7,6},{8,9},{9,8},{10,11... | collective-permute-start | bytes 1572872 | tf_op jit(solution)/shard_map/ppermute | solution.py:179
  18.6 1.2 %copy-start = (bf16[128,3584]{1,0:T(8,128)(2,1)S(1)}, bf16[128,3584]{1,0:T(8,128)(2,1)}, u32[]{:S(2)}) copy-start(bf16[128,3584]{1,0:T(8,128)(2,1)} %up_ref.5) | copy-start | bytes 2752516
  19.9 8.8 %collective-permute-start.1 = (bf16[128,1024]{1,0:T(8,128)(2,1)S(1)}, bf16[128,1024]{1,0:T(8,128)(2,1)S(1)}, u32[]{:S(2)}, u32[]{:S(2)}) collective-permute-start(bf16[128,1024]{1,0:T(8,128)(2,1)S(1)} %shard_map.77), channel_id=1, source_target_pairs={{0,16},{16,0},{1,17},{17,1},{2,18},{18,2},{3,19},{19,3},{4,20},{20... | collective-permute-start | bytes 786440 | tf_op jit(solution)/shard_map/ppermute | solution.py:167
  22.4 0.7 copy-start.8
  28.9 2.0 %collective-permute-start.12 = (bf16[224,256]{1,0:T(8,128)(2,1)S(1)}, bf16[224,256]{1,0:T(8,128)(2,1)S(1)}, u32[]{:S(2)}, u32[]{:S(2)}) collective-permute-start(bf16[224,256]{1,0:T(8,128)(2,1)S(1)} %get-tuple-element.43), channel_id=1, source_target_pairs={{0,1},{1,0},{2,3},{3,2},{4,5},{5,4},{6,7},{7,6},{8,9},{9,8},{10,11... | collective-permute-start | bytes 344072 | tf_op jit(solution)/shard_map/ppermute | solution.py:188
  29.0 6.0 %collective-permute-start.13 = (bf16[224,256]{1,0:T(8,128)(2,1)S(1)}, bf16[224,256]{1,0:T(8,128)(2,1)S(1)}, u32[]{:S(2)}, u32[]{:S(2)}) collective-permute-start(bf16[224,256]{1,0:T(8,128)(2,1)S(1)} %get-tuple-element.44), channel_id=1, source_target_pairs={{0,2},{1,3},{2,0},{3,1},{4,6},{5,7},{6,4},{7,5},{8,10},{9,11},{10,... | collective-permute-start | bytes 344072 | tf_op jit(solution)/shard_map/ppermute | solution.py:188
  30.8 5.8 %collective-permute-start.14 = (bf16[224,256]{1,0:T(8,128)(2,1)S(1)}, bf16[224,256]{1,0:T(8,128)(2,1)S(1)}, u32[]{:S(2)}, u32[]{:S(2)}) collective-permute-start(bf16[224,256]{1,0:T(8,128)(2,1)S(1)} %get-tuple-element.45), channel_id=1, source_target_pairs={{0,3},{1,2},{2,1},{3,0},{4,7},{5,6},{6,5},{7,4},{8,11},{9,10},{10,... | collective-permute-start | bytes 344072 | tf_op jit(solution)/shard_map/ppermute | solution.py:188
  30.9 9.7 %collective-permute-start.17 = (bf16[128,896]{1,0:T(8,128)(2,1)S(1)}, bf16[128,896]{1,0:T(8,128)(2,1)S(1)}, u32[]{:S(2)}, u32[]{:S(2)}) collective-permute-start(bf16[128,896]{1,0:T(8,128)(2,1)S(1)} %get-tuple-element.46), channel_id=1, source_target_pairs={{0,16},{16,0},{1,17},{17,1},{2,18},{18,2},{3,19},{19,3},{4,20},{20... | collective-permute-start | bytes 688136 | tf_op jit(solution)/shard_map/ppermute | solution.py:177
  37.2 20.0 %collective-permute-start.15 = (bf16[224,1024]{1,0:T(8,128)(2,1)S(1)}, bf16[224,1024]{1,0:T(8,128)(2,1)S(1)}, u32[]{:S(2)}, u32[]{:S(2)}) collective-permute-start(bf16[224,1024]{1,0:T(8,128)(2,1)S(1)} %shard_map.83), channel_id=1, source_target_pairs={{0,4},{1,5},{2,6},{3,7},{4,0},{5,1},{6,2},{7,3},{8,12},{9,13},{10,... | collective-permute-start | bytes 1376264 | tf_op jit(solution)/shard_map/ppermute | solution.py:197
  39.1 7.8 %collective-permute-start.8 = (bf16[128,896]{1,0:T(8,128)(2,1)S(1)}, bf16[128,896]{1,0:T(8,128)(2,1)S(1)}, u32[]{:S(2)}, u32[]{:S(2)}) collective-permute-start(bf16[128,896]{1,0:T(8,128)(2,1)S(1)} %get-tuple-element.35), channel_id=1, source_target_pairs={{0,16},{16,0},{1,17},{17,1},{2,18},{18,2},{3,19},{19,3},{4,20},{20... | collective-permute-start | bytes 688136 | tf_op jit(solution)/shard_map/ppermute | solution.py:177
  40.8 0.7 copy-start.4
  41.5 7.8 %collective-permute-start.18 = (bf16[224,256]{1,0:T(8,128)(2,1)S(1)}, bf16[224,256]{1,0:T(8,128)(2,1)S(1)}, u32[]{:S(2)}, u32[]{:S(2)}) collective-permute-start(bf16[224,256]{1,0:T(8,128)(2,1)S(1)} %get-tuple-element.49), channel_id=1, source_target_pairs={{0,1},{1,0},{2,3},{3,2},{4,5},{5,4},{6,7},{7,6},{8,9},{9,8},{10,11... | collective-permute-start | bytes 344072 | tf_op jit(solution)/shard_map/ppermute | solution.py:188
  41.5 9.6 %collective-permute-start.19 = (bf16[224,256]{1,0:T(8,128)(2,1)S(1)}, bf16[224,256]{1,0:T(8,128)(2,1)S(1)}, u32[]{:S(2)}, u32[]{:S(2)}) collective-permute-start(bf16[224,256]{1,0:T(8,128)(2,1)S(1)} %get-tuple-element.50), channel_id=1, source_target_pairs={{0,2},{1,3},{2,0},{3,1},{4,6},{5,7},{6,4},{7,5},{8,10},{9,11},{10,... | collective-permute-start | bytes 344072 | tf_op jit(solution)/shard_map/ppermute | solution.py:188
  47.1 0.7 copy-start.6
  47.8 9.2 %collective-permute-start.10 = (bf16[224,256]{1,0:T(8,128)(2,1)S(1)}, bf16[224,256]{1,0:T(8,128)(2,1)S(1)}, u32[]{:S(2)}, u32[]{:S(2)}) collective-permute-start(bf16[224,256]{1,0:T(8,128)(2,1)S(1)} %get-tuple-element.39), channel_id=1, source_target_pairs={{0,2},{1,3},{2,0},{3,1},{4,6},{5,7},{6,4},{7,5},{8,10},{9,11},{10,... | collective-permute-start | bytes 344072 | tf_op jit(solution)/shard_map/ppermute | solution.py:188
  49.4 5.9 %collective-permute-start.20 = (bf16[224,256]{1,0:T(8,128)(2,1)S(1)}, bf16[224,256]{1,0:T(8,128)(2,1)S(1)}, u32[]{:S(2)}, u32[]{:S(2)}) collective-permute-start(bf16[224,256]{1,0:T(8,128)(2,1)S(1)} %get-tuple-element.51), channel_id=1, source_target_pairs={{0,3},{1,2},{2,1},{3,0},{4,7},{5,6},{6,5},{7,4},{8,11},{9,10},{10,... | collective-permute-start | bytes 344072 | tf_op jit(solution)/shard_map/ppermute | solution.py:188
  49.4 7.9 %collective-permute-start.11 = (bf16[224,256]{1,0:T(8,128)(2,1)S(1)}, bf16[224,256]{1,0:T(8,128)(2,1)S(1)}, u32[]{:S(2)}, u32[]{:S(2)}) collective-permute-start(bf16[224,256]{1,0:T(8,128)(2,1)S(1)} %get-tuple-element.40), channel_id=1, source_target_pairs={{0,3},{1,2},{2,1},{3,0},{4,7},{5,6},{6,5},{7,4},{8,11},{9,10},{10,... | collective-permute-start | bytes 344072 | tf_op jit(solution)/shard_map/ppermute | solution.py:188
  51.1 6.1 %collective-permute-start.9 = (bf16[224,256]{1,0:T(8,128)(2,1)S(1)}, bf16[224,256]{1,0:T(8,128)(2,1)S(1)}, u32[]{:S(2)}, u32[]{:S(2)}) collective-permute-start(bf16[224,256]{1,0:T(8,128)(2,1)S(1)} %get-tuple-element.38), channel_id=1, source_target_pairs={{0,1},{1,0},{2,3},{3,2},{4,5},{5,4},{6,7},{7,6},{8,9},{9,8},{10,11... | collective-permute-start | bytes 344072 | tf_op jit(solution)/shard_map/ppermute | solution.py:188
  56.7 35.3 %collective-permute-start.21 = (bf16[224,1024]{1,0:T(8,128)(2,1)}, bf16[224,1024]{1,0:T(8,128)(2,1)}, u32[]{:S(2)}, u32[]{:S(2)}) collective-permute-start(bf16[224,1024]{1,0:T(8,128)(2,1)} %shard_map.86), channel_id=1, source_target_pairs={{0,4},{1,5},{2,6},{3,7},{4,0},{5,1},{6,2},{7,3},{8,12},{9,13},{10,... | collective-permute-start | bytes 1376264 | tf_op jit(solution)/shard_map/ppermute | solution.py:197
  57.3 28.7 %copy-start.10 = (s32[128,2]{0,1:T(2,128)S(1)}, s32[128,2]{0,1:T(2,128)}, u32[]{:S(2)}) copy-start(s32[128,2]{0,1:T(2,128)} %param.7) | copy-start | bytes 3076
  58.7 33.3 %collective-permute-start.16 = (bf16[224,1024]{1,0:T(8,128)(2,1)}, bf16[224,1024]{1,0:T(8,128)(2,1)}, u32[]{:S(2)}, u32[]{:S(2)}) collective-permute-start(bf16[224,1024]{1,0:T(8,128)(2,1)} %shard_map.84), channel_id=1, source_target_pairs={{0,8},{1,9},{2,10},{3,11},{4,12},{5,13},{6,14},{7,15},{8,0},{9,1},... | collective-permute-start | bytes 1376264 | tf_op jit(solution)/shard_map/ppermute | solution.py:197
  61.3 7.7 %collective-permute-start = (bf16[128,896]{1,0:T(8,128)(2,1)}, bf16[128,896]{1,0:T(8,128)(2,1)}, u32[]{:S(2)}, u32[]{:S(2)}) collective-permute-start(bf16[128,896]{1,0:T(8,128)(2,1)} %get-tuple-element.29), channel_id=1, source_target_pairs={{0,16},{16,0},{1,17},{17,1},{2,18},{18,2},{3,19},{19,3},{4,20},{20... | collective-permute-start | bytes 688136 | tf_op jit(solution)/shard_map/ppermute | solution.py:177
  68.9 1.2 %copy-start.3 = (bf16[1,256,2048]{2,1,0:T(8,128)(2,1)S(1)}, bf16[1,256,2048]{2,1,0:T(8,128)(2,1)}, u32[]{:S(2)}) copy-start(bf16[1,256,2048]{2,1,0:T(8,128)(2,1)} %param.8) | copy-start | bytes 3145732
  70.2 0.9 copy-start.5
  71.1 0.9 copy-start.7
  80.1 5.2 %collective-permute-start.22 = (f32[128,1]{1,0:T(8,128)S(1)}, f32[128,1]{1,0:T(8,128)S(1)}, u32[]{:S(2)}, u32[]{:S(2)}) collective-permute-start(f32[128,1]{1,0:T(8,128)S(1)} %get-tuple-element.54), channel_id=1, source_target_pairs={{0,16},{16,0},{1,17},{17,1},{2,18},{18,2},{3,19},{19,3},{4,20},{20... | collective-permute-start | bytes 1544 | tf_op jit(solution)/shard_map/ppermute | solution.py:206
  81.6 0.9 copy-start.9
  83.7 2.8 %collective-permute-start.2 = (bf16[224,256]{1,0:T(8,128)(2,1)S(1)}, bf16[224,256]{1,0:T(8,128)(2,1)S(1)}, u32[]{:S(2)}, u32[]{:S(2)}) collective-permute-start(bf16[224,256]{1,0:T(8,128)(2,1)S(1)} %get-tuple-element.32), channel_id=1, source_target_pairs={{0,1},{1,0},{2,3},{3,2},{4,5},{5,4},{6,7},{7,6},{8,9},{9,8},{10,11... | collective-permute-start | bytes 344072 | tf_op jit(solution)/shard_map/ppermute | solution.py:188
  83.8 6.0 %collective-permute-start.3 = (bf16[224,256]{1,0:T(8,128)(2,1)S(1)}, bf16[224,256]{1,0:T(8,128)(2,1)S(1)}, u32[]{:S(2)}, u32[]{:S(2)}) collective-permute-start(bf16[224,256]{1,0:T(8,128)(2,1)S(1)} %get-tuple-element.33), channel_id=1, source_target_pairs={{0,2},{1,3},{2,0},{3,1},{4,6},{5,7},{6,4},{7,5},{8,10},{9,11},{10,... | collective-permute-start | bytes 344072 | tf_op jit(solution)/shard_map/ppermute | solution.py:188
  85.3 6.0 %collective-permute-start.4 = (bf16[224,256]{1,0:T(8,128)(2,1)S(1)}, bf16[224,256]{1,0:T(8,128)(2,1)S(1)}, u32[]{:S(2)}, u32[]{:S(2)}) collective-permute-start(bf16[224,256]{1,0:T(8,128)(2,1)S(1)} %get-tuple-element.34), channel_id=1, source_target_pairs={{0,3},{1,2},{2,1},{3,0},{4,7},{5,6},{6,5},{7,4},{8,11},{9,10},{10,... | collective-permute-start | bytes 344072 | tf_op jit(solution)/shard_map/ppermute | solution.py:188

commit v2 on v0

--- a/solution.py
+++ b/solution.py
@@ -1,7 +1,19 @@
+import functools
+
 import jax
 import jax.numpy as jnp
 from jax import lax
+from jax.experimental import pallas as pl
+from jax.experimental.pallas import tpu as pltpu
 from jax.sharding import PartitionSpec as P
+
+INNER = 4
+LANES = 128
+VMEM = pl.BlockSpec(memory_space=pltpu.VMEM)
+HBM = pl.BlockSpec(memory_space=pltpu.HBM)
+LOAD = pl.BlockSpec(memory_space=pltpu.VMEM)
+ANY = pl.BlockSpec(memory_space=pl.ANY)
+TURNED = (((1,), (1,)), ((), ()))
 
 
 def contract_rows(left_rows, right_rows):
@@ -10,7 +22,271 @@
     )
 
 
-def local(upstream, combine_weights, expert_ids, saved_hidden, down_weight):
+def after(value, *others):
+    return lax.optimization_barrier((value, *others))[0]
+
+
+def call(*jobs, waits=(), vmem=8, cost=0):
+    specs = [spec for job in jobs for spec in job[4] or [VMEM] * len(job[1])]
+    args = [arg for job in jobs for arg in job[1]]
+    outs = tuple(jax.ShapeDtypeStruct(*out) for job in jobs for out in job[2])
+    scratch = [item for job in jobs for item in job[3]]
+
+    def body(*refs):
+        ins, rest = refs[: len(args)], refs[len(args) + len(waits) :]
+        out_refs, temps = rest[: len(outs)], rest[len(outs) :]
+        for kernel, job_args, job_outs, job_scratch, _ in jobs:
+            x, y, z = len(job_args), len(job_outs), len(job_scratch)
+            kernel(*ins[:x], *out_refs[:y], *temps[:z])
+            ins, out_refs, temps = ins[x:], out_refs[y:], temps[z:]
+
+    place = lambda arg, spec: arg if spec is VMEM else pltpu.with_memory_space_constraint(arg, pltpu.HBM)
+    return pl.pallas_call(
+        body,
+        out_shape=outs,
+        in_specs=specs + [ANY] * len(waits),
+        out_specs=tuple(VMEM for _ in outs),
+        scratch_shapes=scratch,
+        compiler_params=pltpu.CompilerParams(vmem_limit_bytes=vmem << 20),
+        cost_estimate=pl.CostEstimate(flops=cost, bytes_accessed=cost, transcendentals=0),
+    )(*[place(*pair) for pair in zip(args, specs)], *waits)
+
+
+def chunk_start(k, chunk):
+    group = lax.axis_index("dp") // INNER
+    return pl.multiple_of((group ^ k) * chunk, LANES)
+
+
+def prepare_kernel(outer, chunk, up_hbm, hidden_hbm, ids_ref, weights_ref, *refs):
+    first_ref, column_ref, act_refs = refs[0], refs[1], refs[2:4]
+    own_refs, send_refs = refs[4 : 4 + outer], refs[4 + outer : -3]
+    up_ref, hidden_ref, sems = refs[-3:]
+    top = outer - 1
+    loads = []
+    for k in range(outer):
+        cols = pl.ds(chunk_start(k, chunk), chunk)
+        loads.append(pltpu.make_async_copy(up_hbm.at[:, cols], up_ref.at[k], sems.at[k]))
+    loads.append(pltpu.make_async_copy(hidden_hbm, hidden_ref, sems.at[outer]))
+    for k in [top, outer] + list(range(top - 1, -1, -1)):
+        loads[k].start()
+    expert = lax.axis_index("expert")
+
+    def token_weight(of):
+        picked = jnp.where(ids_ref[...] == of, weights_ref[...].astype(jnp.float32), 0.0)
+        lanes = jnp.sum(picked, axis=0, keepdims=True)
+        return jnp.broadcast_to(lanes, (LANES, lanes.shape[1])).T
+
+    weight = token_weight(expert)
+    column_ref[...] = weight
+    weight = weight[:, :1]
+    first_ref[:, chunk:] = token_weight(1 - expert).astype(jnp.bfloat16)
+    for k in range(top, -1, -1):
+        loads[k].wait()
+        rows = up_ref[k]
+        (send_refs[k] if k < top else first_ref)[:, :chunk] = rows
+        own_refs[k][...] = (weight * rows.astype(jnp.float32)).astype(jnp.bfloat16).T
+    loads[outer].wait()
+    half, hidden_units = hidden_ref.shape[0] // 2, hidden_ref.shape[1] // 2
+    for part in range(2):
+        source = pl.ds(pl.multiple_of((expert ^ part) * half, half), half)
+        for start, out_ref in zip((0, act_refs[0].shape[1]), act_refs):
+            stop = start + out_ref.shape[1]
+            gate = hidden_ref[source, start:stop].astype(jnp.float32)
+            up = hidden_ref[source, hidden_units + start : hidden_units + stop].astype(jnp.float32)
+            act = gate * jax.nn.sigmoid(gate) * up
+            out_ref[part * half : (part + 1) * half, :] = act.astype(jnp.bfloat16)
+
+
+def split_kernel(chunk, got_ref, first_ref, own_ref, *refs):
+    pays, scaled_ref = refs[:-1], refs[-1]
+    weight = first_ref[:, chunk : chunk + 1].astype(jnp.float32)
+    scaled = (weight * got_ref[:, :chunk].astype(jnp.float32)).astype(jnp.bfloat16)
+    scaled_ref[...] = scaled.T
+    piece = chunk // INNER
+    mine = lax.axis_index("dp") % INNER
+    for j in range(INNER):
+        rows = pl.ds(pl.multiple_of((mine ^ j) * piece, 16), piece)
+        pays[j][:, :LANES] = own_ref[rows, :]
+        pays[j][:, LANES:] = scaled_ref[rows, :]
+
+
+def partial_kernel(*refs):
+    pays, acts, adds, out_ref = refs[:INNER], refs[INNER : 2 * INNER], refs[2 * INNER : -1], refs[-1]
+    total = None
+    for pay, act in zip(pays, acts):
+        term = jnp.dot(pay[...], act[...], preferred_element_type=jnp.float32)
+        total = term if total is None else total + term
+    for add in adds:
+        total = total + add[...].astype(jnp.float32)
+    out_ref[...] = total.astype(out_ref.dtype)
+
+
+def whole_kernel(*refs):
+    pays, acts, out_ref = refs[:INNER], refs[INNER : 3 * INNER], refs[-1]
+    start = 0
+    for part in (acts[:INNER], acts[INNER:]):
+        stop = start + part[0].shape[1]
+        partial_kernel(*pays, *part, out_ref.at[:, start:stop])
+        start = stop
+
+
+def final_kernel(base_ref, side_ref, left_ref, right_ref, out_ref):
+    split = left_ref.shape[1]
+    for cols, ref in ((slice(0, split), left_ref), (slice(split, None), right_ref)):
+        both = side_ref[:, cols].astype(jnp.float32) + ref[...].astype(jnp.float32)
+        out_ref[:, cols] = base_ref[:, cols] + both
+
+
+def probs_kernel(ids_ref, own_ref, back_ref, out_ref):
+    mine = ids_ref[...] == lax.axis_index("expert")
+    out_ref[...] = jnp.where(mine, own_ref[:1], back_ref[:1])
+
+
+def hidden_kernel(outer, chunk, column_ref, up_hbm, hidden_hbm, w_hbm, *refs):
+    got_refs = refs[:outer]
+    out_ref, own_score, got_score = refs[outer : outer + 3]
+    routed_ref, hidden_ref, w_ref, sems = refs[outer + 3 :]
+    tokens = up_hbm.shape[0]
+    hidden_units = w_ref.shape[0]
+    width = 2 * LANES
+    blocks = hidden_units // width
+    expert = lax.axis_index("expert")
+    top = pltpu.make_async_copy(up_hbm, routed_ref.at[pl.ds(0, tokens)], sems.at[blocks])
+    stored = pltpu.make_async_copy(hidden_hbm, hidden_ref, sems.at[blocks + 1])
+    loads = []
+    for i in range(blocks):
+        rows = pl.ds(i * width, width)
+        loads.append(pltpu.make_async_copy(w_hbm.at[rows], w_ref.at[rows], sems.at[i]))
+    top.start()
+    loads[0].start()
+    stored.start()
+    for load in loads[1:]:
+        load.start()
+    for k in range(outer):
+        routed_ref[tokens:, pl.ds(chunk_start(k, chunk), chunk)] = got_refs[k][:, :chunk]
+    weights = [column_ref[:, :1], got_refs[outer - 1][:, chunk : chunk + 1].astype(jnp.float32)]
+    scores = [None, None]
+    top.wait()
+    for i in range(blocks):
+        loads[i].wait()
+        backward = lax.dot_general(
+            routed_ref[...], w_ref[i * width : (i + 1) * width, :], TURNED, preferred_element_type=jnp.float32
+        )
+        if i == 0:
+            stored.wait()
+        gate_cols = slice(i * width, (i + 1) * width)
+        up_cols = slice(hidden_units + i * width, hidden_units + (i + 1) * width)
+        for part in range(2):
+            back = backward[part * tokens : (part + 1) * tokens]
+            rows = pl.ds(pl.multiple_of((expert ^ part) * tokens, tokens), tokens)
+            gate = hidden_ref[rows, gate_cols].astype(jnp.float32)
+            up = hidden_ref[rows, up_cols].astype(jnp.float32)
+            sig = jax.nn.sigmoid(gate)
+            act = (gate * sig * up).astype(jnp.bfloat16).astype(jnp.float32)
+            score = jnp.sum(back * act, axis=1, keepdims=True)
+            scores[part] = score if i == 0 else scores[part] + score
+            grad = weights[part] * back
+            out_ref[rows, gate_cols] = (grad * up * sig * (1.0 + gate * (1.0 - sig))).astype(jnp.bfloat16)
+            out_ref[rows, up_cols] = (grad * gate * sig).astype(jnp.bfloat16)
+    for score, ref in zip(scores, (own_score, got_score)):
+        ref[...] = jnp.broadcast_to(score, (tokens, LANES)).T[:8]
+
+
+def both_experts(upstream, combine_weights, expert_ids, saved_hidden, down_weight):
+    tokens, features = upstream.shape
+    n = lax.axis_size("dp")
+    outer = n // INNER
+    chunk, piece = features // outer, features // n
+    hidden_units = down_weight.shape[1]
+    stored, weights = saved_hidden[0], down_weight[0]
+    ids, combine = expert_ids.T, combine_weights.T
+    flip = [(0, 1), (1, 0)]
+    cross = lambda value: lax.ppermute(value, "expert", flip)
+    swap = lambda value, bit: lax.ppermute(value, "dp", [(i, i ^ bit) for i in range(n)])
+    rows = stored.shape[0]
+    widths = (hidden_units // 2, hidden_units // 2)
+    bf16, f32 = jnp.bfloat16, jnp.float32
+
+    prepared = call((
+        functools.partial(prepare_kernel, outer, chunk),
+        [upstream, stored, ids, combine],
+        [((tokens, chunk + LANES), bf16), ((tokens, LANES), f32)]
+        + [((rows, width), bf16) for width in widths]
+        + [((chunk, tokens), bf16)] * outer
+        + [((tokens, chunk), bf16)] * (outer - 1),
+        [
+            pltpu.VMEM((outer, tokens, chunk), bf16),
+            pltpu.VMEM((rows, 2 * hidden_units), bf16),
+            pltpu.SemaphoreType.DMA((outer + 1,)),
+        ],
+        [HBM, HBM, LOAD, LOAD],
+    ))
+    first, column, mine = prepared[0], prepared[1], prepared[2:4]
+    own, send = prepared[4 : 4 + outer], prepared[4 + outer :]
+
+    def split(k):
+        shapes = [((piece, 2 * tokens), bf16)] * INNER
+        scratch = [pltpu.VMEM((chunk, tokens), bf16)]
+        return functools.partial(split_kernel, chunk), [got[k], got[3], own[k]], shapes, scratch, None
+
+    def spread(pays):
+        return [pays[0]] + [swap(pays[j], j) for j in range(1, INNER)]
+
+    def partial(pays, h, *adds):
+        sides = [acts[h][j] for j in range(INNER)]
+        return partial_kernel, [*pays, *sides, *adds], [((piece, widths[h]), bf16)], [], None
+
+    def whole(pays, kind):
+        sides = [acts[h][j] for h in range(2) for j in range(INNER)]
+        return whole_kernel, [*pays, *sides], [((piece, hidden_units), kind)], [], None
+
+    got = {3: cross(first)}
+    acts = [{0: mine[h], 1: swap(mine[h], 1), 2: swap(mine[h], 2)} for h in range(2)]
+    pays = {}
+    cut = call(split(3))
+    pays[3] = spread(cut)
+    got[2] = cross(after(send[2], cut[0]))
+    acts[0][3] = swap(after(acts[0][2], cut[0]), 1)
+    acts[1][3] = swap(after(acts[1][2], acts[0][3]), 1)
+    far0, *cut = call(partial(pays[3], 0), split(2))
+    near0 = swap(far0, INNER)
+    pays[2] = spread(cut)
+    got[1] = cross(after(send[1], cut[0]))
+    far1, = call(partial(pays[3], 1), waits=(far0,))
+    near1 = swap(far1, INNER)
+    wide0, *cut = call(partial(pays[2], 0, near0), split(1), waits=(far1,))
+    last0 = swap(wide0, 2 * INNER)
+    pays[1] = spread(cut)
+    got[0] = cross(after(send[0], cut[0]))
+    wide1, = call(partial(pays[2], 1, near1), waits=(wide0,))
+    last1 = swap(wide1, 2 * INNER)
+    side, *cut = call(whole(pays[1], bf16), split(0), waits=(wide1,))
+    pays[0] = spread(cut)
+
+    grad_hidden, own_score, got_score = call(
+        (
+            functools.partial(hidden_kernel, outer, chunk),
+            [column, upstream, stored, weights, *[got[k] for k in range(outer)]],
+            [(stored.shape, bf16), ((8, tokens), f32), ((8, tokens), f32)],
+            [
+                pltpu.VMEM((rows, features), bf16),
+                pltpu.VMEM(stored.shape, bf16),
+                pltpu.VMEM(weights.shape, bf16),
+                pltpu.SemaphoreType.DMA((hidden_units // (2 * LANES) + 2,)),
+            ],
+            [VMEM, HBM, HBM, HBM] + [VMEM] * outer,
+        ),
+        waits=(side,), vmem=18,
+    )
+    side = swap(side, INNER)
+    back_score = cross(got_score)
+    base, = call(whole(pays[0], f32), waits=(own_score,))
+    grad_probs, = call((probs_kernel, [ids, own_score, back_score], [(ids.shape, f32)], [], None))
+    grad_down, = call((final_kernel, [base, side, last0, last1], [((piece, hidden_units), f32)], [], None))
+    return grad_down[None], grad_hidden[None], grad_probs.T
+
+
+def any_experts(upstream, combine_weights, expert_ids, saved_hidden, down_weight):
     tok_rows, features = upstream.shape
     experts = lax.axis_size("expert")
     hidden_units = down_weight.shape[1]
@@ -69,6 +345,23 @@
     return (grad_down[None], grad_hidden[None], grad_probs)
 
 
+def local(upstream, combine_weights, expert_ids, saved_hidden, down_weight):
+    tokens, features = upstream.shape
+    n = lax.axis_size("dp")
+    outer = n // INNER
+    every_token_to_both = (
+        lax.axis_size("expert") == 2
+        and expert_ids.shape[1] == 2
+        and saved_hidden.shape[1] == 2 * tokens
+        and tokens == LANES
+    )
+    splits = n == 4 * INNER and features % (n * 16) == 0 and features % (outer * LANES) == 0
+    hidden_units = down_weight.shape[1]
+    if every_token_to_both and splits and hidden_units % (4 * LANES) == 0:
+        return both_experts(upstream, combine_weights, expert_ids, saved_hidden, down_weight)
+    return any_experts(upstream, combine_weights, expert_ids, saved_hidden, down_weight)
+
+
 def solution(mesh):
     return jax.shard_map(
         local,

time: 213 us -> 71.9 us (0.34)
  waiting for transfers between devices: 154 us -> 33.8 us
  matrix products: 22 us -> 0 us
  Pallas kernels: 0 us -> 15.5 us
  between operations: 14.1 us -> 0.77 us
  starting transfers between devices: 11.2 us -> 21.5 us
  other arithmetic: 5.93 us -> 0 us
  local copies, waits for them, and re-layouts: 5.68 us -> 0.01 us
    reduce_scatter x1 -> x0, waiting for transfers between devices: 131 us -> none  [local(): lax.psum_scatter(contract_rows(scaled, activated), 'dp', scatter_dimensio...]
    ppermute x0 -> x28, waiting for transfers between devices: none -> 33.8 us  [the longest x23 26.4 us: both_experts(): lax.ppermute(value, 'dp', [(i, i ^ bit) for i in range(n)])]
    all_to_all x3 -> x0, waiting for transfers between devices: 22.4 us -> none  [the longest x1 21.9 us: local(): lax.all_to_all(send_rows, 'expert', split_axis=0, concat_axis=0, tiled=True)]
    dot_general x3 -> x0, matrix products: 22 us -> none  [the longest x1 8.72 us: contract_rows(): lax.dot_general(left_rows, right_rows, (((0,), (0,)), ((), ())), preferre...]
    ppermute x0 -> x28, starting transfers between devices: none -> 21.5 us  [the longest x23 15.7 us: both_experts(): lax.ppermute(value, 'dp', [(i, i ^ bit) for i in range(n)])]
    pallas_call x0 -> x11, Pallas kernels: none -> 15.5 us  [call(): pl.pallas_call(body, out_shape=outs, in_specs=specs + [ANY] * len(waits),...]
    all_to_all x3 -> x0, starting transfers between devices: 11.1 us -> none  [the longest x1 4.21 us: local(): lax.all_to_all(send_weight, 'expert', split_axis=0, concat_axis=0, tiled=...]
    gather x2 -> x0, local copies, waits for them, and re-layouts: 4.14 us -> none  [the longest x1 2.42 us: local(): jnp.take_along_axis(token_weight.T, source, axis=1)]
  transfers between devices with their start and end apart: 4 -> 28, of which waited for: 3 -> 12; matrix products, arithmetic and copies ran while one was open for 9% -> 0% of each run, Pallas kernels for 0% -> 15%
where the time goes in v2:
time: 71.9 us; the launch traced here: 71.5 us
  waiting for transfers between devices  33.8 us (47%)
  starting transfers between devices  21.5 us (30%)
  Pallas kernels  15.5 us (22%)
  between operations  0.77 us (1%)
    ppermute x23, waiting for transfers between devices, both_experts(): lax.ppermute(value, 'dp', [(i, i ^ bit) for i in range(n)])  26.4 us
    ppermute x23, starting transfers between devices, both_experts(): lax.ppermute(value, 'dp', [(i, i ^ bit) for i in range(n)])  15.7 us
    pallas_call x11, Pallas kernels, call(): pl.pallas_call(body, out_shape=outs, in_specs=specs + [ANY] * len(waits),...  15.5 us
    ppermute x5, waiting for transfers between devices, both_experts(): cross = lambda value: lax.ppermute(value, 'expert', flip)  7.36 us
    ppermute x5, starting transfers between devices, both_experts(): cross = lambda value: lax.ppermute(value, 'expert', flip)  5.83 us
  transfers between devices with their start and end apart: 28, of which 12 were waited for; matrix products, arithmetic and copies ran while one was open for 0% of the time, Pallas kernels for 15%

profile of v2, /device:TPU:0, one launch (start us, length us, event | category | flops | bytes accessed | tf_op | source)
XLA Modules:
  0.0 71.5 jit_solution(4661704226412910186)
XLA Ops:
  0.6 2.8 %shard_map.76 = (bf16[128,1024]{1,0:T(8,128)(2,1)S(1)}, f32[128,128]{1,0:T(8,128)S(1)}, bf16[256,512]{1,0:T(8,128)(2,1)S(1)}, bf16[256,512]{1,0:T(8,128)(2,1)S(1...) custom-call(bf16[128,3584]{1,0:T(8,128)(2,1)} %refs_1_.1, ...), custom_call_target="tpu_custom_call" | custom-call | tf_op jit(solution)/shard_map/pallas_call | solution.py:44
  3.4 3.0 %collective-permute-start = (bf16[128,1024]{1,0:T(8,128)(2,1)S(1)}, bf16[128,1024]{1,0:T(8,128)(2,1)S(1)}, u32[]{:S(2)}, u32[]{:S(2)}) collective-permute-start(bf16[128,1024]{1,0:T(8,128)(2,1)S(1)} %get-tuple-element.41), channel_id=1, source_target_pairs={{0,16},{16,0},{1,17},{17,1},{2,18},{18,2},{3,19},{19,3},{4,20},{20... | collective-permute-start | bytes 786440 | tf_op jit(solution)/shard_map/ppermute | solution.py:204
  6.4 1.5 %collective-permute-start.5 = (bf16[256,512]{1,0:T(8,128)(2,1)S(1)}, bf16[256,512]{1,0:T(8,128)(2,1)S(1)}, u32[]{:S(2)}, u32[]{:S(2)}) collective-permute-start(bf16[256,512]{1,0:T(8,128)(2,1)S(1)} %get-tuple-element.47.refs_4_), channel_id=1, source_target_pairs={{0,2},{1,3},{2,0},{3,1},{4,6},{5,7},{6,4},{7,5},{8,10},{9,11},{10,... | collective-permute-start | bytes 786440 | tf_op jit(solution)/shard_map/ppermute | solution.py:205
  7.9 0.5 collective-permute-start.14
  8.4 4.3 %collective-permute-done.refs_0_.refs_1_.refs_9_.refs_10_.refs_13_.refs_7_ = bf16[128,1024]{1,0:T(8,128)(2,1)S(1)} collective-permute-done((bf16[128,1024]{1,0:T(8,128)(2,1)S(1)}, bf16[128,1024]{1,0:T(8,128)(2,1)S(1)}, u32[]{:S(2)}, u32[]{:S(2)}) %collective-permute-start) | collective-permute-done | bytes 262176 | tf_op jit(solution)/shard_map/ppermute | solution.py:204
  12.7 0.2 shard_map.77
  13.0 2.7 %collective-permute-done.5.refs_6_ = bf16[256,512]{1,0:T(8,128)(2,1)S(1)} collective-permute-done((bf16[256,512]{1,0:T(8,128)(2,1)S(1)}, bf16[256,512]{1,0:T(8,128)(2,1)S(1)}, u32[]{:S(2)}, u32[]{:S(2)}) %collective-permute-start.5) | collective-permute-done | bytes 262176 | tf_op jit(solution)/shard_map/ppermute | solution.py:205
  15.6 0.0 collective-permute-start.6
  15.6 0.5 collective-permute-start.4
  16.1 0.0 collective-permute-start.1
  16.1 0.0 collective-permute-start.7
  16.2 3.6 %collective-permute-done.14.refs_6_.refs_10_ = bf16[256,512]{1,0:T(8,128)(2,1)S(1)} collective-permute-done((bf16[256,512]{1,0:T(8,128)(2,1)S(1)}, bf16[256,512]{1,0:T(8,128)(2,1)S(1)}, u32[]{:S(2)}, u32[]{:S(2)}) %collective-permute-start.14) | collective-permute-done | bytes 262176 | tf_op jit(solution)/shard_map/ppermute | solution.py:205
  19.8 0.0 collective-permute-start.13
  19.8 0.0 collective-permute-done.6.refs_7_
  19.8 0.5 collective-permute-start.15
  20.3 0.0 collective-permute-done.4.refs_5_
  20.3 1.5 %collective-permute-start.2 = (bf16[224,256]{1,0:T(8,128)(2,1)S(1)}, bf16[224,256]{1,0:T(8,128)(2,1)S(1)}, u32[]{:S(2)}, u32[]{:S(2)}) collective-permute-start(bf16[224,256]{1,0:T(8,128)(2,1)S(1)} %get-tuple-element.45), channel_id=1, source_target_pairs={{0,2},{1,3},{2,0},{3,1},{4,6},{5,7},{6,4},{7,5},{8,10},{9,11},{10,... | collective-permute-start | bytes 344072 | tf_op jit(solution)/shard_map/ppermute | solution.py:205
  21.8 0.0 collective-permute-done.1.refs_1_
  21.8 0.0 collective-permute-start.3
  21.8 4.2 %collective-permute-done.2.refs_2_ = bf16[224,256]{1,0:T(8,128)(2,1)S(1)} collective-permute-done((bf16[224,256]{1,0:T(8,128)(2,1)S(1)}, bf16[224,256]{1,0:T(8,128)(2,1)S(1)}, u32[]{:S(2)}, u32[]{:S(2)}) %collective-permute-start.2) | collective-permute-done | bytes 114720 | tf_op jit(solution)/shard_map/ppermute | solution.py:205
  26.0 1.2 %collective-permute-done.3.refs_3_ = bf16[224,256]{1,0:T(8,128)(2,1)S(1)} collective-permute-done((bf16[224,256]{1,0:T(8,128)(2,1)S(1)}, bf16[224,256]{1,0:T(8,128)(2,1)S(1)}, u32[]{:S(2)}, u32[]{:S(2)}) %collective-permute-start.3) | collective-permute-done | bytes 114720 | tf_op jit(solution)/shard_map/ppermute | solution.py:205
  27.3 0.0 collective-permute-done.7.refs_8_.refs_6_
  27.3 0.4 shard_map.78
  27.7 0.6 collective-permute-start.12
  28.3 1.5 %collective-permute-start.11 = (bf16[224,512]{1,0:T(8,128)(2,1)S(1)}, bf16[224,512]{1,0:T(8,128)(2,1)S(1)}, u32[]{:S(2)}, u32[]{:S(2)}) collective-permute-start(bf16[224,512]{1,0:T(8,128)(2,1)S(1)} %get-tuple-element.56.refs_8_), channel_id=1, source_target_pairs={{0,4},{1,5},{2,6},{3,7},{4,0},{5,1},{6,2},{7,3},{8,12},{9,13},{10,... | collective-permute-start | bytes 688136 | tf_op jit(solution)/shard_map/ppermute | solution.py:205
  29.9 0.0 collective-permute-start.8
  29.9 0.0 collective-permute-done.13.refs_5_.refs_9_
  29.9 1.4 %collective-permute-start.9 = (bf16[224,256]{1,0:T(8,128)(2,1)S(1)}, bf16[224,256]{1,0:T(8,128)(2,1)S(1)}, u32[]{:S(2)}, u32[]{:S(2)}) collective-permute-start(bf16[224,256]{1,0:T(8,128)(2,1)S(1)} %get-tuple-element.54), channel_id=1, source_target_pairs={{0,2},{1,3},{2,0},{3,1},{4,6},{5,7},{6,4},{7,5},{8,10},{9,11},{10,... | collective-permute-start | bytes 344072 | tf_op jit(solution)/shard_map/ppermute | solution.py:205
  31.3 0.0 collective-permute-done.15.refs_7_.refs_11_
  31.3 0.4 collective-permute-start.10
  31.7 0.4 shard_map.79.refs_12_
  32.1 0.0 collective-permute-done.8.refs_1_
  32.1 0.5 collective-permute-start.20
  32.7 3.1 %collective-permute-done.9.refs_2_ = bf16[224,256]{1,0:T(8,128)(2,1)S(1)} collective-permute-done((bf16[224,256]{1,0:T(8,128)(2,1)S(1)}, bf16[224,256]{1,0:T(8,128)(2,1)S(1)}, u32[]{:S(2)}, u32[]{:S(2)}) %collective-permute-start.9) | collective-permute-done | bytes 114720 | tf_op jit(solution)/shard_map/ppermute | solution.py:205
  35.8 1.7 %collective-permute-done.10.refs_3_ = bf16[224,256]{1,0:T(8,128)(2,1)S(1)} collective-permute-done((bf16[224,256]{1,0:T(8,128)(2,1)S(1)}, bf16[224,256]{1,0:T(8,128)(2,1)S(1)}, u32[]{:S(2)}, u32[]{:S(2)}) %collective-permute-start.10) | collective-permute-done | bytes 114720 | tf_op jit(solution)/shard_map/ppermute | solution.py:205
  37.5 0.0 collective-permute-done.12.refs_9_.refs_5_
  37.5 0.0 collective-permute-done.11.refs_8_
  37.5 0.4 shard_map.80
  37.9 1.6 %collective-permute-start.19 = (bf16[128,896]{1,0:T(8,128)(2,1)S(1)}, bf16[128,896]{1,0:T(8,128)(2,1)S(1)}, u32[]{:S(2)}, u32[]{:S(2)}) collective-permute-start(bf16[128,896]{1,0:T(8,128)(2,1)S(1)} %get-tuple-element.67), channel_id=1, source_target_pairs={{0,16},{16,0},{1,17},{17,1},{2,18},{18,2},{3,19},{19,3},{4,20},{20... | collective-permute-start | bytes 688136 | tf_op jit(solution)/shard_map/ppermute | solution.py:204
  39.5 0.2 collective-permute-start.16
  39.7 1.3 %collective-permute-start.17 = (bf16[224,256]{1,0:T(8,128)(2,1)S(1)}, bf16[224,256]{1,0:T(8,128)(2,1)S(1)}, u32[]{:S(2)}, u32[]{:S(2)}) collective-permute-start(bf16[224,256]{1,0:T(8,128)(2,1)S(1)} %get-tuple-element.64), channel_id=1, source_target_pairs={{0,2},{1,3},{2,0},{3,1},{4,6},{5,7},{6,4},{7,5},{8,10},{9,11},{10,... | collective-permute-start | bytes 344072 | tf_op jit(solution)/shard_map/ppermute | solution.py:205
  41.0 0.4 collective-permute-start.18
  41.3 0.0 collective-permute-done.20.refs_8_
  41.3 0.4 shard_map.81.refs_15_
  41.8 0.0 copy-start
  41.8 0.0 collective-permute-done.16.refs_1_
  41.8 3.9 %collective-permute-done.17.refs_2_ = bf16[224,256]{1,0:T(8,128)(2,1)S(1)} collective-permute-done((bf16[224,256]{1,0:T(8,128)(2,1)S(1)}, bf16[224,256]{1,0:T(8,128)(2,1)S(1)}, u32[]{:S(2)}, u32[]{:S(2)}) %collective-permute-start.17) | collective-permute-done | bytes 114720 | tf_op jit(solution)/shard_map/ppermute | solution.py:205
  45.7 1.2 %collective-permute-done.18.refs_3_ = bf16[224,256]{1,0:T(8,128)(2,1)S(1)} collective-permute-done((bf16[224,256]{1,0:T(8,128)(2,1)S(1)}, bf16[224,256]{1,0:T(8,128)(2,1)S(1)}, u32[]{:S(2)}, u32[]{:S(2)}) %collective-permute-start.18) | collective-permute-done | bytes 114720 | tf_op jit(solution)/shard_map/ppermute | solution.py:205
  46.9 0.0 collective-permute-done.19.refs_12_.refs_4_
  46.9 0.6 shard_map.82
  47.5 1.1 %collective-permute-start.24 = (bf16[224,1024]{1,0:T(8,128)(2,1)S(1)}, bf16[224,1024]{1,0:T(8,128)(2,1)S(1)}, u32[]{:S(2)}, u32[]{:S(2)}) collective-permute-start(bf16[224,1024]{1,0:T(8,128)(2,1)S(1)} %get-tuple-element.75.refs_8_), channel_id=1, source_target_pairs={{0,4},{1,5},{2,6},{3,7},{4,0},{5,1},{6,2},{7,3},{8,12},{9,13},{10,... | collective-permute-start | bytes 1376264 | tf_op jit(solution)/shard_map/ppermute | solution.py:205
  48.6 2.6 %collective-permute-start.25 = (bf16[224,512]{1,0:T(8,128)(2,1)S(1)}, bf16[224,512]{1,0:T(8,128)(2,1)S(1)}, u32[]{:S(2)}, u32[]{:S(2)}) collective-permute-start(bf16[224,512]{1,0:T(8,128)(2,1)S(1)} %get-tuple-element.69.refs_9_), channel_id=1, source_target_pairs={{0,8},{1,9},{2,10},{3,11},{4,12},{5,13},{6,14},{7,15},{8,0},{9,1},... | collective-permute-start | bytes 688136 | tf_op jit(solution)/shard_map/ppermute | solution.py:205
  51.2 0.3 collective-permute-start.26
  51.6 7.9 %shard_map.83 = (bf16[256,2048]{1,0:T(8,128)(2,1)}, f32[8,128]{1,0:T(8,128)S(1)}, f32[8,128]{1,0:T(8,128)S(1)}) custom-call(f32[128,128]{1,0:T(8,128)S(1)} %get-tuple-element.74.refs_0_, bf16[128,3584]{1,0:T(8,128)(2,1)} %refs_1_.1, bf16[256,2048]{1,0:T(8,128)(2,1)} %bitcast.11, bf16[1024,3584]{1,0:T(8,128)(2,1)} %bitcast.9, ...), custom_call_target="tpu_custom_call" | custom-call | tf_op jit(solution)/shard_map/pallas_call | solution.py:44
  59.5 0.6 collective-permute-start.27
  60.1 3.1 %collective-permute-done.27.refs_2_ = f32[8,128]{1,0:T(8,128)S(1)} collective-permute-done((f32[8,128]{1,0:T(8,128)S(1)}, f32[8,128]{1,0:T(8,128)S(1)}, u32[]{:S(2)}, u32[]{:S(2)}) %collective-permute-start.27) | collective-permute-done | bytes 4128 | tf_op jit(solution)/shard_map/ppermute | solution.py:204
  63.2 1.2 %collective-permute-start.22 = (bf16[224,256]{1,0:T(8,128)(2,1)S(1)}, bf16[224,256]{1,0:T(8,128)(2,1)S(1)}, u32[]{:S(2)}, u32[]{:S(2)}) collective-permute-start(bf16[224,256]{1,0:T(8,128)(2,1)S(1)} %get-tuple-element.72), channel_id=1, source_target_pairs={{0,2},{1,3},{2,0},{3,1},{4,6},{5,7},{6,4},{7,5},{8,10},{9,11},{10,... | collective-permute-start | bytes 344072 | tf_op jit(solution)/shard_map/ppermute | solution.py:205
  64.4 0.0 collective-permute-start.23
  64.4 0.6 shard_map.86
  65.0 3.6 %collective-permute-done.22.refs_2_ = bf16[224,256]{1,0:T(8,128)(2,1)S(1)} collective-permute-done((bf16[224,256]{1,0:T(8,128)(2,1)S(1)}, bf16[224,256]{1,0:T(8,128)(2,1)S(1)}, u32[]{:S(2)}, u32[]{:S(2)}) %collective-permute-start.22) | collective-permute-done | bytes 114720 | tf_op jit(solution)/shard_map/ppermute | solution.py:205
  68.6 1.2 %collective-permute-done.23.refs_3_ = bf16[224,256]{1,0:T(8,128)(2,1)S(1)} collective-permute-done((bf16[224,256]{1,0:T(8,128)(2,1)S(1)}, bf16[224,256]{1,0:T(8,128)(2,1)S(1)}, u32[]{:S(2)}, u32[]{:S(2)}) %collective-permute-start.23) | collective-permute-done | bytes 114720 | tf_op jit(solution)/shard_map/ppermute | solution.py:205
  69.8 0.6 shard_map.84.refs_0_
  70.4 0.0 collective-permute-done.25.refs_2_
  70.4 1.1 %shard_map.85 = f32[224,1024]{1,0:T(8,128)} custom-call(f32[224,1024]{1,0:T(8,128)S(1)} %shard_map.84.refs_0_, bf16[224,1024]{1,0:T(8,128)(2,1)S(1)} %collective-permute-done.24.refs_1_, bf16[224,512]{1,0:T(8,128)(2,1)S(1)} %collective-permute-done.25.refs_2_, bf16[224,512]{1,0:T(8,128)(2,1)S(1)} %collective-permute-done.26.refs_3_), custom_call_target="tpu_custom_call" | custom-call | tf_op jit(solution)/shard_map/pallas_call | solution.py:44
  (5 shorter events, 0.0 us)
Async XLA Ops:
  3.4 9.3 %collective-permute-start = (bf16[128,1024]{1,0:T(8,128)(2,1)S(1)}, bf16[128,1024]{1,0:T(8,128)(2,1)S(1)}, u32[]{:S(2)}, u32[]{:S(2)}) collective-permute-start(bf16[128,1024]{1,0:T(8,128)(2,1)S(1)} %get-tuple-element.41), channel_id=1, source_target_pairs={{0,16},{16,0},{1,17},{17,1},{2,18},{18,2},{3,19},{19,3},{4,20},{20... | collective-permute-start | bytes 786440 | tf_op jit(solution)/shard_map/ppermute | solution.py:204
  6.4 9.2 %collective-permute-start.5 = (bf16[256,512]{1,0:T(8,128)(2,1)S(1)}, bf16[256,512]{1,0:T(8,128)(2,1)S(1)}, u32[]{:S(2)}, u32[]{:S(2)}) collective-permute-start(bf16[256,512]{1,0:T(8,128)(2,1)S(1)} %get-tuple-element.47.refs_4_), channel_id=1, source_target_pairs={{0,2},{1,3},{2,0},{3,1},{4,6},{5,7},{6,4},{7,5},{8,10},{9,11},{10,... | collective-permute-start | bytes 786440 | tf_op jit(solution)/shard_map/ppermute | solution.py:205
  7.9 11.9 %collective-permute-start.14 = (bf16[256,512]{1,0:T(8,128)(2,1)S(1)}, bf16[256,512]{1,0:T(8,128)(2,1)S(1)}, u32[]{:S(2)}, u32[]{:S(2)}) collective-permute-start(bf16[256,512]{1,0:T(8,128)(2,1)S(1)} %get-tuple-element.60.refs_4_.refs_8_), channel_id=1, source_target_pairs={{0,2},{1,3},{2,0},{3,1},{4,6},{5,7},{6,4},{7,5},{8,10},{9,11},{10,... | collective-permute-start | bytes 786440 | tf_op jit(solution)/shard_map/ppermute | solution.py:205
  15.6 4.2 %collective-permute-start.6 = (bf16[256,512]{1,0:T(8,128)(2,1)S(1)}, bf16[256,512]{1,0:T(8,128)(2,1)S(1)}, u32[]{:S(2)}, u32[]{:S(2)}) collective-permute-start(bf16[256,512]{1,0:T(8,128)(2,1)S(1)} %collective-permute-done.5.refs_6_), channel_id=1, source_target_pairs={{0,1},{1,0},{2,3},{3,2},{4,5},{5,4},{6,7},{7,6},{8,9},{9,8},{10,11... | collective-permute-start | bytes 786440 | tf_op jit(solution)/shard_map/ppermute | solution.py:205
  15.6 4.7 %collective-permute-start.4 = (bf16[256,512]{1,0:T(8,128)(2,1)S(1)}, bf16[256,512]{1,0:T(8,128)(2,1)S(1)}, u32[]{:S(2)}, u32[]{:S(2)}) collective-permute-start(bf16[256,512]{1,0:T(8,128)(2,1)S(1)} %get-tuple-element.47.refs_4_), channel_id=1, source_target_pairs={{0,1},{1,0},{2,3},{3,2},{4,5},{5,4},{6,7},{7,6},{8,9},{9,8},{10,11... | collective-permute-start | bytes 786440 | tf_op jit(solution)/shard_map/ppermute | solution.py:205
  16.1 5.7 %collective-permute-start.1 = (bf16[224,256]{1,0:T(8,128)(2,1)S(1)}, bf16[224,256]{1,0:T(8,128)(2,1)S(1)}, u32[]{:S(2)}, u32[]{:S(2)}) collective-permute-start(bf16[224,256]{1,0:T(8,128)(2,1)S(1)} %get-tuple-element.44), channel_id=1, source_target_pairs={{0,1},{1,0},{2,3},{3,2},{4,5},{5,4},{6,7},{7,6},{8,9},{9,8},{10,11... | collective-permute-start | bytes 344072 | tf_op jit(solution)/shard_map/ppermute | solution.py:205
  16.1 11.1 %collective-permute-start.7 = (bf16[128,896]{1,0:T(8,128)(2,1)S(1)}, bf16[128,896]{1,0:T(8,128)(2,1)S(1)}, u32[]{:S(2)}, u32[]{:S(2)}) collective-permute-start(bf16[128,896]{1,0:T(8,128)(2,1)S(1)} %get-tuple-element.50), channel_id=1, source_target_pairs={{0,16},{16,0},{1,17},{17,1},{2,18},{18,2},{3,19},{19,3},{4,20},{20... | collective-permute-start | bytes 688136 | tf_op jit(solution)/shard_map/ppermute | solution.py:204
  19.8 10.1 %collective-permute-start.13 = (bf16[256,512]{1,0:T(8,128)(2,1)S(1)}, bf16[256,512]{1,0:T(8,128)(2,1)S(1)}, u32[]{:S(2)}, u32[]{:S(2)}) collective-permute-start(bf16[256,512]{1,0:T(8,128)(2,1)S(1)} %get-tuple-element.60.refs_4_.refs_8_), channel_id=1, source_target_pairs={{0,1},{1,0},{2,3},{3,2},{4,5},{5,4},{6,7},{7,6},{8,9},{9,8},{10,11... | collective-permute-start | bytes 786440 | tf_op jit(solution)/shard_map/ppermute | solution.py:205
  19.8 11.5 %collective-permute-start.15 = (bf16[256,512]{1,0:T(8,128)(2,1)S(1)}, bf16[256,512]{1,0:T(8,128)(2,1)S(1)}, u32[]{:S(2)}, u32[]{:S(2)}) collective-permute-start(bf16[256,512]{1,0:T(8,128)(2,1)S(1)} %collective-permute-done.14.refs_6_.refs_10_), channel_id=1, source_target_pairs={{0,1},{1,0},{2,3},{3,2},{4,5},{5,4},{6,7},{7,6},{8,9},{9,8},{10,11... | collective-permute-start | bytes 786440 | tf_op jit(solution)/shard_map/ppermute | solution.py:205
  20.3 5.7 %collective-permute-start.2 = (bf16[224,256]{1,0:T(8,128)(2,1)S(1)}, bf16[224,256]{1,0:T(8,128)(2,1)S(1)}, u32[]{:S(2)}, u32[]{:S(2)}) collective-permute-start(bf16[224,256]{1,0:T(8,128)(2,1)S(1)} %get-tuple-element.45), channel_id=1, source_target_pairs={{0,2},{1,3},{2,0},{3,1},{4,6},{5,7},{6,4},{7,5},{8,10},{9,11},{10,... | collective-permute-start | bytes 344072 | tf_op jit(solution)/shard_map/ppermute | solution.py:205
  21.8 5.4 %collective-permute-start.3 = (bf16[224,256]{1,0:T(8,128)(2,1)S(1)}, bf16[224,256]{1,0:T(8,128)(2,1)S(1)}, u32[]{:S(2)}, u32[]{:S(2)}) collective-permute-start(bf16[224,256]{1,0:T(8,128)(2,1)S(1)} %get-tuple-element.46), channel_id=1, source_target_pairs={{0,3},{1,2},{2,1},{3,0},{4,7},{5,6},{6,5},{7,4},{8,11},{9,10},{10,... | collective-permute-start | bytes 344072 | tf_op jit(solution)/shard_map/ppermute | solution.py:205
  27.7 9.8 %collective-permute-start.12 = (bf16[128,896]{1,0:T(8,128)(2,1)S(1)}, bf16[128,896]{1,0:T(8,128)(2,1)S(1)}, u32[]{:S(2)}, u32[]{:S(2)}) collective-permute-start(bf16[128,896]{1,0:T(8,128)(2,1)S(1)} %get-tuple-element.58), channel_id=1, source_target_pairs={{0,16},{16,0},{1,17},{17,1},{2,18},{18,2},{3,19},{19,3},{4,20},{20... | collective-permute-start | bytes 688136 | tf_op jit(solution)/shard_map/ppermute | solution.py:204
  28.3 9.2 %collective-permute-start.11 = (bf16[224,512]{1,0:T(8,128)(2,1)S(1)}, bf16[224,512]{1,0:T(8,128)(2,1)S(1)}, u32[]{:S(2)}, u32[]{:S(2)}) collective-permute-start(bf16[224,512]{1,0:T(8,128)(2,1)S(1)} %get-tuple-element.56.refs_8_), channel_id=1, source_target_pairs={{0,4},{1,5},{2,6},{3,7},{4,0},{5,1},{6,2},{7,3},{8,12},{9,13},{10,... | collective-permute-start | bytes 688136 | tf_op jit(solution)/shard_map/ppermute | solution.py:205
  29.9 2.3 %collective-permute-start.8 = (bf16[224,256]{1,0:T(8,128)(2,1)S(1)}, bf16[224,256]{1,0:T(8,128)(2,1)S(1)}, u32[]{:S(2)}, u32[]{:S(2)}) collective-permute-start(bf16[224,256]{1,0:T(8,128)(2,1)S(1)} %get-tuple-element.53), channel_id=1, source_target_pairs={{0,1},{1,0},{2,3},{3,2},{4,5},{5,4},{6,7},{7,6},{8,9},{9,8},{10,11... | collective-permute-start | bytes 344072 | tf_op jit(solution)/shard_map/ppermute | solution.py:205
  29.9 5.9 %collective-permute-start.9 = (bf16[224,256]{1,0:T(8,128)(2,1)S(1)}, bf16[224,256]{1,0:T(8,128)(2,1)S(1)}, u32[]{:S(2)}, u32[]{:S(2)}) collective-permute-start(bf16[224,256]{1,0:T(8,128)(2,1)S(1)} %get-tuple-element.54), channel_id=1, source_target_pairs={{0,2},{1,3},{2,0},{3,1},{4,6},{5,7},{6,4},{7,5},{8,10},{9,11},{10,... | collective-permute-start | bytes 344072 | tf_op jit(solution)/shard_map/ppermute | solution.py:205
  31.3 6.2 %collective-permute-start.10 = (bf16[224,256]{1,0:T(8,128)(2,1)S(1)}, bf16[224,256]{1,0:T(8,128)(2,1)S(1)}, u32[]{:S(2)}, u32[]{:S(2)}) collective-permute-start(bf16[224,256]{1,0:T(8,128)(2,1)S(1)} %get-tuple-element.55), channel_id=1, source_target_pairs={{0,3},{1,2},{2,1},{3,0},{4,7},{5,6},{6,5},{7,4},{8,11},{9,10},{10,... | collective-permute-start | bytes 344072 | tf_op jit(solution)/shard_map/ppermute | solution.py:205
  32.1 9.2 %collective-permute-start.20 = (bf16[224,512]{1,0:T(8,128)(2,1)S(1)}, bf16[224,512]{1,0:T(8,128)(2,1)S(1)}, u32[]{:S(2)}, u32[]{:S(2)}) collective-permute-start(bf16[224,512]{1,0:T(8,128)(2,1)S(1)} %shard_map.79.refs_12_), channel_id=1, source_target_pairs={{0,4},{1,5},{2,6},{3,7},{4,0},{5,1},{6,2},{7,3},{8,12},{9,13},{10,... | collective-permute-start | bytes 688136 | tf_op jit(solution)/shard_map/ppermute | solution.py:205
  37.9 8.9 %collective-permute-start.19 = (bf16[128,896]{1,0:T(8,128)(2,1)S(1)}, bf16[128,896]{1,0:T(8,128)(2,1)S(1)}, u32[]{:S(2)}, u32[]{:S(2)}) collective-permute-start(bf16[128,896]{1,0:T(8,128)(2,1)S(1)} %get-tuple-element.67), channel_id=1, source_target_pairs={{0,16},{16,0},{1,17},{17,1},{2,18},{18,2},{3,19},{19,3},{4,20},{20... | collective-permute-start | bytes 688136 | tf_op jit(solution)/shard_map/ppermute | solution.py:204
  39.5 2.3 %collective-permute-start.16 = (bf16[224,256]{1,0:T(8,128)(2,1)S(1)}, bf16[224,256]{1,0:T(8,128)(2,1)S(1)}, u32[]{:S(2)}, u32[]{:S(2)}) collective-permute-start(bf16[224,256]{1,0:T(8,128)(2,1)S(1)} %get-tuple-element.63), channel_id=1, source_target_pairs={{0,1},{1,0},{2,3},{3,2},{4,5},{5,4},{6,7},{7,6},{8,9},{9,8},{10,11... | collective-permute-start | bytes 344072 | tf_op jit(solution)/shard_map/ppermute | solution.py:205
  39.7 6.0 %collective-permute-start.17 = (bf16[224,256]{1,0:T(8,128)(2,1)S(1)}, bf16[224,256]{1,0:T(8,128)(2,1)S(1)}, u32[]{:S(2)}, u32[]{:S(2)}) collective-permute-start(bf16[224,256]{1,0:T(8,128)(2,1)S(1)} %get-tuple-element.64), channel_id=1, source_target_pairs={{0,2},{1,3},{2,0},{3,1},{4,6},{5,7},{6,4},{7,5},{8,10},{9,11},{10,... | collective-permute-start | bytes 344072 | tf_op jit(solution)/shard_map/ppermute | solution.py:205
  41.0 5.9 %collective-permute-start.18 = (bf16[224,256]{1,0:T(8,128)(2,1)S(1)}, bf16[224,256]{1,0:T(8,128)(2,1)S(1)}, u32[]{:S(2)}, u32[]{:S(2)}) collective-permute-start(bf16[224,256]{1,0:T(8,128)(2,1)S(1)} %get-tuple-element.65), channel_id=1, source_target_pairs={{0,3},{1,2},{2,1},{3,0},{4,7},{5,6},{6,5},{7,4},{8,11},{9,10},{10,... | collective-permute-start | bytes 344072 | tf_op jit(solution)/shard_map/ppermute | solution.py:205
  41.8 22.6 %copy-start = (s32[128,2]{0,1:T(2,128)S(1)}, s32[128,2]{0,1:T(2,128)}, u32[]{:S(2)}) copy-start(s32[128,2]{0,1:T(2,128)} %param.7) | copy-start | bytes 3076
  47.5 22.9 %collective-permute-start.24 = (bf16[224,1024]{1,0:T(8,128)(2,1)S(1)}, bf16[224,1024]{1,0:T(8,128)(2,1)S(1)}, u32[]{:S(2)}, u32[]{:S(2)}) collective-permute-start(bf16[224,1024]{1,0:T(8,128)(2,1)S(1)} %get-tuple-element.75.refs_8_), channel_id=1, source_target_pairs={{0,4},{1,5},{2,6},{3,7},{4,0},{5,1},{6,2},{7,3},{8,12},{9,13},{10,... | collective-permute-start | bytes 1376264 | tf_op jit(solution)/shard_map/ppermute | solution.py:205
  48.6 15.7 %collective-permute-start.21 = (bf16[224,256]{1,0:T(8,128)(2,1)S(1)}, bf16[224,256]{1,0:T(8,128)(2,1)S(1)}, u32[]{:S(2)}, u32[]{:S(2)}) collective-permute-start(bf16[224,256]{1,0:T(8,128)(2,1)S(1)} %get-tuple-element.71), channel_id=1, source_target_pairs={{0,1},{1,0},{2,3},{3,2},{4,5},{5,4},{6,7},{7,6},{8,9},{9,8},{10,11... | collective-permute-start | bytes 344072 | tf_op jit(solution)/shard_map/ppermute | solution.py:205
  48.6 21.8 %collective-permute-start.25 = (bf16[224,512]{1,0:T(8,128)(2,1)S(1)}, bf16[224,512]{1,0:T(8,128)(2,1)S(1)}, u32[]{:S(2)}, u32[]{:S(2)}) collective-permute-start(bf16[224,512]{1,0:T(8,128)(2,1)S(1)} %get-tuple-element.69.refs_9_), channel_id=1, source_target_pairs={{0,8},{1,9},{2,10},{3,11},{4,12},{5,13},{6,14},{7,15},{8,0},{9,1},... | collective-permute-start | bytes 688136 | tf_op jit(solution)/shard_map/ppermute | solution.py:205
  51.2 19.2 %collective-permute-start.26 = (bf16[224,512]{1,0:T(8,128)(2,1)S(1)}, bf16[224,512]{1,0:T(8,128)(2,1)S(1)}, u32[]{:S(2)}, u32[]{:S(2)}) collective-permute-start(bf16[224,512]{1,0:T(8,128)(2,1)S(1)} %shard_map.81.refs_15_), channel_id=1, source_target_pairs={{0,8},{1,9},{2,10},{3,11},{4,12},{5,13},{6,14},{7,15},{8,0},{9,1},... | collective-permute-start | bytes 688136 | tf_op jit(solution)/shard_map/ppermute | solution.py:205
  59.5 3.7 %collective-permute-start.27 = (f32[8,128]{1,0:T(8,128)S(1)}, f32[8,128]{1,0:T(8,128)S(1)}, u32[]{:S(2)}, u32[]{:S(2)}) collective-permute-start(f32[8,128]{1,0:T(8,128)S(1)} %get-tuple-element.78), channel_id=1, source_target_pairs={{0,16},{16,0},{1,17},{17,1},{2,18},{18,2},{3,19},{19,3},{4,20},{20... | collective-permute-start | bytes 12296 | tf_op jit(solution)/shard_map/ppermute | solution.py:204
  63.2 5.4 %collective-permute-start.22 = (bf16[224,256]{1,0:T(8,128)(2,1)S(1)}, bf16[224,256]{1,0:T(8,128)(2,1)S(1)}, u32[]{:S(2)}, u32[]{:S(2)}) collective-permute-start(bf16[224,256]{1,0:T(8,128)(2,1)S(1)} %get-tuple-element.72), channel_id=1, source_target_pairs={{0,2},{1,3},{2,0},{3,1},{4,6},{5,7},{6,4},{7,5},{8,10},{9,11},{10,... | collective-permute-start | bytes 344072 | tf_op jit(solution)/shard_map/ppermute | solution.py:205
  64.4 5.4 %collective-permute-start.23 = (bf16[224,256]{1,0:T(8,128)(2,1)S(1)}, bf16[224,256]{1,0:T(8,128)(2,1)S(1)}, u32[]{:S(2)}, u32[]{:S(2)}) collective-permute-start(bf16[224,256]{1,0:T(8,128)(2,1)S(1)} %get-tuple-element.73), channel_id=1, source_target_pairs={{0,3},{1,2},{2,1},{3,0},{4,7},{5,6},{6,5},{7,4},{8,11},{9,10},{10,... | collective-permute-start | bytes 344072 | tf_op jit(solution)/shard_map/ppermute | solution.py:205

commit v3 on v2

--- a/solution.py
+++ b/solution.py
@@ -26,7 +26,7 @@
     return lax.optimization_barrier((value, *others))[0]
 
 
-def call(*jobs, waits=(), vmem=8, cost=0):
+def call(*jobs, waits=(), vmem=8):
     specs = [spec for job in jobs for spec in job[4] or [VMEM] * len(job[1])]
     args = [arg for job in jobs for arg in job[1]]
     outs = tuple(jax.ShapeDtypeStruct(*out) for job in jobs for out in job[2])
@@ -48,7 +48,6 @@
         out_specs=tuple(VMEM for _ in outs),
         scratch_shapes=scratch,
         compiler_params=pltpu.CompilerParams(vmem_limit_bytes=vmem << 20),
-        cost_estimate=pl.CostEstimate(flops=cost, bytes_accessed=cost, transcendentals=0),
     )(*[place(*pair) for pair in zip(args, specs)], *waits)
 
 
@@ -57,18 +56,19 @@
     return pl.multiple_of((group ^ k) * chunk, LANES)
 
 
-def prepare_kernel(outer, chunk, up_hbm, hidden_hbm, ids_ref, weights_ref, *refs):
-    first_ref, column_ref, act_refs = refs[0], refs[1], refs[2:4]
-    own_refs, send_refs = refs[4 : 4 + outer], refs[4 + outer : -3]
+def prepare_kernel(pairs, chunk, up_hbm, hidden_hbm, ids_ref, weights_ref, *refs):
+    send_refs, column_ref, act_refs = refs[: len(pairs)], refs[len(pairs)], refs[len(pairs) + 1 : len(pairs) + 3]
+    own_refs = refs[len(pairs) + 3 : -3]
     up_ref, hidden_ref, sems = refs[-3:]
-    top = outer - 1
-    loads = []
-    for k in range(outer):
+    order = [k for pair in pairs for k in pair]
+    outer = len(order)
+    loads = {}
+    for k in order:
         cols = pl.ds(chunk_start(k, chunk), chunk)
-        loads.append(pltpu.make_async_copy(up_hbm.at[:, cols], up_ref.at[k], sems.at[k]))
-    loads.append(pltpu.make_async_copy(hidden_hbm, hidden_ref, sems.at[outer]))
-    for k in [top, outer] + list(range(top - 1, -1, -1)):
+        loads[k] = pltpu.make_async_copy(up_hbm.at[:, cols], up_ref.at[k], sems.at[k])
         loads[k].start()
+    stored = pltpu.make_async_copy(hidden_hbm, hidden_ref, sems.at[outer])
+    stored.start()
     expert = lax.axis_index("expert")
 
     def token_weight(of):
@@ -79,62 +79,64 @@
     weight = token_weight(expert)
     column_ref[...] = weight
     weight = weight[:, :1]
-    first_ref[:, chunk:] = token_weight(1 - expert).astype(jnp.bfloat16)
-    for k in range(top, -1, -1):
-        loads[k].wait()
-        rows = up_ref[k]
-        (send_refs[k] if k < top else first_ref)[:, :chunk] = rows
-        own_refs[k][...] = (weight * rows.astype(jnp.float32)).astype(jnp.bfloat16).T
-    loads[outer].wait()
+    send_refs[0][:, len(pairs[0]) * chunk :] = token_weight(1 - expert).astype(jnp.bfloat16)
+    for send_ref, pair in zip(send_refs, pairs):
+        for i, k in enumerate(pair):
+            loads[k].wait()
+            rows = up_ref[k]
+            send_ref[:, i * chunk : (i + 1) * chunk] = rows
+            own_refs[order.index(k)][...] = (weight * rows.astype(jnp.float32)).astype(jnp.bfloat16).T
+    stored.wait()
     half, hidden_units = hidden_ref.shape[0] // 2, hidden_ref.shape[1] // 2
     for part in range(2):
         source = pl.ds(pl.multiple_of((expert ^ part) * half, half), half)
-        for start, out_ref in zip((0, act_refs[0].shape[1]), act_refs):
-            stop = start + out_ref.shape[1]
-            gate = hidden_ref[source, start:stop].astype(jnp.float32)
-            up = hidden_ref[source, hidden_units + start : hidden_units + stop].astype(jnp.float32)
-            act = gate * jax.nn.sigmoid(gate) * up
-            out_ref[part * half : (part + 1) * half, :] = act.astype(jnp.bfloat16)
-
-
-def split_kernel(chunk, got_ref, first_ref, own_ref, *refs):
-    pays, scaled_ref = refs[:-1], refs[-1]
-    weight = first_ref[:, chunk : chunk + 1].astype(jnp.float32)
-    scaled = (weight * got_ref[:, :chunk].astype(jnp.float32)).astype(jnp.bfloat16)
-    scaled_ref[...] = scaled.T
+        gate = hidden_ref[source, :hidden_units].astype(jnp.float32)
+        up = hidden_ref[source, hidden_units:].astype(jnp.float32)
+        act = (gate * jax.nn.sigmoid(gate) * up).astype(jnp.bfloat16)
+        for i, act_ref in enumerate(act_refs):
+            width = act_ref.shape[1]
+            act_ref[part * half : (part + 1) * half, :] = act[:, i * width : (i + 1) * width]
+
+
+def split_kernel(chunk, got_ref, first_ref, *refs):
+    owns, pays, scaled_ref = refs[: -INNER - 1], refs[-INNER - 1 : -1], refs[-1]
+    column = first_ref.shape[1] - LANES
+    weight = first_ref[:, column : column + 1].astype(jnp.float32)
     piece = chunk // INNER
     mine = lax.axis_index("dp") % INNER
-    for j in range(INNER):
-        rows = pl.ds(pl.multiple_of((mine ^ j) * piece, 16), piece)
-        pays[j][:, :LANES] = own_ref[rows, :]
-        pays[j][:, LANES:] = scaled_ref[rows, :]
-
-
-def partial_kernel(*refs):
-    pays, acts, adds, out_ref = refs[:INNER], refs[INNER : 2 * INNER], refs[2 * INNER : -1], refs[-1]
-    total = None
-    for pay, act in zip(pays, acts):
-        term = jnp.dot(pay[...], act[...], preferred_element_type=jnp.float32)
-        total = term if total is None else total + term
+    for i, own_ref in enumerate(owns):
+        scaled = weight * got_ref[:, i * chunk : (i + 1) * chunk].astype(jnp.float32)
+        scaled_ref[...] = scaled.astype(jnp.bfloat16).T
+        for j in range(INNER):
+            rows = pl.ds(pl.multiple_of((mine ^ j) * piece, 16), piece)
+            pays[j][i * piece : (i + 1) * piece, :LANES] = own_ref[rows, :]
+            pays[j][i * piece : (i + 1) * piece, LANES:] = scaled_ref[rows, :]
+
+
+def parts_kernel(adds, *refs):
+    pays, acts, rest = refs[:INNER], refs[INNER : 3 * INNER], refs[3 * INNER :]
+    adds, outs = rest[:adds], rest[adds:]
+    total = []
+    for half in (acts[:INNER], acts[INNER:]):
+        terms = [jnp.dot(p[...], a[...], preferred_element_type=jnp.float32) for p, a in zip(pays, half)]
+        total.append(functools.reduce(jnp.add, terms))
+    total = jnp.concatenate(total, axis=1)
     for add in adds:
         total = total + add[...].astype(jnp.float32)
-    out_ref[...] = total.astype(out_ref.dtype)
-
-
-def whole_kernel(*refs):
-    pays, acts, out_ref = refs[:INNER], refs[INNER : 3 * INNER], refs[-1]
     start = 0
-    for part in (acts[:INNER], acts[INNER:]):
-        stop = start + part[0].shape[1]
-        partial_kernel(*pays, *part, out_ref.at[:, start:stop])
+    for out_ref in outs:
+        stop = start + out_ref.shape[1]
+        out_ref[...] = total[:, start:stop].astype(out_ref.dtype)
         start = stop
 
 
-def final_kernel(base_ref, side_ref, left_ref, right_ref, out_ref):
-    split = left_ref.shape[1]
-    for cols, ref in ((slice(0, split), left_ref), (slice(split, None), right_ref)):
-        both = side_ref[:, cols].astype(jnp.float32) + ref[...].astype(jnp.float32)
-        out_ref[:, cols] = base_ref[:, cols] + both
+def final_kernel(sides, base_ref, *refs):
+    terms, out_ref = refs[:-1], refs[-1]
+    side, last = [
+        jnp.concatenate([ref[...].astype(jnp.float32) for ref in part], axis=1)
+        for part in (terms[:sides], terms[sides:])
+    ]
+    out_ref[...] = base_ref[...] + (side + last)
 
 
 def probs_kernel(ids_ref, own_ref, back_ref, out_ref):
@@ -142,10 +144,10 @@
     out_ref[...] = jnp.where(mine, own_ref[:1], back_ref[:1])
 
 
-def hidden_kernel(outer, chunk, column_ref, up_hbm, hidden_hbm, w_hbm, *refs):
-    got_refs = refs[:outer]
-    out_ref, own_score, got_score = refs[outer : outer + 3]
-    routed_ref, hidden_ref, w_ref, sems = refs[outer + 3 :]
+def hidden_kernel(pairs, chunk, column_ref, up_hbm, hidden_hbm, w_hbm, *refs):
+    got_refs = refs[: len(pairs)]
+    out_ref, own_score, got_score = refs[len(pairs) : len(pairs) + 3]
+    routed_ref, hidden_ref, w_ref, sems = refs[len(pairs) + 3 :]
     tokens = up_hbm.shape[0]
     hidden_units = w_ref.shape[0]
     width = 2 * LANES
@@ -162,9 +164,11 @@
     stored.start()
     for load in loads[1:]:
         load.start()
-    for k in range(outer):
-        routed_ref[tokens:, pl.ds(chunk_start(k, chunk), chunk)] = got_refs[k][:, :chunk]
-    weights = [column_ref[:, :1], got_refs[outer - 1][:, chunk : chunk + 1].astype(jnp.float32)]
+    for got_ref, pair in zip(got_refs, pairs):
+        for i, k in enumerate(pair):
+            routed_ref[tokens:, pl.ds(chunk_start(k, chunk), chunk)] = got_ref[:, i * chunk : (i + 1) * chunk]
+    column = len(pairs[0]) * chunk
+    weights = [column_ref[:, :1], got_refs[0][:, column : column + 1].astype(jnp.float32)]
     scores = [None, None]
     top.wait()
     for i in range(blocks):
@@ -204,16 +208,16 @@
     cross = lambda value: lax.ppermute(value, "expert", flip)
     swap = lambda value, bit: lax.ppermute(value, "dp", [(i, i ^ bit) for i in range(n)])
     rows = stored.shape[0]
-    widths = (hidden_units // 2, hidden_units // 2)
     bf16, f32 = jnp.bfloat16, jnp.float32
+    pairs = ((3,), (2,), (1,), (0,))
+    sides = (hidden_units,)
 
     prepared = call((
-        functools.partial(prepare_kernel, outer, chunk),
+        functools.partial(prepare_kernel, pairs, chunk),
         [upstream, stored, ids, combine],
-        [((tokens, chunk + LANES), bf16), ((tokens, LANES), f32)]
-        + [((rows, width), bf16) for width in widths]
-        + [((chunk, tokens), bf16)] * outer
-        + [((tokens, chunk), bf16)] * (outer - 1),
+        [((tokens, chunk + LANES), bf16)] + [((tokens, chunk), bf16)] * 3
+        + [((tokens, LANES), f32)] + [((rows, hidden_units // 2), bf16)] * 2
+        + [((chunk, tokens), bf16)] * outer,
         [
             pltpu.VMEM((outer, tokens, chunk), bf16),
             pltpu.VMEM((rows, 2 * hidden_units), bf16),
@@ -221,52 +225,52 @@
         ],
         [HBM, HBM, LOAD, LOAD],
     ))
-    first, column, mine = prepared[0], prepared[1], prepared[2:4]
-    own, send = prepared[4 : 4 + outer], prepared[4 + outer :]
-
-    def split(k):
-        shapes = [((piece, 2 * tokens), bf16)] * INNER
-        scratch = [pltpu.VMEM((chunk, tokens), bf16)]
-        return functools.partial(split_kernel, chunk), [got[k], got[3], own[k]], shapes, scratch, None
-
-    def spread(pays):
-        return [pays[0]] + [swap(pays[j], j) for j in range(1, INNER)]
-
-    def partial(pays, h, *adds):
-        sides = [acts[h][j] for j in range(INNER)]
-        return partial_kernel, [*pays, *sides, *adds], [((piece, widths[h]), bf16)], [], None
-
-    def whole(pays, kind):
-        sides = [acts[h][j] for h in range(2) for j in range(INNER)]
-        return whole_kernel, [*pays, *sides], [((piece, hidden_units), kind)], [], None
-
-    got = {3: cross(first)}
-    acts = [{0: mine[h], 1: swap(mine[h], 1), 2: swap(mine[h], 2)} for h in range(2)]
-    pays = {}
-    cut = call(split(3))
-    pays[3] = spread(cut)
-    got[2] = cross(after(send[2], cut[0]))
-    acts[0][3] = swap(after(acts[0][2], cut[0]), 1)
-    acts[1][3] = swap(after(acts[1][2], acts[0][3]), 1)
-    far0, *cut = call(partial(pays[3], 0), split(2))
-    near0 = swap(far0, INNER)
-    pays[2] = spread(cut)
-    got[1] = cross(after(send[1], cut[0]))
-    far1, = call(partial(pays[3], 1), waits=(far0,))
-    near1 = swap(far1, INNER)
-    wide0, *cut = call(partial(pays[2], 0, near0), split(1), waits=(far1,))
-    last0 = swap(wide0, 2 * INNER)
-    pays[1] = spread(cut)
-    got[0] = cross(after(send[0], cut[0]))
-    wide1, = call(partial(pays[2], 1, near1), waits=(wide0,))
-    last1 = swap(wide1, 2 * INNER)
-    side, *cut = call(whole(pays[1], bf16), split(0), waits=(wide1,))
-    pays[0] = spread(cut)
+    send, column = prepared[:outer], prepared[outer]
+    mine, own = prepared[outer + 1 : outer + 3], prepared[outer + 3 :]
+
+    def split_job(i):
+        return (
+            functools.partial(split_kernel, chunk),
+            [got[i], got[0], own[i]],
+            [((piece, 2 * tokens), bf16)] * INNER,
+            [pltpu.VMEM((chunk, tokens), bf16)],
+            None,
+        )
+
+    def spread(cut):
+        return [cut[0]] + [swap(cut[j], j) for j in range(1, INNER)], cut[0]
+
+    def split(i, *waits):
+        return spread(call(split_job(i), waits=waits))
+
+    def parts(i, kind, cuts, *adds):
+        kernel = functools.partial(parts_kernel, len(adds))
+        args = [*pays[i], *acts[0], *acts[1], *adds]
+        return kernel, args, [((piece, width), kind) for width in cuts], [], None
+
+    got, pays, marks = {}, {}, {}
+    got[0] = cross(send[0])
+    acts = [[mine[h], swap(mine[h], 1), swap(mine[h], 2)] for h in range(2)]
+    pays[0], marks[0] = split(0)
+    got[1] = cross(after(send[1], marks[0]))
+    acts[0].append(swap(after(acts[0][2], marks[0]), 1))
+    acts[1].append(swap(after(acts[1][2], acts[0][3]), 1))
+    far, *cut = call(parts(0, bf16, (hidden_units,)), split_job(1))
+    near = swap(far, INNER)
+    pays[1], marks[1] = spread(cut)
+    got[2] = cross(after(send[2], acts[0][3]))
+    pays[2], marks[2] = split(2, far)
+    wide, = call(parts(1, bf16, (hidden_units,), near), waits=(marks[2],))
+    last = [swap(wide, 2 * INNER)]
+    got[3] = cross(after(send[3], marks[2]))
+    *side, _0, _1, _2, _3 = call(parts(2, bf16, sides), split_job(3), waits=(wide,))
+    pays[3], marks[3] = spread((_0, _1, _2, _3))
+    side = [swap(part, INNER) for part in side]
 
     grad_hidden, own_score, got_score = call(
         (
-            functools.partial(hidden_kernel, outer, chunk),
-            [column, upstream, stored, weights, *[got[k] for k in range(outer)]],
+            functools.partial(hidden_kernel, pairs, chunk),
+            [column, upstream, stored, weights, *[got[i] for i in range(outer)]],
             [(stored.shape, bf16), ((8, tokens), f32), ((8, tokens), f32)],
             [
                 pltpu.VMEM((rows, features), bf16),
@@ -276,13 +280,15 @@
             ],
             [VMEM, HBM, HBM, HBM] + [VMEM] * outer,
         ),
-        waits=(side,), vmem=18,
-    )
-    side = swap(side, INNER)
+        waits=(marks[3],), vmem=18,
+    )
     back_score = cross(got_score)
-    base, = call(whole(pays[0], f32), waits=(own_score,))
-    grad_probs, = call((probs_kernel, [ids, own_score, back_score], [(ids.shape, f32)], [], None))
-    grad_down, = call((final_kernel, [base, side, last0, last1], [((piece, hidden_units), f32)], [], None))
+    base, = call(parts(3, f32, (hidden_units,)), waits=(own_score,))
+    grad_probs, = call((probs_kernel, [ids, own_score, back_score], [(ids.shape, f32)], [], None), waits=last)
+    grad_down, = call((
+        functools.partial(final_kernel, len(side)), [base, *side, *last],
+        [((piece, hidden_units), f32)], [], None,
+    ))
     return grad_down[None], grad_hidden[None], grad_probs.T
 
 

time: 71.9 us -> 67.1 us (0.933)
  waiting for transfers between devices: 33.8 us -> 25.7 us
  starting transfers between devices: 21.5 us -> 25.2 us
    ppermute x23 -> x21, waiting for transfers between devices: 26.4 us -> 18.9 us  [both_experts(): lax.ppermute(value, 'dp', [(i, i ^ bit) for i in range(n)])]
    ppermute x23 -> x21, starting transfers between devices: 15.7 us -> 17.9 us  [both_experts(): lax.ppermute(value, 'dp', [(i, i ^ bit) for i in range(n)])]
    ppermute x5, starting transfers between devices: 5.83 us -> 7.36 us  [both_experts(): cross = lambda value: lax.ppermute(value, 'expert', flip)]
    pallas_call x11 -> x10, Pallas kernels: 15.5 us -> 15.2 us  [call(): pl.pallas_call(body, out_shape=outs, in_specs=specs + [ANY] * len(waits),...]
  transfers between devices with their start and end apart: 28 -> 26, of which waited for: 12 -> 13; matrix products, arithmetic and copies ran while one was open for 0% -> 0% of each run, Pallas kernels for 15% -> 17%
where the time goes in v3:
time: 67.1 us; the launch traced here: 66.9 us
  waiting for transfers between devices  25.7 us (38%)
  starting transfers between devices  25.2 us (38%)
  Pallas kernels  15.2 us (23%)
  between operations  0.74 us (1%)
    ppermute x21, waiting for transfers between devices, both_experts(): lax.ppermute(value, 'dp', [(i, i ^ bit) for i in range(n)])  18.9 us
    ppermute x21, starting transfers between devices, both_experts(): lax.ppermute(value, 'dp', [(i, i ^ bit) for i in range(n)])  17.9 us
    pallas_call x10, Pallas kernels, call(): pl.pallas_call(body, out_shape=outs, in_specs=specs + [ANY] * len(waits),...  15.2 us
    ppermute x5, starting transfers between devices, both_experts(): cross = lambda value: lax.ppermute(value, 'expert', flip)  7.36 us
    ppermute x5, waiting for transfers between devices, both_experts(): cross = lambda value: lax.ppermute(value, 'expert', flip)  6.76 us
  transfers between devices with their start and end apart: 26, of which 13 were waited for; matrix products, arithmetic and copies ran while one was open for 0% of the time, Pallas kernels for 17%

profile of v3, /device:TPU:0, one launch (start us, length us, event | category | flops | bytes accessed | tf_op | source)
XLA Modules:
  0.0 66.9 jit_solution(17944827506900067120)
XLA Ops:
  0.6 2.6 %shard_map.76 = (bf16[128,1024]{1,0:T(8,128)(2,1)S(1)}, bf16[128,896]{1,0:T(8,128)(2,1)S(1)}, bf16[128,896]{1,0:T(8,128)(2,1)S(1)}, bf16[128,896]{1,0:T(8,128)(2...) custom-call(bf16[128,3584]{1,0:T(8,128)(2,1)} %refs_1_.1, ...), custom_call_target="tpu_custom_call" | custom-call | tf_op jit(solution)/shard_map/pallas_call | solution.py:44
  3.3 3.0 %collective-permute-start.1 = (bf16[128,1024]{1,0:T(8,128)(2,1)S(1)}, bf16[128,1024]{1,0:T(8,128)(2,1)S(1)}, u32[]{:S(2)}, u32[]{:S(2)}) collective-permute-start(bf16[128,1024]{1,0:T(8,128)(2,1)S(1)} %get-tuple-element.42), channel_id=1, source_target_pairs={{0,16},{16,0},{1,17},{17,1},{2,18},{18,2},{3,19},{19,3},{4,20},{20... | collective-permute-start | bytes 786440 | tf_op jit(solution)/shard_map/ppermute | solution.py:208
  6.3 1.5 %collective-permute-start = (bf16[256,512]{1,0:T(8,128)(2,1)S(1)}, bf16[256,512]{1,0:T(8,128)(2,1)S(1)}, u32[]{:S(2)}, u32[]{:S(2)}) collective-permute-start(bf16[256,512]{1,0:T(8,128)(2,1)S(1)} %get-tuple-element.41.refs_4_), channel_id=1, source_target_pairs={{0,2},{1,3},{2,0},{3,1},{4,6},{5,7},{6,4},{7,5},{8,10},{9,11},{10,... | collective-permute-start | bytes 786440 | tf_op jit(solution)/shard_map/ppermute | solution.py:209
  7.8 0.5 collective-permute-start.9
  8.3 4.3 %collective-permute-done.1.refs_0_.refs_1_.refs_13_.refs_4_ = bf16[128,1024]{1,0:T(8,128)(2,1)S(1)} collective-permute-done((bf16[128,1024]{1,0:T(8,128)(2,1)S(1)}, bf16[128,1024]{1,0:T(8,128)(2,1)S(1)}, u32[]{:S(2)}, u32[]{:S(2)}) %collective-permute-start.1) | collective-permute-done | bytes 262176 | tf_op jit(solution)/shard_map/ppermute | solution.py:208
  12.6 0.2 shard_map.77
  12.8 2.7 %collective-permute-done.refs_6_ = bf16[256,512]{1,0:T(8,128)(2,1)S(1)} collective-permute-done((bf16[256,512]{1,0:T(8,128)(2,1)S(1)}, bf16[256,512]{1,0:T(8,128)(2,1)S(1)}, u32[]{:S(2)}, u32[]{:S(2)}) %collective-permute-start) | collective-permute-done | bytes 262176 | tf_op jit(solution)/shard_map/ppermute | solution.py:209
  15.5 0.0 collective-permute-start.2
  15.5 0.5 collective-permute-start.7
  16.0 0.0 collective-permute-start.8
  16.0 3.6 %collective-permute-done.9.refs_10_ = bf16[256,512]{1,0:T(8,128)(2,1)S(1)} collective-permute-done((bf16[256,512]{1,0:T(8,128)(2,1)S(1)}, bf16[256,512]{1,0:T(8,128)(2,1)S(1)}, u32[]{:S(2)}, u32[]{:S(2)}) %collective-permute-start.9) | collective-permute-done | bytes 262176 | tf_op jit(solution)/shard_map/ppermute | solution.py:209
  19.6 0.0 collective-permute-done.2.refs_7_
  19.6 0.0 collective-permute-start.10
  19.6 0.4 collective-permute-start.11
  20.0 0.2 collective-permute-start.4
  20.2 0.0 collective-permute-done.7.refs_5_
  20.2 1.7 %collective-permute-start.5 = (bf16[224,256]{1,0:T(8,128)(2,1)S(1)}, bf16[224,256]{1,0:T(8,128)(2,1)S(1)}, u32[]{:S(2)}, u32[]{:S(2)}) collective-permute-start(bf16[224,256]{1,0:T(8,128)(2,1)S(1)} %get-tuple-element.49), channel_id=1, source_target_pairs={{0,2},{1,3},{2,0},{3,1},{4,6},{5,7},{6,4},{7,5},{8,10},{9,11},{10,... | collective-permute-start | bytes 344072 | tf_op jit(solution)/shard_map/ppermute | solution.py:209
  21.9 0.0 collective-permute-done.8.refs_9_
  22.0 0.0 collective-permute-start.6
  22.0 0.0 collective-permute-done.4.refs_1_
  22.0 1.6 %collective-permute-start.3 = (bf16[128,896]{1,0:T(8,128)(2,1)S(1)}, bf16[128,896]{1,0:T(8,128)(2,1)S(1)}, u32[]{:S(2)}, u32[]{:S(2)}) collective-permute-start(bf16[128,896]{1,0:T(8,128)(2,1)S(1)} %get-tuple-element.46), channel_id=1, source_target_pairs={{0,16},{16,0},{1,17},{17,1},{2,18},{18,2},{3,19},{19,3},{4,20},{20... | collective-permute-start | bytes 688136 | tf_op jit(solution)/shard_map/ppermute | solution.py:208
  23.5 2.6 %collective-permute-done.5.refs_2_ = bf16[224,256]{1,0:T(8,128)(2,1)S(1)} collective-permute-done((bf16[224,256]{1,0:T(8,128)(2,1)S(1)}, bf16[224,256]{1,0:T(8,128)(2,1)S(1)}, u32[]{:S(2)}, u32[]{:S(2)}) %collective-permute-start.5) | collective-permute-done | bytes 114720 | tf_op jit(solution)/shard_map/ppermute | solution.py:209
  26.2 1.2 %collective-permute-done.6.refs_3_ = bf16[224,256]{1,0:T(8,128)(2,1)S(1)} collective-permute-done((bf16[224,256]{1,0:T(8,128)(2,1)S(1)}, bf16[224,256]{1,0:T(8,128)(2,1)S(1)}, u32[]{:S(2)}, u32[]{:S(2)}) %collective-permute-start.6) | collective-permute-done | bytes 114720 | tf_op jit(solution)/shard_map/ppermute | solution.py:209
  27.4 0.6 collective-permute-done.11.refs_12_.refs_5_
  28.0 0.0 collective-permute-done.10.refs_11_
  28.1 0.6 shard_map.78
  28.7 1.6 %collective-permute-start.19 = (bf16[224,1024]{1,0:T(8,128)(2,1)S(1)}, bf16[224,1024]{1,0:T(8,128)(2,1)S(1)}, u32[]{:S(2)}, u32[]{:S(2)}) collective-permute-start(bf16[224,1024]{1,0:T(8,128)(2,1)S(1)} %get-tuple-element.56.refs_3_), channel_id=1, source_target_pairs={{0,4},{1,5},{2,6},{3,7},{4,0},{5,1},{6,2},{7,3},{8,12},{9,13},{10,... | collective-permute-start | bytes 1376264 | tf_op jit(solution)/shard_map/ppermute | solution.py:209
  30.3 0.0 collective-permute-start.16
  30.4 1.5 %collective-permute-start.17 = (bf16[224,256]{1,0:T(8,128)(2,1)S(1)}, bf16[224,256]{1,0:T(8,128)(2,1)S(1)}, u32[]{:S(2)}, u32[]{:S(2)}) collective-permute-start(bf16[224,256]{1,0:T(8,128)(2,1)S(1)} %get-tuple-element.66), channel_id=1, source_target_pairs={{0,2},{1,3},{2,0},{3,1},{4,6},{5,7},{6,4},{7,5},{8,10},{9,11},{10,... | collective-permute-start | bytes 344072 | tf_op jit(solution)/shard_map/ppermute | solution.py:209
  31.9 0.3 collective-permute-start.18
  32.2 0.4 collective-permute-done.3.refs_0_.refs_6_
  32.6 0.2 shard_map.79
  32.8 0.8 %collective-permute-start.15 = (bf16[128,896]{1,0:T(8,128)(2,1)S(1)}, bf16[128,896]{1,0:T(8,128)(2,1)S(1)}, u32[]{:S(2)}, u32[]{:S(2)}) collective-permute-start(bf16[128,896]{1,0:T(8,128)(2,1)S(1)} %get-tuple-element.62), channel_id=1, source_target_pairs={{0,16},{16,0},{1,17},{17,1},{2,18},{18,2},{3,19},{19,3},{4,20},{20... | collective-permute-start | bytes 688136 | tf_op jit(solution)/shard_map/ppermute | solution.py:208
  33.7 0.0 collective-permute-done.16.refs_1_
  33.7 0.3 collective-permute-start.12
  34.0 2.3 %collective-permute-done.17.refs_2_ = bf16[224,256]{1,0:T(8,128)(2,1)S(1)} collective-permute-done((bf16[224,256]{1,0:T(8,128)(2,1)S(1)}, bf16[224,256]{1,0:T(8,128)(2,1)S(1)}, u32[]{:S(2)}, u32[]{:S(2)}) %collective-permute-start.17) | collective-permute-done | bytes 114720 | tf_op jit(solution)/shard_map/ppermute | solution.py:209
  36.3 1.5 %collective-permute-start.13 = (bf16[224,256]{1,0:T(8,128)(2,1)S(1)}, bf16[224,256]{1,0:T(8,128)(2,1)S(1)}, u32[]{:S(2)}, u32[]{:S(2)}) collective-permute-start(bf16[224,256]{1,0:T(8,128)(2,1)S(1)} %get-tuple-element.59), channel_id=1, source_target_pairs={{0,2},{1,3},{2,0},{3,1},{4,6},{5,7},{6,4},{7,5},{8,10},{9,11},{10,... | collective-permute-start | bytes 344072 | tf_op jit(solution)/shard_map/ppermute | solution.py:209
  37.8 0.2 collective-permute-done.18.refs_3_
  38.0 1.7 %collective-permute-start.14 = (bf16[224,256]{1,0:T(8,128)(2,1)S(1)}, bf16[224,256]{1,0:T(8,128)(2,1)S(1)}, u32[]{:S(2)}, u32[]{:S(2)}) collective-permute-start(bf16[224,256]{1,0:T(8,128)(2,1)S(1)} %get-tuple-element.60), channel_id=1, source_target_pairs={{0,3},{1,2},{2,1},{3,0},{4,7},{5,6},{6,5},{7,4},{8,11},{9,10},{10,... | collective-permute-start | bytes 344072 | tf_op jit(solution)/shard_map/ppermute | solution.py:209
  39.7 1.6 %collective-permute-done.19.refs_12_ = bf16[224,1024]{1,0:T(8,128)(2,1)S(1)} collective-permute-done((bf16[224,1024]{1,0:T(8,128)(2,1)S(1)}, bf16[224,1024]{1,0:T(8,128)(2,1)S(1)}, u32[]{:S(2)}, u32[]{:S(2)}) %collective-permute-start.19) | collective-permute-done | bytes 458784 | tf_op jit(solution)/shard_map/ppermute | solution.py:209
  41.3 0.6 shard_map.80.refs_15_
  42.0 2.8 %collective-permute-start.24 = (bf16[224,1024]{1,0:T(8,128)(2,1)S(1)}, bf16[224,1024]{1,0:T(8,128)(2,1)S(1)}, u32[]{:S(2)}, u32[]{:S(2)}) collective-permute-start(bf16[224,1024]{1,0:T(8,128)(2,1)S(1)} %shard_map.80.refs_15_), channel_id=1, source_target_pairs={{0,8},{1,9},{2,10},{3,11},{4,12},{5,13},{6,14},{7,15},{8,0},{9,1},... | collective-permute-start | bytes 1376264 | tf_op jit(solution)/shard_map/ppermute | solution.py:209
  44.8 0.0 collective-permute-done.12.refs_1_
  44.8 0.0 collective-permute-done.13.refs_2_
  44.8 0.0 collective-permute-done.14.refs_3_
  44.8 0.0 collective-permute-done.15.refs_12_.refs_7_
  44.8 0.7 shard_map.81
  45.5 0.0 copy-start
  45.5 1.6 %collective-permute-start.23 = (bf16[224,1024]{1,0:T(8,128)(2,1)S(1)}, bf16[224,1024]{1,0:T(8,128)(2,1)S(1)}, u32[]{:S(2)}, u32[]{:S(2)}) collective-permute-start(bf16[224,1024]{1,0:T(8,128)(2,1)S(1)} %get-tuple-element.74), channel_id=1, source_target_pairs={{0,4},{1,5},{2,6},{3,7},{4,0},{5,1},{6,2},{7,3},{8,12},{9,13},{10,... | collective-permute-start | bytes 1376264 | tf_op jit(solution)/shard_map/ppermute | solution.py:209
  47.1 0.0 collective-permute-start.20
  47.1 1.5 %collective-permute-start.21 = (bf16[224,256]{1,0:T(8,128)(2,1)S(1)}, bf16[224,256]{1,0:T(8,128)(2,1)S(1)}, u32[]{:S(2)}, u32[]{:S(2)}) collective-permute-start(bf16[224,256]{1,0:T(8,128)(2,1)S(1)} %get-tuple-element.70), channel_id=1, source_target_pairs={{0,2},{1,3},{2,0},{3,1},{4,6},{5,7},{6,4},{7,5},{8,10},{9,11},{10,... | collective-permute-start | bytes 344072 | tf_op jit(solution)/shard_map/ppermute | solution.py:209
  48.6 0.3 collective-permute-start.22
  49.0 7.9 %shard_map.82 = (bf16[256,2048]{1,0:T(8,128)(2,1)}, f32[8,128]{1,0:T(8,128)S(1)}, f32[8,128]{1,0:T(8,128)S(1)}) custom-call(f32[128,128]{1,0:T(8,128)S(1)} %get-tuple-element.72.refs_0_, bf16[128,3584]{1,0:T(8,128)(2,1)} %refs_1_.1, bf16[256,2048]{1,0:T(8,128)(2,1)} %bitcast.11, bf16[1024,3584]{1,0:T(8,128)(2,1)} %bitcast.9, ...), custom_call_target="tpu_custom_call" | custom-call | tf_op jit(solution)/shard_map/pallas_call | solution.py:44
  56.9 0.0 collective-permute-done.20.refs_1_
  56.9 1.6 %collective-permute-start.25 = (f32[8,128]{1,0:T(8,128)S(1)}, f32[8,128]{1,0:T(8,128)S(1)}, u32[]{:S(2)}, u32[]{:S(2)}) collective-permute-start(f32[8,128]{1,0:T(8,128)S(1)} %get-tuple-element.76), channel_id=1, source_target_pairs={{0,16},{16,0},{1,17},{17,1},{2,18},{18,2},{3,19},{19,3},{4,20},{20... | collective-permute-start | bytes 12296 | tf_op jit(solution)/shard_map/ppermute | solution.py:208
  58.5 0.0 collective-permute-done.21.refs_2_
  58.5 0.0 collective-permute-done.22.refs_3_
  58.5 0.6 shard_map.83.refs_0_
  59.1 1.5 %collective-permute-done.25.refs_2_ = f32[8,128]{1,0:T(8,128)S(1)} collective-permute-done((f32[8,128]{1,0:T(8,128)S(1)}, f32[8,128]{1,0:T(8,128)S(1)}, u32[]{:S(2)}, u32[]{:S(2)}) %collective-permute-start.25) | collective-permute-done | bytes 4128 | tf_op jit(solution)/shard_map/ppermute | solution.py:208
  60.6 4.3 %collective-permute-done.24.refs_2_.refs_3_ = bf16[224,1024]{1,0:T(8,128)(2,1)S(1)} collective-permute-done((bf16[224,1024]{1,0:T(8,128)(2,1)S(1)}, bf16[224,1024]{1,0:T(8,128)(2,1)S(1)}, u32[]{:S(2)}, u32[]{:S(2)}) %collective-permute-start.24) | collective-permute-done | bytes 458784 | tf_op jit(solution)/shard_map/ppermute | solution.py:209
  64.9 0.0 copy-done
  64.9 0.6 shard_map.85
  65.4 0.4 collective-permute-done.23.refs_1_
  65.8 1.1 %shard_map.84 = f32[224,1024]{1,0:T(8,128)} custom-call(f32[224,1024]{1,0:T(8,128)S(1)} %shard_map.83.refs_0_, bf16[224,1024]{1,0:T(8,128)(2,1)S(1)} %collective-permute-done.23.refs_1_, bf16[224,1024]{1,0:T(8,128)(2,1)S(1)} %collective-permute-done.24.refs_2_.refs_3_), custom_call_target="tpu_custom_call" | custom-call | tf_op jit(solution)/shard_map/pallas_call | solution.py:44
Async XLA Ops:
  3.3 9.3 %collective-permute-start.1 = (bf16[128,1024]{1,0:T(8,128)(2,1)S(1)}, bf16[128,1024]{1,0:T(8,128)(2,1)S(1)}, u32[]{:S(2)}, u32[]{:S(2)}) collective-permute-start(bf16[128,1024]{1,0:T(8,128)(2,1)S(1)} %get-tuple-element.42), channel_id=1, source_target_pairs={{0,16},{16,0},{1,17},{17,1},{2,18},{18,2},{3,19},{19,3},{4,20},{20... | collective-permute-start | bytes 786440 | tf_op jit(solution)/shard_map/ppermute | solution.py:208
  6.3 9.2 %collective-permute-start = (bf16[256,512]{1,0:T(8,128)(2,1)S(1)}, bf16[256,512]{1,0:T(8,128)(2,1)S(1)}, u32[]{:S(2)}, u32[]{:S(2)}) collective-permute-start(bf16[256,512]{1,0:T(8,128)(2,1)S(1)} %get-tuple-element.41.refs_4_), channel_id=1, source_target_pairs={{0,2},{1,3},{2,0},{3,1},{4,6},{5,7},{6,4},{7,5},{8,10},{9,11},{10,... | collective-permute-start | bytes 786440 | tf_op jit(solution)/shard_map/ppermute | solution.py:209
  7.8 11.9 %collective-permute-start.9 = (bf16[256,512]{1,0:T(8,128)(2,1)S(1)}, bf16[256,512]{1,0:T(8,128)(2,1)S(1)}, u32[]{:S(2)}, u32[]{:S(2)}) collective-permute-start(bf16[256,512]{1,0:T(8,128)(2,1)S(1)} %get-tuple-element.51.refs_8_), channel_id=1, source_target_pairs={{0,2},{1,3},{2,0},{3,1},{4,6},{5,7},{6,4},{7,5},{8,10},{9,11},{10,... | collective-permute-start | bytes 786440 | tf_op jit(solution)/shard_map/ppermute | solution.py:209
  15.5 4.2 %collective-permute-start.2 = (bf16[256,512]{1,0:T(8,128)(2,1)S(1)}, bf16[256,512]{1,0:T(8,128)(2,1)S(1)}, u32[]{:S(2)}, u32[]{:S(2)}) collective-permute-start(bf16[256,512]{1,0:T(8,128)(2,1)S(1)} %collective-permute-done.refs_6_), channel_id=1, source_target_pairs={{0,1},{1,0},{2,3},{3,2},{4,5},{5,4},{6,7},{7,6},{8,9},{9,8},{10,11... | collective-permute-start | bytes 786440 | tf_op jit(solution)/shard_map/ppermute | solution.py:209
  15.5 4.7 %collective-permute-start.7 = (bf16[256,512]{1,0:T(8,128)(2,1)S(1)}, bf16[256,512]{1,0:T(8,128)(2,1)S(1)}, u32[]{:S(2)}, u32[]{:S(2)}) collective-permute-start(bf16[256,512]{1,0:T(8,128)(2,1)S(1)} %get-tuple-element.41.refs_4_), channel_id=1, source_target_pairs={{0,1},{1,0},{2,3},{3,2},{4,5},{5,4},{6,7},{7,6},{8,9},{9,8},{10,11... | collective-permute-start | bytes 786440 | tf_op jit(solution)/shard_map/ppermute | solution.py:209
  16.0 6.0 %collective-permute-start.8 = (bf16[256,512]{1,0:T(8,128)(2,1)S(1)}, bf16[256,512]{1,0:T(8,128)(2,1)S(1)}, u32[]{:S(2)}, u32[]{:S(2)}) collective-permute-start(bf16[256,512]{1,0:T(8,128)(2,1)S(1)} %get-tuple-element.51.refs_8_), channel_id=1, source_target_pairs={{0,1},{1,0},{2,3},{3,2},{4,5},{5,4},{6,7},{7,6},{8,9},{9,8},{10,11... | collective-permute-start | bytes 786440 | tf_op jit(solution)/shard_map/ppermute | solution.py:209
  19.6 8.4 %collective-permute-start.10 = (bf16[256,512]{1,0:T(8,128)(2,1)S(1)}, bf16[256,512]{1,0:T(8,128)(2,1)S(1)}, u32[]{:S(2)}, u32[]{:S(2)}) collective-permute-start(bf16[256,512]{1,0:T(8,128)(2,1)S(1)} %collective-permute-done.9.refs_10_), channel_id=1, source_target_pairs={{0,1},{1,0},{2,3},{3,2},{4,5},{5,4},{6,7},{7,6},{8,9},{9,8},{10,11... | collective-permute-start | bytes 786440 | tf_op jit(solution)/shard_map/ppermute | solution.py:209
  19.6 8.4 %collective-permute-start.11 = (bf16[128,896]{1,0:T(8,128)(2,1)S(1)}, bf16[128,896]{1,0:T(8,128)(2,1)S(1)}, u32[]{:S(2)}, u32[]{:S(2)}) collective-permute-start(bf16[128,896]{1,0:T(8,128)(2,1)S(1)} %get-tuple-element.54), channel_id=1, source_target_pairs={{0,16},{16,0},{1,17},{17,1},{2,18},{18,2},{3,19},{19,3},{4,20},{20... | collective-permute-start | bytes 688136 | tf_op jit(solution)/shard_map/ppermute | solution.py:208
  20.0 2.0 %collective-permute-start.4 = (bf16[224,256]{1,0:T(8,128)(2,1)S(1)}, bf16[224,256]{1,0:T(8,128)(2,1)S(1)}, u32[]{:S(2)}, u32[]{:S(2)}) collective-permute-start(bf16[224,256]{1,0:T(8,128)(2,1)S(1)} %get-tuple-element.48), channel_id=1, source_target_pairs={{0,1},{1,0},{2,3},{3,2},{4,5},{5,4},{6,7},{7,6},{8,9},{9,8},{10,11... | collective-permute-start | bytes 344072 | tf_op jit(solution)/shard_map/ppermute | solution.py:209
  20.2 5.9 %collective-permute-start.5 = (bf16[224,256]{1,0:T(8,128)(2,1)S(1)}, bf16[224,256]{1,0:T(8,128)(2,1)S(1)}, u32[]{:S(2)}, u32[]{:S(2)}) collective-permute-start(bf16[224,256]{1,0:T(8,128)(2,1)S(1)} %get-tuple-element.49), channel_id=1, source_target_pairs={{0,2},{1,3},{2,0},{3,1},{4,6},{5,7},{6,4},{7,5},{8,10},{9,11},{10,... | collective-permute-start | bytes 344072 | tf_op jit(solution)/shard_map/ppermute | solution.py:209
  22.0 5.5 %collective-permute-start.6 = (bf16[224,256]{1,0:T(8,128)(2,1)S(1)}, bf16[224,256]{1,0:T(8,128)(2,1)S(1)}, u32[]{:S(2)}, u32[]{:S(2)}) collective-permute-start(bf16[224,256]{1,0:T(8,128)(2,1)S(1)} %get-tuple-element.50), channel_id=1, source_target_pairs={{0,3},{1,2},{2,1},{3,0},{4,7},{5,6},{6,5},{7,4},{8,11},{9,10},{10,... | collective-permute-start | bytes 344072 | tf_op jit(solution)/shard_map/ppermute | solution.py:209
  22.0 10.6 %collective-permute-start.3 = (bf16[128,896]{1,0:T(8,128)(2,1)S(1)}, bf16[128,896]{1,0:T(8,128)(2,1)S(1)}, u32[]{:S(2)}, u32[]{:S(2)}) collective-permute-start(bf16[128,896]{1,0:T(8,128)(2,1)S(1)} %get-tuple-element.46), channel_id=1, source_target_pairs={{0,16},{16,0},{1,17},{17,1},{2,18},{18,2},{3,19},{19,3},{4,20},{20... | collective-permute-start | bytes 688136 | tf_op jit(solution)/shard_map/ppermute | solution.py:208
  28.7 12.6 %collective-permute-start.19 = (bf16[224,1024]{1,0:T(8,128)(2,1)S(1)}, bf16[224,1024]{1,0:T(8,128)(2,1)S(1)}, u32[]{:S(2)}, u32[]{:S(2)}) collective-permute-start(bf16[224,1024]{1,0:T(8,128)(2,1)S(1)} %get-tuple-element.56.refs_3_), channel_id=1, source_target_pairs={{0,4},{1,5},{2,6},{3,7},{4,0},{5,1},{6,2},{7,3},{8,12},{9,13},{10,... | collective-permute-start | bytes 1376264 | tf_op jit(solution)/shard_map/ppermute | solution.py:209
  30.3 3.3 %collective-permute-start.16 = (bf16[224,256]{1,0:T(8,128)(2,1)S(1)}, bf16[224,256]{1,0:T(8,128)(2,1)S(1)}, u32[]{:S(2)}, u32[]{:S(2)}) collective-permute-start(bf16[224,256]{1,0:T(8,128)(2,1)S(1)} %get-tuple-element.65), channel_id=1, source_target_pairs={{0,1},{1,0},{2,3},{3,2},{4,5},{5,4},{6,7},{7,6},{8,9},{9,8},{10,11... | collective-permute-start | bytes 344072 | tf_op jit(solution)/shard_map/ppermute | solution.py:209
  30.4 5.9 %collective-permute-start.17 = (bf16[224,256]{1,0:T(8,128)(2,1)S(1)}, bf16[224,256]{1,0:T(8,128)(2,1)S(1)}, u32[]{:S(2)}, u32[]{:S(2)}) collective-permute-start(bf16[224,256]{1,0:T(8,128)(2,1)S(1)} %get-tuple-element.66), channel_id=1, source_target_pairs={{0,2},{1,3},{2,0},{3,1},{4,6},{5,7},{6,4},{7,5},{8,10},{9,11},{10,... | collective-permute-start | bytes 344072 | tf_op jit(solution)/shard_map/ppermute | solution.py:209
  31.9 6.1 %collective-permute-start.18 = (bf16[224,256]{1,0:T(8,128)(2,1)S(1)}, bf16[224,256]{1,0:T(8,128)(2,1)S(1)}, u32[]{:S(2)}, u32[]{:S(2)}) collective-permute-start(bf16[224,256]{1,0:T(8,128)(2,1)S(1)} %get-tuple-element.67), channel_id=1, source_target_pairs={{0,3},{1,2},{2,1},{3,0},{4,7},{5,6},{6,5},{7,4},{8,11},{9,10},{10,... | collective-permute-start | bytes 344072 | tf_op jit(solution)/shard_map/ppermute | solution.py:209
  32.8 12.0 %collective-permute-start.15 = (bf16[128,896]{1,0:T(8,128)(2,1)S(1)}, bf16[128,896]{1,0:T(8,128)(2,1)S(1)}, u32[]{:S(2)}, u32[]{:S(2)}) collective-permute-start(bf16[128,896]{1,0:T(8,128)(2,1)S(1)} %get-tuple-element.62), channel_id=1, source_target_pairs={{0,16},{16,0},{1,17},{17,1},{2,18},{18,2},{3,19},{19,3},{4,20},{20... | collective-permute-start | bytes 688136 | tf_op jit(solution)/shard_map/ppermute | solution.py:208
  33.7 11.1 %collective-permute-start.12 = (bf16[224,256]{1,0:T(8,128)(2,1)S(1)}, bf16[224,256]{1,0:T(8,128)(2,1)S(1)}, u32[]{:S(2)}, u32[]{:S(2)}) collective-permute-start(bf16[224,256]{1,0:T(8,128)(2,1)S(1)} %get-tuple-element.58), channel_id=1, source_target_pairs={{0,1},{1,0},{2,3},{3,2},{4,5},{5,4},{6,7},{7,6},{8,9},{9,8},{10,11... | collective-permute-start | bytes 344072 | tf_op jit(solution)/shard_map/ppermute | solution.py:209
  36.3 8.5 %collective-permute-start.13 = (bf16[224,256]{1,0:T(8,128)(2,1)S(1)}, bf16[224,256]{1,0:T(8,128)(2,1)S(1)}, u32[]{:S(2)}, u32[]{:S(2)}) collective-permute-start(bf16[224,256]{1,0:T(8,128)(2,1)S(1)} %get-tuple-element.59), channel_id=1, source_target_pairs={{0,2},{1,3},{2,0},{3,1},{4,6},{5,7},{6,4},{7,5},{8,10},{9,11},{10,... | collective-permute-start | bytes 344072 | tf_op jit(solution)/shard_map/ppermute | solution.py:209
  38.0 6.8 %collective-permute-start.14 = (bf16[224,256]{1,0:T(8,128)(2,1)S(1)}, bf16[224,256]{1,0:T(8,128)(2,1)S(1)}, u32[]{:S(2)}, u32[]{:S(2)}) collective-permute-start(bf16[224,256]{1,0:T(8,128)(2,1)S(1)} %get-tuple-element.60), channel_id=1, source_target_pairs={{0,3},{1,2},{2,1},{3,0},{4,7},{5,6},{6,5},{7,4},{8,11},{9,10},{10,... | collective-permute-start | bytes 344072 | tf_op jit(solution)/shard_map/ppermute | solution.py:209
  42.0 22.9 %collective-permute-start.24 = (bf16[224,1024]{1,0:T(8,128)(2,1)S(1)}, bf16[224,1024]{1,0:T(8,128)(2,1)S(1)}, u32[]{:S(2)}, u32[]{:S(2)}) collective-permute-start(bf16[224,1024]{1,0:T(8,128)(2,1)S(1)} %shard_map.80.refs_15_), channel_id=1, source_target_pairs={{0,8},{1,9},{2,10},{3,11},{4,12},{5,13},{6,14},{7,15},{8,0},{9,1},... | collective-permute-start | bytes 1376264 | tf_op jit(solution)/shard_map/ppermute | solution.py:209
  45.5 19.4 %copy-start = (s32[128,2]{0,1:T(2,128)S(1)}, s32[128,2]{0,1:T(2,128)}, u32[]{:S(2)}) copy-start(s32[128,2]{0,1:T(2,128)} %param.7) | copy-start | bytes 3076
  45.5 20.3 %collective-permute-start.23 = (bf16[224,1024]{1,0:T(8,128)(2,1)S(1)}, bf16[224,1024]{1,0:T(8,128)(2,1)S(1)}, u32[]{:S(2)}, u32[]{:S(2)}) collective-permute-start(bf16[224,1024]{1,0:T(8,128)(2,1)S(1)} %get-tuple-element.74), channel_id=1, source_target_pairs={{0,4},{1,5},{2,6},{3,7},{4,0},{5,1},{6,2},{7,3},{8,12},{9,13},{10,... | collective-permute-start | bytes 1376264 | tf_op jit(solution)/shard_map/ppermute | solution.py:209
  47.1 9.8 %collective-permute-start.20 = (bf16[224,256]{1,0:T(8,128)(2,1)S(1)}, bf16[224,256]{1,0:T(8,128)(2,1)S(1)}, u32[]{:S(2)}, u32[]{:S(2)}) collective-permute-start(bf16[224,256]{1,0:T(8,128)(2,1)S(1)} %get-tuple-element.69), channel_id=1, source_target_pairs={{0,1},{1,0},{2,3},{3,2},{4,5},{5,4},{6,7},{7,6},{8,9},{9,8},{10,11... | collective-permute-start | bytes 344072 | tf_op jit(solution)/shard_map/ppermute | solution.py:209
  47.1 11.4 %collective-permute-start.21 = (bf16[224,256]{1,0:T(8,128)(2,1)S(1)}, bf16[224,256]{1,0:T(8,128)(2,1)S(1)}, u32[]{:S(2)}, u32[]{:S(2)}) collective-permute-start(bf16[224,256]{1,0:T(8,128)(2,1)S(1)} %get-tuple-element.70), channel_id=1, source_target_pairs={{0,2},{1,3},{2,0},{3,1},{4,6},{5,7},{6,4},{7,5},{8,10},{9,11},{10,... | collective-permute-start | bytes 344072 | tf_op jit(solution)/shard_map/ppermute | solution.py:209
  48.6 9.8 %collective-permute-start.22 = (bf16[224,256]{1,0:T(8,128)(2,1)S(1)}, bf16[224,256]{1,0:T(8,128)(2,1)S(1)}, u32[]{:S(2)}, u32[]{:S(2)}) collective-permute-start(bf16[224,256]{1,0:T(8,128)(2,1)S(1)} %get-tuple-element.71), channel_id=1, source_target_pairs={{0,3},{1,2},{2,1},{3,0},{4,7},{5,6},{6,5},{7,4},{8,11},{9,10},{10,... | collective-permute-start | bytes 344072 | tf_op jit(solution)/shard_map/ppermute | solution.py:209
  56.9 3.7 %collective-permute-start.25 = (f32[8,128]{1,0:T(8,128)S(1)}, f32[8,128]{1,0:T(8,128)S(1)}, u32[]{:S(2)}, u32[]{:S(2)}) collective-permute-start(f32[8,128]{1,0:T(8,128)S(1)} %get-tuple-element.76), channel_id=1, source_target_pairs={{0,16},{16,0},{1,17},{17,1},{2,18},{18,2},{3,19},{19,3},{4,20},{20... | collective-permute-start | bytes 12296 | tf_op jit(solution)/shard_map/ppermute | solution.py:208

commit v4 on v3

--- a/solution.py
+++ b/solution.py
@@ -56,46 +56,55 @@
     return pl.multiple_of((group ^ k) * chunk, LANES)
 
 
-def prepare_kernel(pairs, chunk, up_hbm, hidden_hbm, ids_ref, weights_ref, *refs):
-    send_refs, column_ref, act_refs = refs[: len(pairs)], refs[len(pairs)], refs[len(pairs) + 1 : len(pairs) + 3]
-    own_refs = refs[len(pairs) + 3 : -3]
-    up_ref, hidden_ref, sems = refs[-3:]
-    order = [k for pair in pairs for k in pair]
-    outer = len(order)
-    loads = {}
-    for k in order:
+def token_weight(ids_ref, weights_ref, expert):
+    picked = jnp.where(ids_ref[...] == expert, weights_ref[...].astype(jnp.float32), 0.0)
+    lanes = jnp.sum(picked, axis=0, keepdims=True)
+    return jnp.broadcast_to(lanes, (LANES, lanes.shape[1])).T
+
+
+def first_kernel(k, chunk, up_hbm, hidden_hbm, ids_ref, weights_ref, send_ref, act0_ref, act1_ref, hidden_ref, sems):
+    cols = pl.ds(chunk_start(k, chunk), chunk)
+    rows = pltpu.make_async_copy(up_hbm.at[:, cols], send_ref.at[:, pl.ds(0, chunk)], sems.at[0])
+    half, hidden_units = hidden_ref.shape[0] // 2, hidden_ref.shape[1] // 2
+    loads = []
+    for part in range(2):
+        span = pl.ds(part * half, half)
+        loads.append(pltpu.make_async_copy(hidden_hbm.at[span], hidden_ref.at[span], sems.at[1 + part]))
+    for load in loads:
+        load.start()
+    rows.start()
+    expert = lax.axis_index("expert")
+    send_ref[:, chunk:] = token_weight(ids_ref, weights_ref, 1 - expert).astype(jnp.bfloat16)
+    for part in range(2):
+        loads[part].wait()
+        target = pl.ds(pl.multiple_of((expert ^ part) * half, half), half)
+        gate = hidden_ref[part * half : (part + 1) * half, :hidden_units].astype(jnp.float32)
+        up = hidden_ref[part * half : (part + 1) * half, hidden_units:].astype(jnp.float32)
+        act = (gate * jax.nn.sigmoid(gate) * up).astype(jnp.bfloat16)
+        for i, act_ref in enumerate((act0_ref, act1_ref)):
+            width = act_ref.shape[1]
+            act_ref[target, :] = act[:, i * width : (i + 1) * width]
+    rows.wait()
+
+
+def own_kernel(order, chunk, up_hbm, ids_ref, weights_ref, *refs):
+    column_ref, refs = refs[0], refs[1:]
+    own_refs, send_refs = refs[: len(order)], refs[len(order) : -2]
+    up_ref, sems = refs[-2:]
+    loads = []
+    for i, k in enumerate(order):
         cols = pl.ds(chunk_start(k, chunk), chunk)
-        loads[k] = pltpu.make_async_copy(up_hbm.at[:, cols], up_ref.at[k], sems.at[k])
-        loads[k].start()
-    stored = pltpu.make_async_copy(hidden_hbm, hidden_ref, sems.at[outer])
-    stored.start()
-    expert = lax.axis_index("expert")
-
-    def token_weight(of):
-        picked = jnp.where(ids_ref[...] == of, weights_ref[...].astype(jnp.float32), 0.0)
-        lanes = jnp.sum(picked, axis=0, keepdims=True)
-        return jnp.broadcast_to(lanes, (LANES, lanes.shape[1])).T
-
-    weight = token_weight(expert)
+        loads.append(pltpu.make_async_copy(up_hbm.at[:, cols], up_ref.at[i], sems.at[i]))
+        loads[i].start()
+    weight = token_weight(ids_ref, weights_ref, lax.axis_index("expert"))
     column_ref[...] = weight
     weight = weight[:, :1]
-    send_refs[0][:, len(pairs[0]) * chunk :] = token_weight(1 - expert).astype(jnp.bfloat16)
-    for send_ref, pair in zip(send_refs, pairs):
-        for i, k in enumerate(pair):
-            loads[k].wait()
-            rows = up_ref[k]
-            send_ref[:, i * chunk : (i + 1) * chunk] = rows
-            own_refs[order.index(k)][...] = (weight * rows.astype(jnp.float32)).astype(jnp.bfloat16).T
-    stored.wait()
-    half, hidden_units = hidden_ref.shape[0] // 2, hidden_ref.shape[1] // 2
-    for part in range(2):
-        source = pl.ds(pl.multiple_of((expert ^ part) * half, half), half)
-        gate = hidden_ref[source, :hidden_units].astype(jnp.float32)
-        up = hidden_ref[source, hidden_units:].astype(jnp.float32)
-        act = (gate * jax.nn.sigmoid(gate) * up).astype(jnp.bfloat16)
-        for i, act_ref in enumerate(act_refs):
-            width = act_ref.shape[1]
-            act_ref[part * half : (part + 1) * half, :] = act[:, i * width : (i + 1) * width]
+    for i in range(len(order)):
+        loads[i].wait()
+        rows = up_ref[i]
+        if i:
+            send_refs[i - 1][...] = rows
+        own_refs[i][...] = (weight * rows.astype(jnp.float32)).astype(jnp.bfloat16).T
 
 
 def split_kernel(chunk, got_ref, first_ref, *refs):
@@ -212,21 +221,22 @@
     pairs = ((3,), (2,), (1,), (0,))
     sides = (hidden_units,)
 
-    prepared = call((
-        functools.partial(prepare_kernel, pairs, chunk),
+    order = tuple(pair[0] for pair in pairs)
+    first, *mine = call((
+        functools.partial(first_kernel, order[0], chunk),
         [upstream, stored, ids, combine],
-        [((tokens, chunk + LANES), bf16)] + [((tokens, chunk), bf16)] * 3
-        + [((tokens, LANES), f32)] + [((rows, hidden_units // 2), bf16)] * 2
-        + [((chunk, tokens), bf16)] * outer,
-        [
-            pltpu.VMEM((outer, tokens, chunk), bf16),
-            pltpu.VMEM((rows, 2 * hidden_units), bf16),
-            pltpu.SemaphoreType.DMA((outer + 1,)),
-        ],
+        [((tokens, chunk + LANES), bf16)] + [((rows, hidden_units // 2), bf16)] * 2,
+        [pltpu.VMEM((rows, 2 * hidden_units), bf16), pltpu.SemaphoreType.DMA((3,))],
         [HBM, HBM, LOAD, LOAD],
     ))
-    send, column = prepared[:outer], prepared[outer]
-    mine, own = prepared[outer + 1 : outer + 3], prepared[outer + 3 :]
+    column, *own = call((
+        functools.partial(own_kernel, order, chunk),
+        [upstream, ids, combine],
+        [((tokens, LANES), f32)] + [((chunk, tokens), bf16)] * outer + [((tokens, chunk), bf16)] * (outer - 1),
+        [pltpu.VMEM((outer, tokens, chunk), bf16), pltpu.SemaphoreType.DMA((outer,))],
+        [HBM, LOAD, LOAD],
+    ), waits=(first,))
+    send, own = [first] + own[outer:], own[:outer]
 
     def split_job(i):
         return (
@@ -260,7 +270,7 @@
     pays[1], marks[1] = spread(cut)
     got[2] = cross(after(send[2], acts[0][3]))
     pays[2], marks[2] = split(2, far)
-    wide, = call(parts(1, bf16, (hidden_units,), near), waits=(marks[2],))
+    wide, = call(parts(1, bf16, (hidden_units,), near))
     last = [swap(wide, 2 * INNER)]
     got[3] = cross(after(send[3], marks[2]))
     *side, _0, _1, _2, _3 = call(parts(2, bf16, sides), split_job(3), waits=(wide,))

time: 67.1 us -> 66.5 us (level)
  waiting for transfers between devices: 25.7 us -> 23.4 us
  Pallas kernels: 15.2 us -> 16.9 us
    ppermute x5, waiting for transfers between devices: 6.76 us -> 4.48 us  [both_experts(): cross = lambda value: lax.ppermute(value, 'expert', flip)]
    pallas_call x10 -> x11, Pallas kernels: 15.2 us -> 16.9 us  [call(): pl.pallas_call(body, out_shape=outs, in_specs=specs + [ANY] * len(waits),...]
  transfers between devices with their start and end apart: 26 -> 26, of which waited for: 13 -> 13; matrix products, arithmetic and copies ran while one was open for 0% -> 0% of each run, Pallas kernels for 17% -> 21%
where the time goes in v4:
time: 66.5 us; the launch traced here: 66.3 us
  starting transfers between devices  25.2 us (38%)
  waiting for transfers between devices  23.4 us (35%)
  Pallas kernels  16.9 us (25%)
  between operations  0.75 us (1%)
    ppermute x21, waiting for transfers between devices, both_experts(): lax.ppermute(value, 'dp', [(i, i ^ bit) for i in range(n)])  18.9 us
    ppermute x21, starting transfers between devices, both_experts(): lax.ppermute(value, 'dp', [(i, i ^ bit) for i in range(n)])  17.9 us
    pallas_call x11, Pallas kernels, call(): pl.pallas_call(body, out_shape=outs, in_specs=specs + [ANY] * len(waits),...  16.9 us
    ppermute x5, starting transfers between devices, both_experts(): cross = lambda value: lax.ppermute(value, 'expert', flip)  7.36 us
    ppermute x5, waiting for transfers between devices, both_experts(): cross = lambda value: lax.ppermute(value, 'expert', flip)  4.48 us
  transfers between devices with their start and end apart: 26, of which 13 were waited for; matrix products, arithmetic and copies ran while one was open for 0% of the time, Pallas kernels for 21%

profile of v4, /device:TPU:0, one launch (start us, length us, event | category | flops | bytes accessed | tf_op | source)
XLA Modules:
  0.0 66.3 jit_solution(8490946835564785519)
XLA Ops:
  0.6 2.0 %shard_map.76 = (bf16[128,1024]{1,0:T(8,128)(2,1)S(1)}, bf16[256,512]{1,0:T(8,128)(2,1)S(1)}, bf16[256,512]{1,0:T(8,128)(2,1)S(1)}) custom-call(bf16[128,3584]{1,0:T(8,128)(2,1)} %refs_1_.1, bf16[256,2048]{1,0:T(8,128)(2,1)} %bitcast.11, s32[2,128]{1,0:T(2,128)} %bitcast.7, bf16[2,128]{1,0:T(2,128)(2,1)} %bitcast.14), custom_call_target="tpu_custom_call" | custom-call | tf_op jit(solution)/shard_map/pallas_call | solution.py:44
  2.7 3.0 %collective-permute-start.1 = (bf16[128,1024]{1,0:T(8,128)(2,1)S(1)}, bf16[128,1024]{1,0:T(8,128)(2,1)S(1)}, u32[]{:S(2)}, u32[]{:S(2)}) collective-permute-start(bf16[128,1024]{1,0:T(8,128)(2,1)S(1)} %get-tuple-element.40.refs_3_), channel_id=1, source_target_pairs={{0,16},{16,0},{1,17},{17,1},{2,18},{18,2},{3,19},{19,3},{4,20},{20... | collective-permute-start | bytes 786440 | tf_op jit(solution)/shard_map/ppermute | solution.py:217
  5.7 1.5 %collective-permute-start = (bf16[256,512]{1,0:T(8,128)(2,1)S(1)}, bf16[256,512]{1,0:T(8,128)(2,1)S(1)}, u32[]{:S(2)}, u32[]{:S(2)}) collective-permute-start(bf16[256,512]{1,0:T(8,128)(2,1)S(1)} %get-tuple-element.42.refs_4_), channel_id=1, source_target_pairs={{0,2},{1,3},{2,0},{3,1},{4,6},{5,7},{6,4},{7,5},{8,10},{9,11},{10,... | collective-permute-start | bytes 786440 | tf_op jit(solution)/shard_map/ppermute | solution.py:218
  7.2 0.5 collective-permute-start.9
  7.7 2.3 %shard_map.77 = (f32[128,128]{1,0:T(8,128)S(1)}, bf16[896,128]{1,0:T(8,128)(2,1)S(1)}, bf16[896,128]{1,0:T(8,128)(2,1)S(1)}, bf16[896,128]{1,0:T(8,128)(2,1)S(1)...) custom-call(bf16[128,3584]{1,0:T(8,128)(2,1)} %refs_1_.1, ...), custom_call_target="tpu_custom_call" | custom-call | tf_op jit(solution)/shard_map/pallas_call | solution.py:44
  10.0 2.0 %collective-permute-done.1.refs_0_.refs_1_.refs_13_.refs_4_ = bf16[128,1024]{1,0:T(8,128)(2,1)S(1)} collective-permute-done((bf16[128,1024]{1,0:T(8,128)(2,1)S(1)}, bf16[128,1024]{1,0:T(8,128)(2,1)S(1)}, u32[]{:S(2)}, u32[]{:S(2)}) %collective-permute-start.1) | collective-permute-done | bytes 262176 | tf_op jit(solution)/shard_map/ppermute | solution.py:217
  12.0 0.2 shard_map.78
  12.2 2.7 %collective-permute-done.refs_6_ = bf16[256,512]{1,0:T(8,128)(2,1)S(1)} collective-permute-done((bf16[256,512]{1,0:T(8,128)(2,1)S(1)}, bf16[256,512]{1,0:T(8,128)(2,1)S(1)}, u32[]{:S(2)}, u32[]{:S(2)}) %collective-permute-start) | collective-permute-done | bytes 262176 | tf_op jit(solution)/shard_map/ppermute | solution.py:218
  14.9 0.0 collective-permute-start.2
  14.9 0.5 collective-permute-start.7
  15.4 0.0 collective-permute-start.8
  15.4 3.6 %collective-permute-done.9.refs_10_ = bf16[256,512]{1,0:T(8,128)(2,1)S(1)} collective-permute-done((bf16[256,512]{1,0:T(8,128)(2,1)S(1)}, bf16[256,512]{1,0:T(8,128)(2,1)S(1)}, u32[]{:S(2)}, u32[]{:S(2)}) %collective-permute-start.9) | collective-permute-done | bytes 262176 | tf_op jit(solution)/shard_map/ppermute | solution.py:218
  19.1 0.0 collective-permute-done.2.refs_7_
  19.1 0.0 collective-permute-start.10
  19.1 0.4 collective-permute-start.11
  19.4 0.2 collective-permute-start.4
  19.6 0.0 collective-permute-done.7.refs_5_
  19.6 1.7 %collective-permute-start.5 = (bf16[224,256]{1,0:T(8,128)(2,1)S(1)}, bf16[224,256]{1,0:T(8,128)(2,1)S(1)}, u32[]{:S(2)}, u32[]{:S(2)}) collective-permute-start(bf16[224,256]{1,0:T(8,128)(2,1)S(1)} %get-tuple-element.49), channel_id=1, source_target_pairs={{0,2},{1,3},{2,0},{3,1},{4,6},{5,7},{6,4},{7,5},{8,10},{9,11},{10,... | collective-permute-start | bytes 344072 | tf_op jit(solution)/shard_map/ppermute | solution.py:218
  21.4 0.0 collective-permute-done.8.refs_9_
  21.4 0.0 collective-permute-start.6
  21.4 0.0 collective-permute-done.4.refs_1_
  21.4 1.6 %collective-permute-start.3 = (bf16[128,896]{1,0:T(8,128)(2,1)S(1)}, bf16[128,896]{1,0:T(8,128)(2,1)S(1)}, u32[]{:S(2)}, u32[]{:S(2)}) collective-permute-start(bf16[128,896]{1,0:T(8,128)(2,1)S(1)} %get-tuple-element.46), channel_id=1, source_target_pairs={{0,16},{16,0},{1,17},{17,1},{2,18},{18,2},{3,19},{19,3},{4,20},{20... | collective-permute-start | bytes 688136 | tf_op jit(solution)/shard_map/ppermute | solution.py:217
  23.0 2.6 %collective-permute-done.5.refs_2_ = bf16[224,256]{1,0:T(8,128)(2,1)S(1)} collective-permute-done((bf16[224,256]{1,0:T(8,128)(2,1)S(1)}, bf16[224,256]{1,0:T(8,128)(2,1)S(1)}, u32[]{:S(2)}, u32[]{:S(2)}) %collective-permute-start.5) | collective-permute-done | bytes 114720 | tf_op jit(solution)/shard_map/ppermute | solution.py:218
  25.6 1.2 %collective-permute-done.6.refs_3_ = bf16[224,256]{1,0:T(8,128)(2,1)S(1)} collective-permute-done((bf16[224,256]{1,0:T(8,128)(2,1)S(1)}, bf16[224,256]{1,0:T(8,128)(2,1)S(1)}, u32[]{:S(2)}, u32[]{:S(2)}) %collective-permute-start.6) | collective-permute-done | bytes 114720 | tf_op jit(solution)/shard_map/ppermute | solution.py:218
  26.8 0.6 collective-permute-done.11.refs_12_.refs_5_
  27.5 0.0 collective-permute-done.10.refs_11_
  27.5 0.6 shard_map.79
  28.1 1.6 %collective-permute-start.19 = (bf16[224,1024]{1,0:T(8,128)(2,1)S(1)}, bf16[224,1024]{1,0:T(8,128)(2,1)S(1)}, u32[]{:S(2)}, u32[]{:S(2)}) collective-permute-start(bf16[224,1024]{1,0:T(8,128)(2,1)S(1)} %get-tuple-element.56.refs_3_), channel_id=1, source_target_pairs={{0,4},{1,5},{2,6},{3,7},{4,0},{5,1},{6,2},{7,3},{8,12},{9,13},{10,... | collective-permute-start | bytes 1376264 | tf_op jit(solution)/shard_map/ppermute | solution.py:218
  29.8 0.0 collective-permute-start.16
  29.8 1.5 %collective-permute-start.17 = (bf16[224,256]{1,0:T(8,128)(2,1)S(1)}, bf16[224,256]{1,0:T(8,128)(2,1)S(1)}, u32[]{:S(2)}, u32[]{:S(2)}) collective-permute-start(bf16[224,256]{1,0:T(8,128)(2,1)S(1)} %get-tuple-element.66), channel_id=1, source_target_pairs={{0,2},{1,3},{2,0},{3,1},{4,6},{5,7},{6,4},{7,5},{8,10},{9,11},{10,... | collective-permute-start | bytes 344072 | tf_op jit(solution)/shard_map/ppermute | solution.py:218
  31.3 0.3 collective-permute-start.18
  31.6 0.4 collective-permute-done.3.refs_0_.refs_6_
  32.0 0.2 shard_map.80
  32.2 0.8 %collective-permute-start.15 = (bf16[128,896]{1,0:T(8,128)(2,1)S(1)}, bf16[128,896]{1,0:T(8,128)(2,1)S(1)}, u32[]{:S(2)}, u32[]{:S(2)}) collective-permute-start(bf16[128,896]{1,0:T(8,128)(2,1)S(1)} %get-tuple-element.62), channel_id=1, source_target_pairs={{0,16},{16,0},{1,17},{17,1},{2,18},{18,2},{3,19},{19,3},{4,20},{20... | collective-permute-start | bytes 688136 | tf_op jit(solution)/shard_map/ppermute | solution.py:217
  33.1 0.0 collective-permute-done.16.refs_1_
  33.1 0.3 collective-permute-start.12
  33.4 2.3 %collective-permute-done.17.refs_2_ = bf16[224,256]{1,0:T(8,128)(2,1)S(1)} collective-permute-done((bf16[224,256]{1,0:T(8,128)(2,1)S(1)}, bf16[224,256]{1,0:T(8,128)(2,1)S(1)}, u32[]{:S(2)}, u32[]{:S(2)}) %collective-permute-start.17) | collective-permute-done | bytes 114720 | tf_op jit(solution)/shard_map/ppermute | solution.py:218
  35.7 1.5 %collective-permute-start.13 = (bf16[224,256]{1,0:T(8,128)(2,1)S(1)}, bf16[224,256]{1,0:T(8,128)(2,1)S(1)}, u32[]{:S(2)}, u32[]{:S(2)}) collective-permute-start(bf16[224,256]{1,0:T(8,128)(2,1)S(1)} %get-tuple-element.59), channel_id=1, source_target_pairs={{0,2},{1,3},{2,0},{3,1},{4,6},{5,7},{6,4},{7,5},{8,10},{9,11},{10,... | collective-permute-start | bytes 344072 | tf_op jit(solution)/shard_map/ppermute | solution.py:218
  37.2 0.2 collective-permute-done.18.refs_3_
  37.4 1.7 %collective-permute-start.14 = (bf16[224,256]{1,0:T(8,128)(2,1)S(1)}, bf16[224,256]{1,0:T(8,128)(2,1)S(1)}, u32[]{:S(2)}, u32[]{:S(2)}) collective-permute-start(bf16[224,256]{1,0:T(8,128)(2,1)S(1)} %get-tuple-element.60), channel_id=1, source_target_pairs={{0,3},{1,2},{2,1},{3,0},{4,7},{5,6},{6,5},{7,4},{8,11},{9,10},{10,... | collective-permute-start | bytes 344072 | tf_op jit(solution)/shard_map/ppermute | solution.py:218
  39.1 1.6 %collective-permute-done.19.refs_12_ = bf16[224,1024]{1,0:T(8,128)(2,1)S(1)} collective-permute-done((bf16[224,1024]{1,0:T(8,128)(2,1)S(1)}, bf16[224,1024]{1,0:T(8,128)(2,1)S(1)}, u32[]{:S(2)}, u32[]{:S(2)}) %collective-permute-start.19) | collective-permute-done | bytes 458784 | tf_op jit(solution)/shard_map/ppermute | solution.py:218
  40.7 0.6 shard_map.81.refs_15_
  41.4 2.8 %collective-permute-start.24 = (bf16[224,1024]{1,0:T(8,128)(2,1)S(1)}, bf16[224,1024]{1,0:T(8,128)(2,1)S(1)}, u32[]{:S(2)}, u32[]{:S(2)}) collective-permute-start(bf16[224,1024]{1,0:T(8,128)(2,1)S(1)} %shard_map.81.refs_15_), channel_id=1, source_target_pairs={{0,8},{1,9},{2,10},{3,11},{4,12},{5,13},{6,14},{7,15},{8,0},{9,1},... | collective-permute-start | bytes 1376264 | tf_op jit(solution)/shard_map/ppermute | solution.py:218
  44.2 0.0 collective-permute-done.12.refs_1_
  44.2 0.0 collective-permute-done.13.refs_2_
  44.2 0.0 collective-permute-done.14.refs_3_
  44.2 0.0 collective-permute-done.15.refs_12_.refs_7_
  44.2 0.7 shard_map.82
  44.9 0.0 copy-start
  44.9 1.6 %collective-permute-start.23 = (bf16[224,1024]{1,0:T(8,128)(2,1)S(1)}, bf16[224,1024]{1,0:T(8,128)(2,1)S(1)}, u32[]{:S(2)}, u32[]{:S(2)}) collective-permute-start(bf16[224,1024]{1,0:T(8,128)(2,1)S(1)} %get-tuple-element.74), channel_id=1, source_target_pairs={{0,4},{1,5},{2,6},{3,7},{4,0},{5,1},{6,2},{7,3},{8,12},{9,13},{10,... | collective-permute-start | bytes 1376264 | tf_op jit(solution)/shard_map/ppermute | solution.py:218
  46.5 0.0 collective-permute-start.20
  46.5 1.5 %collective-permute-start.21 = (bf16[224,256]{1,0:T(8,128)(2,1)S(1)}, bf16[224,256]{1,0:T(8,128)(2,1)S(1)}, u32[]{:S(2)}, u32[]{:S(2)}) collective-permute-start(bf16[224,256]{1,0:T(8,128)(2,1)S(1)} %get-tuple-element.70), channel_id=1, source_target_pairs={{0,2},{1,3},{2,0},{3,1},{4,6},{5,7},{6,4},{7,5},{8,10},{9,11},{10,... | collective-permute-start | bytes 344072 | tf_op jit(solution)/shard_map/ppermute | solution.py:218
  48.0 0.3 collective-permute-start.22
  48.4 7.9 %shard_map.83 = (bf16[256,2048]{1,0:T(8,128)(2,1)}, f32[8,128]{1,0:T(8,128)S(1)}, f32[8,128]{1,0:T(8,128)S(1)}) custom-call(f32[128,128]{1,0:T(8,128)S(1)} %get-tuple-element.72.refs_0_, bf16[128,3584]{1,0:T(8,128)(2,1)} %refs_1_.1, bf16[256,2048]{1,0:T(8,128)(2,1)} %bitcast.12, bf16[1024,3584]{1,0:T(8,128)(2,1)} %bitcast.10, ...), custom_call_target="tpu_custom_call" | custom-call | tf_op jit(solution)/shard_map/pallas_call | solution.py:44
  56.3 0.0 collective-permute-done.20.refs_1_
  56.3 1.6 %collective-permute-start.25 = (f32[8,128]{1,0:T(8,128)S(1)}, f32[8,128]{1,0:T(8,128)S(1)}, u32[]{:S(2)}, u32[]{:S(2)}) collective-permute-start(f32[8,128]{1,0:T(8,128)S(1)} %get-tuple-element.76), channel_id=1, source_target_pairs={{0,16},{16,0},{1,17},{17,1},{2,18},{18,2},{3,19},{19,3},{4,20},{20... | collective-permute-start | bytes 12296 | tf_op jit(solution)/shard_map/ppermute | solution.py:217
  57.9 0.0 collective-permute-done.21.refs_2_
  57.9 0.0 collective-permute-done.22.refs_3_
  57.9 0.6 shard_map.84.refs_0_
  58.5 1.5 %collective-permute-done.25.refs_2_ = f32[8,128]{1,0:T(8,128)S(1)} collective-permute-done((f32[8,128]{1,0:T(8,128)S(1)}, f32[8,128]{1,0:T(8,128)S(1)}, u32[]{:S(2)}, u32[]{:S(2)}) %collective-permute-start.25) | collective-permute-done | bytes 4128 | tf_op jit(solution)/shard_map/ppermute | solution.py:217
  60.0 4.3 %collective-permute-done.24.refs_2_.refs_3_ = bf16[224,1024]{1,0:T(8,128)(2,1)S(1)} collective-permute-done((bf16[224,1024]{1,0:T(8,128)(2,1)S(1)}, bf16[224,1024]{1,0:T(8,128)(2,1)S(1)}, u32[]{:S(2)}, u32[]{:S(2)}) %collective-permute-start.24) | collective-permute-done | bytes 458784 | tf_op jit(solution)/shard_map/ppermute | solution.py:218
  64.3 0.6 shard_map.86
  64.8 0.4 collective-permute-done.23.refs_1_
  65.2 1.1 %shard_map.85 = f32[224,1024]{1,0:T(8,128)} custom-call(f32[224,1024]{1,0:T(8,128)S(1)} %shard_map.84.refs_0_, bf16[224,1024]{1,0:T(8,128)(2,1)S(1)} %collective-permute-done.23.refs_1_, bf16[224,1024]{1,0:T(8,128)(2,1)S(1)} %collective-permute-done.24.refs_2_.refs_3_), custom_call_target="tpu_custom_call" | custom-call | tf_op jit(solution)/shard_map/pallas_call | solution.py:44
  (1 shorter events, 0.0 us)
Async XLA Ops:
  2.7 9.3 %collective-permute-start.1 = (bf16[128,1024]{1,0:T(8,128)(2,1)S(1)}, bf16[128,1024]{1,0:T(8,128)(2,1)S(1)}, u32[]{:S(2)}, u32[]{:S(2)}) collective-permute-start(bf16[128,1024]{1,0:T(8,128)(2,1)S(1)} %get-tuple-element.40.refs_3_), channel_id=1, source_target_pairs={{0,16},{16,0},{1,17},{17,1},{2,18},{18,2},{3,19},{19,3},{4,20},{20... | collective-permute-start | bytes 786440 | tf_op jit(solution)/shard_map/ppermute | solution.py:217
  5.7 9.2 %collective-permute-start = (bf16[256,512]{1,0:T(8,128)(2,1)S(1)}, bf16[256,512]{1,0:T(8,128)(2,1)S(1)}, u32[]{:S(2)}, u32[]{:S(2)}) collective-permute-start(bf16[256,512]{1,0:T(8,128)(2,1)S(1)} %get-tuple-element.42.refs_4_), channel_id=1, source_target_pairs={{0,2},{1,3},{2,0},{3,1},{4,6},{5,7},{6,4},{7,5},{8,10},{9,11},{10,... | collective-permute-start | bytes 786440 | tf_op jit(solution)/shard_map/ppermute | solution.py:218
  7.2 11.9 %collective-permute-start.9 = (bf16[256,512]{1,0:T(8,128)(2,1)S(1)}, bf16[256,512]{1,0:T(8,128)(2,1)S(1)}, u32[]{:S(2)}, u32[]{:S(2)}) collective-permute-start(bf16[256,512]{1,0:T(8,128)(2,1)S(1)} %get-tuple-element.51.refs_8_), channel_id=1, source_target_pairs={{0,2},{1,3},{2,0},{3,1},{4,6},{5,7},{6,4},{7,5},{8,10},{9,11},{10,... | collective-permute-start | bytes 786440 | tf_op jit(solution)/shard_map/ppermute | solution.py:218
  14.9 4.2 %collective-permute-start.2 = (bf16[256,512]{1,0:T(8,128)(2,1)S(1)}, bf16[256,512]{1,0:T(8,128)(2,1)S(1)}, u32[]{:S(2)}, u32[]{:S(2)}) collective-permute-start(bf16[256,512]{1,0:T(8,128)(2,1)S(1)} %collective-permute-done.refs_6_), channel_id=1, source_target_pairs={{0,1},{1,0},{2,3},{3,2},{4,5},{5,4},{6,7},{7,6},{8,9},{9,8},{10,11... | collective-permute-start | bytes 786440 | tf_op jit(solution)/shard_map/ppermute | solution.py:218
  14.9 4.7 %collective-permute-start.7 = (bf16[256,512]{1,0:T(8,128)(2,1)S(1)}, bf16[256,512]{1,0:T(8,128)(2,1)S(1)}, u32[]{:S(2)}, u32[]{:S(2)}) collective-permute-start(bf16[256,512]{1,0:T(8,128)(2,1)S(1)} %get-tuple-element.42.refs_4_), channel_id=1, source_target_pairs={{0,1},{1,0},{2,3},{3,2},{4,5},{5,4},{6,7},{7,6},{8,9},{9,8},{10,11... | collective-permute-start | bytes 786440 | tf_op jit(solution)/shard_map/ppermute | solution.py:218
  15.4 6.0 %collective-permute-start.8 = (bf16[256,512]{1,0:T(8,128)(2,1)S(1)}, bf16[256,512]{1,0:T(8,128)(2,1)S(1)}, u32[]{:S(2)}, u32[]{:S(2)}) collective-permute-start(bf16[256,512]{1,0:T(8,128)(2,1)S(1)} %get-tuple-element.51.refs_8_), channel_id=1, source_target_pairs={{0,1},{1,0},{2,3},{3,2},{4,5},{5,4},{6,7},{7,6},{8,9},{9,8},{10,11... | collective-permute-start | bytes 786440 | tf_op jit(solution)/shard_map/ppermute | solution.py:218
  19.1 8.4 %collective-permute-start.10 = (bf16[256,512]{1,0:T(8,128)(2,1)S(1)}, bf16[256,512]{1,0:T(8,128)(2,1)S(1)}, u32[]{:S(2)}, u32[]{:S(2)}) collective-permute-start(bf16[256,512]{1,0:T(8,128)(2,1)S(1)} %collective-permute-done.9.refs_10_), channel_id=1, source_target_pairs={{0,1},{1,0},{2,3},{3,2},{4,5},{5,4},{6,7},{7,6},{8,9},{9,8},{10,11... | collective-permute-start | bytes 786440 | tf_op jit(solution)/shard_map/ppermute | solution.py:218
  19.1 8.4 %collective-permute-start.11 = (bf16[128,896]{1,0:T(8,128)(2,1)S(1)}, bf16[128,896]{1,0:T(8,128)(2,1)S(1)}, u32[]{:S(2)}, u32[]{:S(2)}) collective-permute-start(bf16[128,896]{1,0:T(8,128)(2,1)S(1)} %get-tuple-element.54), channel_id=1, source_target_pairs={{0,16},{16,0},{1,17},{17,1},{2,18},{18,2},{3,19},{19,3},{4,20},{20... | collective-permute-start | bytes 688136 | tf_op jit(solution)/shard_map/ppermute | solution.py:217
  19.4 2.0 %collective-permute-start.4 = (bf16[224,256]{1,0:T(8,128)(2,1)S(1)}, bf16[224,256]{1,0:T(8,128)(2,1)S(1)}, u32[]{:S(2)}, u32[]{:S(2)}) collective-permute-start(bf16[224,256]{1,0:T(8,128)(2,1)S(1)} %get-tuple-element.48), channel_id=1, source_target_pairs={{0,1},{1,0},{2,3},{3,2},{4,5},{5,4},{6,7},{7,6},{8,9},{9,8},{10,11... | collective-permute-start | bytes 344072 | tf_op jit(solution)/shard_map/ppermute | solution.py:218
  19.6 5.9 %collective-permute-start.5 = (bf16[224,256]{1,0:T(8,128)(2,1)S(1)}, bf16[224,256]{1,0:T(8,128)(2,1)S(1)}, u32[]{:S(2)}, u32[]{:S(2)}) collective-permute-start(bf16[224,256]{1,0:T(8,128)(2,1)S(1)} %get-tuple-element.49), channel_id=1, source_target_pairs={{0,2},{1,3},{2,0},{3,1},{4,6},{5,7},{6,4},{7,5},{8,10},{9,11},{10,... | collective-permute-start | bytes 344072 | tf_op jit(solution)/shard_map/ppermute | solution.py:218
  21.4 5.5 %collective-permute-start.6 = (bf16[224,256]{1,0:T(8,128)(2,1)S(1)}, bf16[224,256]{1,0:T(8,128)(2,1)S(1)}, u32[]{:S(2)}, u32[]{:S(2)}) collective-permute-start(bf16[224,256]{1,0:T(8,128)(2,1)S(1)} %get-tuple-element.50), channel_id=1, source_target_pairs={{0,3},{1,2},{2,1},{3,0},{4,7},{5,6},{6,5},{7,4},{8,11},{9,10},{10,... | collective-permute-start | bytes 344072 | tf_op jit(solution)/shard_map/ppermute | solution.py:218
  21.4 10.6 %collective-permute-start.3 = (bf16[128,896]{1,0:T(8,128)(2,1)S(1)}, bf16[128,896]{1,0:T(8,128)(2,1)S(1)}, u32[]{:S(2)}, u32[]{:S(2)}) collective-permute-start(bf16[128,896]{1,0:T(8,128)(2,1)S(1)} %get-tuple-element.46), channel_id=1, source_target_pairs={{0,16},{16,0},{1,17},{17,1},{2,18},{18,2},{3,19},{19,3},{4,20},{20... | collective-permute-start | bytes 688136 | tf_op jit(solution)/shard_map/ppermute | solution.py:217
  28.1 12.6 %collective-permute-start.19 = (bf16[224,1024]{1,0:T(8,128)(2,1)S(1)}, bf16[224,1024]{1,0:T(8,128)(2,1)S(1)}, u32[]{:S(2)}, u32[]{:S(2)}) collective-permute-start(bf16[224,1024]{1,0:T(8,128)(2,1)S(1)} %get-tuple-element.56.refs_3_), channel_id=1, source_target_pairs={{0,4},{1,5},{2,6},{3,7},{4,0},{5,1},{6,2},{7,3},{8,12},{9,13},{10,... | collective-permute-start | bytes 1376264 | tf_op jit(solution)/shard_map/ppermute | solution.py:218
  29.8 3.3 %collective-permute-start.16 = (bf16[224,256]{1,0:T(8,128)(2,1)S(1)}, bf16[224,256]{1,0:T(8,128)(2,1)S(1)}, u32[]{:S(2)}, u32[]{:S(2)}) collective-permute-start(bf16[224,256]{1,0:T(8,128)(2,1)S(1)} %get-tuple-element.65), channel_id=1, source_target_pairs={{0,1},{1,0},{2,3},{3,2},{4,5},{5,4},{6,7},{7,6},{8,9},{9,8},{10,11... | collective-permute-start | bytes 344072 | tf_op jit(solution)/shard_map/ppermute | solution.py:218
  29.8 5.9 %collective-permute-start.17 = (bf16[224,256]{1,0:T(8,128)(2,1)S(1)}, bf16[224,256]{1,0:T(8,128)(2,1)S(1)}, u32[]{:S(2)}, u32[]{:S(2)}) collective-permute-start(bf16[224,256]{1,0:T(8,128)(2,1)S(1)} %get-tuple-element.66), channel_id=1, source_target_pairs={{0,2},{1,3},{2,0},{3,1},{4,6},{5,7},{6,4},{7,5},{8,10},{9,11},{10,... | collective-permute-start | bytes 344072 | tf_op jit(solution)/shard_map/ppermute | solution.py:218
  31.3 6.1 %collective-permute-start.18 = (bf16[224,256]{1,0:T(8,128)(2,1)S(1)}, bf16[224,256]{1,0:T(8,128)(2,1)S(1)}, u32[]{:S(2)}, u32[]{:S(2)}) collective-permute-start(bf16[224,256]{1,0:T(8,128)(2,1)S(1)} %get-tuple-element.67), channel_id=1, source_target_pairs={{0,3},{1,2},{2,1},{3,0},{4,7},{5,6},{6,5},{7,4},{8,11},{9,10},{10,... | collective-permute-start | bytes 344072 | tf_op jit(solution)/shard_map/ppermute | solution.py:218
  32.2 12.0 %collective-permute-start.15 = (bf16[128,896]{1,0:T(8,128)(2,1)S(1)}, bf16[128,896]{1,0:T(8,128)(2,1)S(1)}, u32[]{:S(2)}, u32[]{:S(2)}) collective-permute-start(bf16[128,896]{1,0:T(8,128)(2,1)S(1)} %get-tuple-element.62), channel_id=1, source_target_pairs={{0,16},{16,0},{1,17},{17,1},{2,18},{18,2},{3,19},{19,3},{4,20},{20... | collective-permute-start | bytes 688136 | tf_op jit(solution)/shard_map/ppermute | solution.py:217
  33.1 11.1 %collective-permute-start.12 = (bf16[224,256]{1,0:T(8,128)(2,1)S(1)}, bf16[224,256]{1,0:T(8,128)(2,1)S(1)}, u32[]{:S(2)}, u32[]{:S(2)}) collective-permute-start(bf16[224,256]{1,0:T(8,128)(2,1)S(1)} %get-tuple-element.58), channel_id=1, source_target_pairs={{0,1},{1,0},{2,3},{3,2},{4,5},{5,4},{6,7},{7,6},{8,9},{9,8},{10,11... | collective-permute-start | bytes 344072 | tf_op jit(solution)/shard_map/ppermute | solution.py:218
  35.7 8.5 %collective-permute-start.13 = (bf16[224,256]{1,0:T(8,128)(2,1)S(1)}, bf16[224,256]{1,0:T(8,128)(2,1)S(1)}, u32[]{:S(2)}, u32[]{:S(2)}) collective-permute-start(bf16[224,256]{1,0:T(8,128)(2,1)S(1)} %get-tuple-element.59), channel_id=1, source_target_pairs={{0,2},{1,3},{2,0},{3,1},{4,6},{5,7},{6,4},{7,5},{8,10},{9,11},{10,... | collective-permute-start | bytes 344072 | tf_op jit(solution)/shard_map/ppermute | solution.py:218
  37.4 6.8 %collective-permute-start.14 = (bf16[224,256]{1,0:T(8,128)(2,1)S(1)}, bf16[224,256]{1,0:T(8,128)(2,1)S(1)}, u32[]{:S(2)}, u32[]{:S(2)}) collective-permute-start(bf16[224,256]{1,0:T(8,128)(2,1)S(1)} %get-tuple-element.60), channel_id=1, source_target_pairs={{0,3},{1,2},{2,1},{3,0},{4,7},{5,6},{6,5},{7,4},{8,11},{9,10},{10,... | collective-permute-start | bytes 344072 | tf_op jit(solution)/shard_map/ppermute | solution.py:218
  41.4 22.9 %collective-permute-start.24 = (bf16[224,1024]{1,0:T(8,128)(2,1)S(1)}, bf16[224,1024]{1,0:T(8,128)(2,1)S(1)}, u32[]{:S(2)}, u32[]{:S(2)}) collective-permute-start(bf16[224,1024]{1,0:T(8,128)(2,1)S(1)} %shard_map.81.refs_15_), channel_id=1, source_target_pairs={{0,8},{1,9},{2,10},{3,11},{4,12},{5,13},{6,14},{7,15},{8,0},{9,1},... | collective-permute-start | bytes 1376264 | tf_op jit(solution)/shard_map/ppermute | solution.py:218
  44.9 19.4 %copy-start = (s32[128,2]{0,1:T(2,128)S(1)}, s32[128,2]{0,1:T(2,128)}, u32[]{:S(2)}) copy-start(s32[128,2]{0,1:T(2,128)} %param.7) | copy-start | bytes 3076
  44.9 20.3 %collective-permute-start.23 = (bf16[224,1024]{1,0:T(8,128)(2,1)S(1)}, bf16[224,1024]{1,0:T(8,128)(2,1)S(1)}, u32[]{:S(2)}, u32[]{:S(2)}) collective-permute-start(bf16[224,1024]{1,0:T(8,128)(2,1)S(1)} %get-tuple-element.74), channel_id=1, source_target_pairs={{0,4},{1,5},{2,6},{3,7},{4,0},{5,1},{6,2},{7,3},{8,12},{9,13},{10,... | collective-permute-start | bytes 1376264 | tf_op jit(solution)/shard_map/ppermute | solution.py:218
  46.5 9.8 %collective-permute-start.20 = (bf16[224,256]{1,0:T(8,128)(2,1)S(1)}, bf16[224,256]{1,0:T(8,128)(2,1)S(1)}, u32[]{:S(2)}, u32[]{:S(2)}) collective-permute-start(bf16[224,256]{1,0:T(8,128)(2,1)S(1)} %get-tuple-element.69), channel_id=1, source_target_pairs={{0,1},{1,0},{2,3},{3,2},{4,5},{5,4},{6,7},{7,6},{8,9},{9,8},{10,11... | collective-permute-start | bytes 344072 | tf_op jit(solution)/shard_map/ppermute | solution.py:218
  46.5 11.4 %collective-permute-start.21 = (bf16[224,256]{1,0:T(8,128)(2,1)S(1)}, bf16[224,256]{1,0:T(8,128)(2,1)S(1)}, u32[]{:S(2)}, u32[]{:S(2)}) collective-permute-start(bf16[224,256]{1,0:T(8,128)(2,1)S(1)} %get-tuple-element.70), channel_id=1, source_target_pairs={{0,2},{1,3},{2,0},{3,1},{4,6},{5,7},{6,4},{7,5},{8,10},{9,11},{10,... | collective-permute-start | bytes 344072 | tf_op jit(solution)/shard_map/ppermute | solution.py:218
  48.0 9.8 %collective-permute-start.22 = (bf16[224,256]{1,0:T(8,128)(2,1)S(1)}, bf16[224,256]{1,0:T(8,128)(2,1)S(1)}, u32[]{:S(2)}, u32[]{:S(2)}) collective-permute-start(bf16[224,256]{1,0:T(8,128)(2,1)S(1)} %get-tuple-element.71), channel_id=1, source_target_pairs={{0,3},{1,2},{2,1},{3,0},{4,7},{5,6},{6,5},{7,4},{8,11},{9,10},{10,... | collective-permute-start | bytes 344072 | tf_op jit(solution)/shard_map/ppermute | solution.py:218
  56.3 3.7 %collective-permute-start.25 = (f32[8,128]{1,0:T(8,128)S(1)}, f32[8,128]{1,0:T(8,128)S(1)}, u32[]{:S(2)}, u32[]{:S(2)}) collective-permute-start(f32[8,128]{1,0:T(8,128)S(1)} %get-tuple-element.76), channel_id=1, source_target_pairs={{0,16},{16,0},{1,17},{17,1},{2,18},{18,2},{3,19},{19,3},{4,20},{20... | collective-permute-start | bytes 12296 | tf_op jit(solution)/shard_map/ppermute | solution.py:217

commit v5 on v4

--- a/solution.py
+++ b/solution.py
@@ -88,7 +88,8 @@
 
 
 def own_kernel(order, chunk, up_hbm, ids_ref, weights_ref, *refs):
-    column_ref, refs = refs[0], refs[1:]
+    column_ref, kept_ref, refs = refs[0], refs[1], refs[2:]
+    kept_ref[...] = ids_ref[...]
     own_refs, send_refs = refs[: len(order)], refs[len(order) : -2]
     up_ref, sems = refs[-2:]
     loads = []
@@ -229,10 +230,10 @@
         [pltpu.VMEM((rows, 2 * hidden_units), bf16), pltpu.SemaphoreType.DMA((3,))],
         [HBM, HBM, LOAD, LOAD],
     ))
-    column, *own = call((
+    column, kept, *own = call((
         functools.partial(own_kernel, order, chunk),
         [upstream, ids, combine],
-        [((tokens, LANES), f32)] + [((chunk, tokens), bf16)] * outer + [((tokens, chunk), bf16)] * (outer - 1),
+        [((tokens, LANES), f32), (ids.shape, jnp.int32)] + [((chunk, tokens), bf16)] * outer + [((tokens, chunk), bf16)] * (outer - 1),
         [pltpu.VMEM((outer, tokens, chunk), bf16), pltpu.SemaphoreType.DMA((outer,))],
         [HBM, LOAD, LOAD],
     ), waits=(first,))
@@ -294,7 +295,7 @@
     )
     back_score = cross(got_score)
     base, = call(parts(3, f32, (hidden_units,)), waits=(own_score,))
-    grad_probs, = call((probs_kernel, [ids, own_score, back_score], [(ids.shape, f32)], [], None), waits=last)
+    grad_probs, = call((probs_kernel, [kept, own_score, back_score], [(ids.shape, f32)], [], None), waits=last)
     grad_down, = call((
         functools.partial(final_kernel, len(side)), [base, *side, *last],
         [((piece, hidden_units), f32)], [], None,

time: 66.5 us -> 67.6 us (1.017)
  waiting for transfers between devices: 23.4 us -> 25.6 us
  starting transfers between devices: 25.2 us -> 24.2 us
    ppermute x21, waiting for transfers between devices: 18.9 us -> 22.5 us  [both_experts(): lax.ppermute(value, 'dp', [(i, i ^ bit) for i in range(n)])]
    ppermute x5, waiting for transfers between devices: 4.48 us -> 3.01 us  [both_experts(): cross = lambda value: lax.ppermute(value, 'expert', flip)]
    ppermute x21, starting transfers between devices: 17.9 us -> 16.8 us  [both_experts(): lax.ppermute(value, 'dp', [(i, i ^ bit) for i in range(n)])]
  transfers between devices with their start and end apart: 26 -> 26, of which waited for: 13 -> 12; matrix products, arithmetic and copies ran while one was open for 0% -> 0% of each run, Pallas kernels for 21% -> 20%
where the time goes in v5:
time: 67.6 us; the launch traced here: 67.4 us
  waiting for transfers between devices  25.6 us (38%)
  starting transfers between devices  24.2 us (36%)
  Pallas kernels  16.9 us (25%)
  between operations  0.75 us (1%)
    ppermute x21, waiting for transfers between devices, both_experts(): lax.ppermute(value, 'dp', [(i, i ^ bit) for i in range(n)])  22.5 us
    pallas_call x11, Pallas kernels, call(): pl.pallas_call(body, out_shape=outs, in_specs=specs + [ANY] * len(waits),...  16.9 us
    ppermute x21, starting transfers between devices, both_experts(): lax.ppermute(value, 'dp', [(i, i ^ bit) for i in range(n)])  16.8 us
    ppermute x5, starting transfers between devices, both_experts(): cross = lambda value: lax.ppermute(value, 'expert', flip)  7.36 us
    ppermute x5, waiting for transfers between devices, both_experts(): cross = lambda value: lax.ppermute(value, 'expert', flip)  3.01 us
  transfers between devices with their start and end apart: 26, of which 12 were waited for; matrix products, arithmetic and copies ran while one was open for 0% of the time, Pallas kernels for 20%

profile of v5, /device:TPU:0, one launch (start us, length us, event | category | flops | bytes accessed | tf_op | source)
XLA Modules:
  0.0 67.4 jit_solution(12746990443436432477)
XLA Ops:
  0.6 2.0 %shard_map.76 = (bf16[128,1024]{1,0:T(8,128)(2,1)S(1)}, bf16[256,512]{1,0:T(8,128)(2,1)S(1)}, bf16[256,512]{1,0:T(8,128)(2,1)S(1)}) custom-call(bf16[128,3584]{1,0:T(8,128)(2,1)} %refs_1_.1, bf16[256,2048]{1,0:T(8,128)(2,1)} %bitcast.8, s32[2,128]{1,0:T(2,128)} %bitcast.11, bf16[2,128]{1,0:T(2,128)(2,1)} %bitcast.13), custom_call_target="tpu_custom_call" | custom-call | tf_op jit(solution)/shard_map/pallas_call | solution.py:44
  2.7 3.0 %collective-permute-start.1 = (bf16[128,1024]{1,0:T(8,128)(2,1)S(1)}, bf16[128,1024]{1,0:T(8,128)(2,1)S(1)}, u32[]{:S(2)}, u32[]{:S(2)}) collective-permute-start(bf16[128,1024]{1,0:T(8,128)(2,1)S(1)} %get-tuple-element.41.refs_3_), channel_id=1, source_target_pairs={{0,16},{16,0},{1,17},{17,1},{2,18},{18,2},{3,19},{19,3},{4,20},{20... | collective-permute-start | bytes 786440 | tf_op jit(solution)/shard_map/ppermute | solution.py:218
  5.7 1.5 %collective-permute-start = (bf16[256,512]{1,0:T(8,128)(2,1)S(1)}, bf16[256,512]{1,0:T(8,128)(2,1)S(1)}, u32[]{:S(2)}, u32[]{:S(2)}) collective-permute-start(bf16[256,512]{1,0:T(8,128)(2,1)S(1)} %get-tuple-element.43.refs_4_), channel_id=1, source_target_pairs={{0,2},{1,3},{2,0},{3,1},{4,6},{5,7},{6,4},{7,5},{8,10},{9,11},{10,... | collective-permute-start | bytes 786440 | tf_op jit(solution)/shard_map/ppermute | solution.py:219
  7.2 0.5 collective-permute-start.9
  7.7 2.3 %shard_map.77 = (f32[128,128]{1,0:T(8,128)S(1)}, s32[2,128]{1,0:T(2,128)S(1)}, bf16[896,128]{1,0:T(8,128)(2,1)S(1)}, bf16[896,128]{1,0:T(8,128)(2,1)S(1)}, bf16[...) custom-call(bf16[128,3584]{1,0:T(8,128)(2,1)} %refs_1_.1, ...), custom_call_target="tpu_custom_call" | custom-call | tf_op jit(solution)/shard_map/pallas_call | solution.py:44
  10.0 2.0 %collective-permute-done.1.refs_0_.refs_1_.refs_13_.refs_4_ = bf16[128,1024]{1,0:T(8,128)(2,1)S(1)} collective-permute-done((bf16[128,1024]{1,0:T(8,128)(2,1)S(1)}, bf16[128,1024]{1,0:T(8,128)(2,1)S(1)}, u32[]{:S(2)}, u32[]{:S(2)}) %collective-permute-start.1) | collective-permute-done | bytes 262176 | tf_op jit(solution)/shard_map/ppermute | solution.py:218
  12.0 0.2 shard_map.78
  12.2 2.7 %collective-permute-done.refs_6_ = bf16[256,512]{1,0:T(8,128)(2,1)S(1)} collective-permute-done((bf16[256,512]{1,0:T(8,128)(2,1)S(1)}, bf16[256,512]{1,0:T(8,128)(2,1)S(1)}, u32[]{:S(2)}, u32[]{:S(2)}) %collective-permute-start) | collective-permute-done | bytes 262176 | tf_op jit(solution)/shard_map/ppermute | solution.py:219
  14.9 0.0 collective-permute-start.2
  14.9 0.5 collective-permute-start.7
  15.4 0.0 collective-permute-start.8
  15.4 3.6 %collective-permute-done.9.refs_10_ = bf16[256,512]{1,0:T(8,128)(2,1)S(1)} collective-permute-done((bf16[256,512]{1,0:T(8,128)(2,1)S(1)}, bf16[256,512]{1,0:T(8,128)(2,1)S(1)}, u32[]{:S(2)}, u32[]{:S(2)}) %collective-permute-start.9) | collective-permute-done | bytes 262176 | tf_op jit(solution)/shard_map/ppermute | solution.py:219
  19.1 0.0 collective-permute-done.2.refs_7_
  19.1 0.0 collective-permute-start.10
  19.1 0.4 collective-permute-start.11
  19.4 0.2 collective-permute-start.4
  19.6 0.0 collective-permute-done.7.refs_5_
  19.6 1.7 %collective-permute-start.5 = (bf16[224,256]{1,0:T(8,128)(2,1)S(1)}, bf16[224,256]{1,0:T(8,128)(2,1)S(1)}, u32[]{:S(2)}, u32[]{:S(2)}) collective-permute-start(bf16[224,256]{1,0:T(8,128)(2,1)S(1)} %get-tuple-element.50), channel_id=1, source_target_pairs={{0,2},{1,3},{2,0},{3,1},{4,6},{5,7},{6,4},{7,5},{8,10},{9,11},{10,... | collective-permute-start | bytes 344072 | tf_op jit(solution)/shard_map/ppermute | solution.py:219
  21.4 0.0 collective-permute-done.8.refs_9_
  21.4 0.0 collective-permute-start.6
  21.4 0.0 collective-permute-done.4.refs_1_
  21.4 1.6 %collective-permute-start.3 = (bf16[128,896]{1,0:T(8,128)(2,1)S(1)}, bf16[128,896]{1,0:T(8,128)(2,1)S(1)}, u32[]{:S(2)}, u32[]{:S(2)}) collective-permute-start(bf16[128,896]{1,0:T(8,128)(2,1)S(1)} %get-tuple-element.47), channel_id=1, source_target_pairs={{0,16},{16,0},{1,17},{17,1},{2,18},{18,2},{3,19},{19,3},{4,20},{20... | collective-permute-start | bytes 688136 | tf_op jit(solution)/shard_map/ppermute | solution.py:218
  23.0 2.6 %collective-permute-done.5.refs_2_ = bf16[224,256]{1,0:T(8,128)(2,1)S(1)} collective-permute-done((bf16[224,256]{1,0:T(8,128)(2,1)S(1)}, bf16[224,256]{1,0:T(8,128)(2,1)S(1)}, u32[]{:S(2)}, u32[]{:S(2)}) %collective-permute-start.5) | collective-permute-done | bytes 114720 | tf_op jit(solution)/shard_map/ppermute | solution.py:219
  25.6 1.2 %collective-permute-done.6.refs_3_ = bf16[224,256]{1,0:T(8,128)(2,1)S(1)} collective-permute-done((bf16[224,256]{1,0:T(8,128)(2,1)S(1)}, bf16[224,256]{1,0:T(8,128)(2,1)S(1)}, u32[]{:S(2)}, u32[]{:S(2)}) %collective-permute-start.6) | collective-permute-done | bytes 114720 | tf_op jit(solution)/shard_map/ppermute | solution.py:219
  26.8 0.6 collective-permute-done.11.refs_12_.refs_5_
  27.5 0.0 collective-permute-done.10.refs_11_
  27.5 0.6 shard_map.79
  28.1 1.6 %collective-permute-start.19 = (bf16[224,1024]{1,0:T(8,128)(2,1)S(1)}, bf16[224,1024]{1,0:T(8,128)(2,1)S(1)}, u32[]{:S(2)}, u32[]{:S(2)}) collective-permute-start(bf16[224,1024]{1,0:T(8,128)(2,1)S(1)} %get-tuple-element.57.refs_3_), channel_id=1, source_target_pairs={{0,4},{1,5},{2,6},{3,7},{4,0},{5,1},{6,2},{7,3},{8,12},{9,13},{10,... | collective-permute-start | bytes 1376264 | tf_op jit(solution)/shard_map/ppermute | solution.py:219
  29.8 0.0 collective-permute-start.16
  29.8 1.5 %collective-permute-start.17 = (bf16[224,256]{1,0:T(8,128)(2,1)S(1)}, bf16[224,256]{1,0:T(8,128)(2,1)S(1)}, u32[]{:S(2)}, u32[]{:S(2)}) collective-permute-start(bf16[224,256]{1,0:T(8,128)(2,1)S(1)} %get-tuple-element.67), channel_id=1, source_target_pairs={{0,2},{1,3},{2,0},{3,1},{4,6},{5,7},{6,4},{7,5},{8,10},{9,11},{10,... | collective-permute-start | bytes 344072 | tf_op jit(solution)/shard_map/ppermute | solution.py:219
  31.3 0.3 collective-permute-start.18
  31.6 0.4 collective-permute-done.3.refs_0_.refs_6_
  32.0 0.2 shard_map.80
  32.2 0.8 %collective-permute-start.15 = (bf16[128,896]{1,0:T(8,128)(2,1)S(1)}, bf16[128,896]{1,0:T(8,128)(2,1)S(1)}, u32[]{:S(2)}, u32[]{:S(2)}) collective-permute-start(bf16[128,896]{1,0:T(8,128)(2,1)S(1)} %get-tuple-element.63), channel_id=1, source_target_pairs={{0,16},{16,0},{1,17},{17,1},{2,18},{18,2},{3,19},{19,3},{4,20},{20... | collective-permute-start | bytes 688136 | tf_op jit(solution)/shard_map/ppermute | solution.py:218
  33.1 0.0 collective-permute-done.16.refs_1_
  33.1 0.3 collective-permute-start.12
  33.4 2.3 %collective-permute-done.17.refs_2_ = bf16[224,256]{1,0:T(8,128)(2,1)S(1)} collective-permute-done((bf16[224,256]{1,0:T(8,128)(2,1)S(1)}, bf16[224,256]{1,0:T(8,128)(2,1)S(1)}, u32[]{:S(2)}, u32[]{:S(2)}) %collective-permute-start.17) | collective-permute-done | bytes 114720 | tf_op jit(solution)/shard_map/ppermute | solution.py:219
  35.7 1.5 %collective-permute-start.13 = (bf16[224,256]{1,0:T(8,128)(2,1)S(1)}, bf16[224,256]{1,0:T(8,128)(2,1)S(1)}, u32[]{:S(2)}, u32[]{:S(2)}) collective-permute-start(bf16[224,256]{1,0:T(8,128)(2,1)S(1)} %get-tuple-element.60), channel_id=1, source_target_pairs={{0,2},{1,3},{2,0},{3,1},{4,6},{5,7},{6,4},{7,5},{8,10},{9,11},{10,... | collective-permute-start | bytes 344072 | tf_op jit(solution)/shard_map/ppermute | solution.py:219
  37.2 0.2 collective-permute-done.18.refs_3_
  37.4 1.7 %collective-permute-start.14 = (bf16[224,256]{1,0:T(8,128)(2,1)S(1)}, bf16[224,256]{1,0:T(8,128)(2,1)S(1)}, u32[]{:S(2)}, u32[]{:S(2)}) collective-permute-start(bf16[224,256]{1,0:T(8,128)(2,1)S(1)} %get-tuple-element.61), channel_id=1, source_target_pairs={{0,3},{1,2},{2,1},{3,0},{4,7},{5,6},{6,5},{7,4},{8,11},{9,10},{10,... | collective-permute-start | bytes 344072 | tf_op jit(solution)/shard_map/ppermute | solution.py:219
  39.1 1.6 %collective-permute-done.19.refs_12_ = bf16[224,1024]{1,0:T(8,128)(2,1)S(1)} collective-permute-done((bf16[224,1024]{1,0:T(8,128)(2,1)S(1)}, bf16[224,1024]{1,0:T(8,128)(2,1)S(1)}, u32[]{:S(2)}, u32[]{:S(2)}) %collective-permute-start.19) | collective-permute-done | bytes 458784 | tf_op jit(solution)/shard_map/ppermute | solution.py:219
  40.7 0.6 shard_map.81.refs_15_
  41.4 0.0 collective-permute-done.12.refs_1_
  41.4 0.0 collective-permute-done.13.refs_2_
  41.4 1.0 %collective-permute-done.14.refs_3_ = bf16[224,256]{1,0:T(8,128)(2,1)S(1)} collective-permute-done((bf16[224,256]{1,0:T(8,128)(2,1)S(1)}, bf16[224,256]{1,0:T(8,128)(2,1)S(1)}, u32[]{:S(2)}, u32[]{:S(2)}) %collective-permute-start.14) | collective-permute-done | bytes 114720 | tf_op jit(solution)/shard_map/ppermute | solution.py:219
  42.4 0.0 collective-permute-done.15.refs_12_.refs_7_
  42.4 0.6 shard_map.82
  43.0 0.9 %collective-permute-start.23 = (bf16[224,1024]{1,0:T(8,128)(2,1)S(1)}, bf16[224,1024]{1,0:T(8,128)(2,1)S(1)}, u32[]{:S(2)}, u32[]{:S(2)}) collective-permute-start(bf16[224,1024]{1,0:T(8,128)(2,1)S(1)} %get-tuple-element.75), channel_id=1, source_target_pairs={{0,4},{1,5},{2,6},{3,7},{4,0},{5,1},{6,2},{7,3},{8,12},{9,13},{10,... | collective-permute-start | bytes 1376264 | tf_op jit(solution)/shard_map/ppermute | solution.py:219
  43.9 2.6 %collective-permute-start.24 = (bf16[224,1024]{1,0:T(8,128)(2,1)S(1)}, bf16[224,1024]{1,0:T(8,128)(2,1)S(1)}, u32[]{:S(2)}, u32[]{:S(2)}) collective-permute-start(bf16[224,1024]{1,0:T(8,128)(2,1)S(1)} %shard_map.81.refs_15_), channel_id=1, source_target_pairs={{0,8},{1,9},{2,10},{3,11},{4,12},{5,13},{6,14},{7,15},{8,0},{9,1},... | collective-permute-start | bytes 1376264 | tf_op jit(solution)/shard_map/ppermute | solution.py:219
  46.5 0.0 collective-permute-start.20
  46.5 1.5 %collective-permute-start.21 = (bf16[224,256]{1,0:T(8,128)(2,1)S(1)}, bf16[224,256]{1,0:T(8,128)(2,1)S(1)}, u32[]{:S(2)}, u32[]{:S(2)}) collective-permute-start(bf16[224,256]{1,0:T(8,128)(2,1)S(1)} %get-tuple-element.71), channel_id=1, source_target_pairs={{0,2},{1,3},{2,0},{3,1},{4,6},{5,7},{6,4},{7,5},{8,10},{9,11},{10,... | collective-permute-start | bytes 344072 | tf_op jit(solution)/shard_map/ppermute | solution.py:219
  48.0 0.3 collective-permute-start.22
  48.3 7.9 %shard_map.83 = (bf16[256,2048]{1,0:T(8,128)(2,1)}, f32[8,128]{1,0:T(8,128)S(1)}, f32[8,128]{1,0:T(8,128)S(1)}) custom-call(f32[128,128]{1,0:T(8,128)S(1)} %get-tuple-element.73.refs_0_, bf16[128,3584]{1,0:T(8,128)(2,1)} %refs_1_.1, bf16[256,2048]{1,0:T(8,128)(2,1)} %bitcast.9, bf16[1024,3584]{1,0:T(8,128)(2,1)} %bitcast.7, ...), custom_call_target="tpu_custom_call" | custom-call | tf_op jit(solution)/shard_map/pallas_call | solution.py:44
  56.2 0.0 collective-permute-done.20.refs_1_
  56.3 1.6 %collective-permute-start.25 = (f32[8,128]{1,0:T(8,128)S(1)}, f32[8,128]{1,0:T(8,128)S(1)}, u32[]{:S(2)}, u32[]{:S(2)}) collective-permute-start(f32[8,128]{1,0:T(8,128)S(1)} %get-tuple-element.78), channel_id=1, source_target_pairs={{0,16},{16,0},{1,17},{17,1},{2,18},{18,2},{3,19},{19,3},{4,20},{20... | collective-permute-start | bytes 12296 | tf_op jit(solution)/shard_map/ppermute | solution.py:218
  57.8 0.0 collective-permute-done.21.refs_2_
  57.8 0.0 collective-permute-done.22.refs_3_
  57.8 0.6 shard_map.84.refs_0_
  58.5 7.3 %collective-permute-done.23.refs_1_ = bf16[224,1024]{1,0:T(8,128)(2,1)S(1)} collective-permute-done((bf16[224,1024]{1,0:T(8,128)(2,1)S(1)}, bf16[224,1024]{1,0:T(8,128)(2,1)S(1)}, u32[]{:S(2)}, u32[]{:S(2)}) %collective-permute-start.23) | collective-permute-done | bytes 458784 | tf_op jit(solution)/shard_map/ppermute | solution.py:219
  65.8 0.0 collective-permute-done.24.refs_2_.refs_3_
  65.8 1.1 %shard_map.85 = f32[224,1024]{1,0:T(8,128)} custom-call(f32[224,1024]{1,0:T(8,128)S(1)} %shard_map.84.refs_0_, bf16[224,1024]{1,0:T(8,128)(2,1)S(1)} %collective-permute-done.23.refs_1_, bf16[224,1024]{1,0:T(8,128)(2,1)S(1)} %collective-permute-done.24.refs_2_.refs_3_), custom_call_target="tpu_custom_call" | custom-call | tf_op jit(solution)/shard_map/pallas_call | solution.py:44
  66.8 0.0 collective-permute-done.25.refs_2_
  66.8 0.6 shard_map.86
Async XLA Ops:
  2.7 9.3 %collective-permute-start.1 = (bf16[128,1024]{1,0:T(8,128)(2,1)S(1)}, bf16[128,1024]{1,0:T(8,128)(2,1)S(1)}, u32[]{:S(2)}, u32[]{:S(2)}) collective-permute-start(bf16[128,1024]{1,0:T(8,128)(2,1)S(1)} %get-tuple-element.41.refs_3_), channel_id=1, source_target_pairs={{0,16},{16,0},{1,17},{17,1},{2,18},{18,2},{3,19},{19,3},{4,20},{20... | collective-permute-start | bytes 786440 | tf_op jit(solution)/shard_map/ppermute | solution.py:218
  5.7 9.2 %collective-permute-start = (bf16[256,512]{1,0:T(8,128)(2,1)S(1)}, bf16[256,512]{1,0:T(8,128)(2,1)S(1)}, u32[]{:S(2)}, u32[]{:S(2)}) collective-permute-start(bf16[256,512]{1,0:T(8,128)(2,1)S(1)} %get-tuple-element.43.refs_4_), channel_id=1, source_target_pairs={{0,2},{1,3},{2,0},{3,1},{4,6},{5,7},{6,4},{7,5},{8,10},{9,11},{10,... | collective-permute-start | bytes 786440 | tf_op jit(solution)/shard_map/ppermute | solution.py:219
  7.2 11.9 %collective-permute-start.9 = (bf16[256,512]{1,0:T(8,128)(2,1)S(1)}, bf16[256,512]{1,0:T(8,128)(2,1)S(1)}, u32[]{:S(2)}, u32[]{:S(2)}) collective-permute-start(bf16[256,512]{1,0:T(8,128)(2,1)S(1)} %get-tuple-element.52.refs_8_), channel_id=1, source_target_pairs={{0,2},{1,3},{2,0},{3,1},{4,6},{5,7},{6,4},{7,5},{8,10},{9,11},{10,... | collective-permute-start | bytes 786440 | tf_op jit(solution)/shard_map/ppermute | solution.py:219
  14.9 4.2 %collective-permute-start.2 = (bf16[256,512]{1,0:T(8,128)(2,1)S(1)}, bf16[256,512]{1,0:T(8,128)(2,1)S(1)}, u32[]{:S(2)}, u32[]{:S(2)}) collective-permute-start(bf16[256,512]{1,0:T(8,128)(2,1)S(1)} %collective-permute-done.refs_6_), channel_id=1, source_target_pairs={{0,1},{1,0},{2,3},{3,2},{4,5},{5,4},{6,7},{7,6},{8,9},{9,8},{10,11... | collective-permute-start | bytes 786440 | tf_op jit(solution)/shard_map/ppermute | solution.py:219
  14.9 4.7 %collective-permute-start.7 = (bf16[256,512]{1,0:T(8,128)(2,1)S(1)}, bf16[256,512]{1,0:T(8,128)(2,1)S(1)}, u32[]{:S(2)}, u32[]{:S(2)}) collective-permute-start(bf16[256,512]{1,0:T(8,128)(2,1)S(1)} %get-tuple-element.43.refs_4_), channel_id=1, source_target_pairs={{0,1},{1,0},{2,3},{3,2},{4,5},{5,4},{6,7},{7,6},{8,9},{9,8},{10,11... | collective-permute-start | bytes 786440 | tf_op jit(solution)/shard_map/ppermute | solution.py:219
  15.4 6.0 %collective-permute-start.8 = (bf16[256,512]{1,0:T(8,128)(2,1)S(1)}, bf16[256,512]{1,0:T(8,128)(2,1)S(1)}, u32[]{:S(2)}, u32[]{:S(2)}) collective-permute-start(bf16[256,512]{1,0:T(8,128)(2,1)S(1)} %get-tuple-element.52.refs_8_), channel_id=1, source_target_pairs={{0,1},{1,0},{2,3},{3,2},{4,5},{5,4},{6,7},{7,6},{8,9},{9,8},{10,11... | collective-permute-start | bytes 786440 | tf_op jit(solution)/shard_map/ppermute | solution.py:219
  19.1 8.4 %collective-permute-start.10 = (bf16[256,512]{1,0:T(8,128)(2,1)S(1)}, bf16[256,512]{1,0:T(8,128)(2,1)S(1)}, u32[]{:S(2)}, u32[]{:S(2)}) collective-permute-start(bf16[256,512]{1,0:T(8,128)(2,1)S(1)} %collective-permute-done.9.refs_10_), channel_id=1, source_target_pairs={{0,1},{1,0},{2,3},{3,2},{4,5},{5,4},{6,7},{7,6},{8,9},{9,8},{10,11... | collective-permute-start | bytes 786440 | tf_op jit(solution)/shard_map/ppermute | solution.py:219
  19.1 8.4 %collective-permute-start.11 = (bf16[128,896]{1,0:T(8,128)(2,1)S(1)}, bf16[128,896]{1,0:T(8,128)(2,1)S(1)}, u32[]{:S(2)}, u32[]{:S(2)}) collective-permute-start(bf16[128,896]{1,0:T(8,128)(2,1)S(1)} %get-tuple-element.55), channel_id=1, source_target_pairs={{0,16},{16,0},{1,17},{17,1},{2,18},{18,2},{3,19},{19,3},{4,20},{20... | collective-permute-start | bytes 688136 | tf_op jit(solution)/shard_map/ppermute | solution.py:218
  19.4 2.0 %collective-permute-start.4 = (bf16[224,256]{1,0:T(8,128)(2,1)S(1)}, bf16[224,256]{1,0:T(8,128)(2,1)S(1)}, u32[]{:S(2)}, u32[]{:S(2)}) collective-permute-start(bf16[224,256]{1,0:T(8,128)(2,1)S(1)} %get-tuple-element.49), channel_id=1, source_target_pairs={{0,1},{1,0},{2,3},{3,2},{4,5},{5,4},{6,7},{7,6},{8,9},{9,8},{10,11... | collective-permute-start | bytes 344072 | tf_op jit(solution)/shard_map/ppermute | solution.py:219
  19.6 5.9 %collective-permute-start.5 = (bf16[224,256]{1,0:T(8,128)(2,1)S(1)}, bf16[224,256]{1,0:T(8,128)(2,1)S(1)}, u32[]{:S(2)}, u32[]{:S(2)}) collective-permute-start(bf16[224,256]{1,0:T(8,128)(2,1)S(1)} %get-tuple-element.50), channel_id=1, source_target_pairs={{0,2},{1,3},{2,0},{3,1},{4,6},{5,7},{6,4},{7,5},{8,10},{9,11},{10,... | collective-permute-start | bytes 344072 | tf_op jit(solution)/shard_map/ppermute | solution.py:219
  21.4 5.5 %collective-permute-start.6 = (bf16[224,256]{1,0:T(8,128)(2,1)S(1)}, bf16[224,256]{1,0:T(8,128)(2,1)S(1)}, u32[]{:S(2)}, u32[]{:S(2)}) collective-permute-start(bf16[224,256]{1,0:T(8,128)(2,1)S(1)} %get-tuple-element.51), channel_id=1, source_target_pairs={{0,3},{1,2},{2,1},{3,0},{4,7},{5,6},{6,5},{7,4},{8,11},{9,10},{10,... | collective-permute-start | bytes 344072 | tf_op jit(solution)/shard_map/ppermute | solution.py:219
  21.4 10.6 %collective-permute-start.3 = (bf16[128,896]{1,0:T(8,128)(2,1)S(1)}, bf16[128,896]{1,0:T(8,128)(2,1)S(1)}, u32[]{:S(2)}, u32[]{:S(2)}) collective-permute-start(bf16[128,896]{1,0:T(8,128)(2,1)S(1)} %get-tuple-element.47), channel_id=1, source_target_pairs={{0,16},{16,0},{1,17},{17,1},{2,18},{18,2},{3,19},{19,3},{4,20},{20... | collective-permute-start | bytes 688136 | tf_op jit(solution)/shard_map/ppermute | solution.py:218
  28.1 12.6 %collective-permute-start.19 = (bf16[224,1024]{1,0:T(8,128)(2,1)S(1)}, bf16[224,1024]{1,0:T(8,128)(2,1)S(1)}, u32[]{:S(2)}, u32[]{:S(2)}) collective-permute-start(bf16[224,1024]{1,0:T(8,128)(2,1)S(1)} %get-tuple-element.57.refs_3_), channel_id=1, source_target_pairs={{0,4},{1,5},{2,6},{3,7},{4,0},{5,1},{6,2},{7,3},{8,12},{9,13},{10,... | collective-permute-start | bytes 1376264 | tf_op jit(solution)/shard_map/ppermute | solution.py:219
  29.8 3.3 %collective-permute-start.16 = (bf16[224,256]{1,0:T(8,128)(2,1)S(1)}, bf16[224,256]{1,0:T(8,128)(2,1)S(1)}, u32[]{:S(2)}, u32[]{:S(2)}) collective-permute-start(bf16[224,256]{1,0:T(8,128)(2,1)S(1)} %get-tuple-element.66), channel_id=1, source_target_pairs={{0,1},{1,0},{2,3},{3,2},{4,5},{5,4},{6,7},{7,6},{8,9},{9,8},{10,11... | collective-permute-start | bytes 344072 | tf_op jit(solution)/shard_map/ppermute | solution.py:219
  29.8 5.9 %collective-permute-start.17 = (bf16[224,256]{1,0:T(8,128)(2,1)S(1)}, bf16[224,256]{1,0:T(8,128)(2,1)S(1)}, u32[]{:S(2)}, u32[]{:S(2)}) collective-permute-start(bf16[224,256]{1,0:T(8,128)(2,1)S(1)} %get-tuple-element.67), channel_id=1, source_target_pairs={{0,2},{1,3},{2,0},{3,1},{4,6},{5,7},{6,4},{7,5},{8,10},{9,11},{10,... | collective-permute-start | bytes 344072 | tf_op jit(solution)/shard_map/ppermute | solution.py:219
  31.3 6.1 %collective-permute-start.18 = (bf16[224,256]{1,0:T(8,128)(2,1)S(1)}, bf16[224,256]{1,0:T(8,128)(2,1)S(1)}, u32[]{:S(2)}, u32[]{:S(2)}) collective-permute-start(bf16[224,256]{1,0:T(8,128)(2,1)S(1)} %get-tuple-element.68), channel_id=1, source_target_pairs={{0,3},{1,2},{2,1},{3,0},{4,7},{5,6},{6,5},{7,4},{8,11},{9,10},{10,... | collective-permute-start | bytes 344072 | tf_op jit(solution)/shard_map/ppermute | solution.py:219
  32.2 10.1 %collective-permute-start.15 = (bf16[128,896]{1,0:T(8,128)(2,1)S(1)}, bf16[128,896]{1,0:T(8,128)(2,1)S(1)}, u32[]{:S(2)}, u32[]{:S(2)}) collective-permute-start(bf16[128,896]{1,0:T(8,128)(2,1)S(1)} %get-tuple-element.63), channel_id=1, source_target_pairs={{0,16},{16,0},{1,17},{17,1},{2,18},{18,2},{3,19},{19,3},{4,20},{20... | collective-permute-start | bytes 688136 | tf_op jit(solution)/shard_map/ppermute | solution.py:218
  33.1 8.3 %collective-permute-start.12 = (bf16[224,256]{1,0:T(8,128)(2,1)S(1)}, bf16[224,256]{1,0:T(8,128)(2,1)S(1)}, u32[]{:S(2)}, u32[]{:S(2)}) collective-permute-start(bf16[224,256]{1,0:T(8,128)(2,1)S(1)} %get-tuple-element.59), channel_id=1, source_target_pairs={{0,1},{1,0},{2,3},{3,2},{4,5},{5,4},{6,7},{7,6},{8,9},{9,8},{10,11... | collective-permute-start | bytes 344072 | tf_op jit(solution)/shard_map/ppermute | solution.py:219
  35.7 5.7 %collective-permute-start.13 = (bf16[224,256]{1,0:T(8,128)(2,1)S(1)}, bf16[224,256]{1,0:T(8,128)(2,1)S(1)}, u32[]{:S(2)}, u32[]{:S(2)}) collective-permute-start(bf16[224,256]{1,0:T(8,128)(2,1)S(1)} %get-tuple-element.60), channel_id=1, source_target_pairs={{0,2},{1,3},{2,0},{3,1},{4,6},{5,7},{6,4},{7,5},{8,10},{9,11},{10,... | collective-permute-start | bytes 344072 | tf_op jit(solution)/shard_map/ppermute | solution.py:219
  37.4 5.0 %collective-permute-start.14 = (bf16[224,256]{1,0:T(8,128)(2,1)S(1)}, bf16[224,256]{1,0:T(8,128)(2,1)S(1)}, u32[]{:S(2)}, u32[]{:S(2)}) collective-permute-start(bf16[224,256]{1,0:T(8,128)(2,1)S(1)} %get-tuple-element.61), channel_id=1, source_target_pairs={{0,3},{1,2},{2,1},{3,0},{4,7},{5,6},{6,5},{7,4},{8,11},{9,10},{10,... | collective-permute-start | bytes 344072 | tf_op jit(solution)/shard_map/ppermute | solution.py:219
  43.0 22.8 %collective-permute-start.23 = (bf16[224,1024]{1,0:T(8,128)(2,1)S(1)}, bf16[224,1024]{1,0:T(8,128)(2,1)S(1)}, u32[]{:S(2)}, u32[]{:S(2)}) collective-permute-start(bf16[224,1024]{1,0:T(8,128)(2,1)S(1)} %get-tuple-element.75), channel_id=1, source_target_pairs={{0,4},{1,5},{2,6},{3,7},{4,0},{5,1},{6,2},{7,3},{8,12},{9,13},{10,... | collective-permute-start | bytes 1376264 | tf_op jit(solution)/shard_map/ppermute | solution.py:219
  43.9 21.9 %collective-permute-start.24 = (bf16[224,1024]{1,0:T(8,128)(2,1)S(1)}, bf16[224,1024]{1,0:T(8,128)(2,1)S(1)}, u32[]{:S(2)}, u32[]{:S(2)}) collective-permute-start(bf16[224,1024]{1,0:T(8,128)(2,1)S(1)} %shard_map.81.refs_15_), channel_id=1, source_target_pairs={{0,8},{1,9},{2,10},{3,11},{4,12},{5,13},{6,14},{7,15},{8,0},{9,1},... | collective-permute-start | bytes 1376264 | tf_op jit(solution)/shard_map/ppermute | solution.py:219
  46.5 9.8 %collective-permute-start.20 = (bf16[224,256]{1,0:T(8,128)(2,1)S(1)}, bf16[224,256]{1,0:T(8,128)(2,1)S(1)}, u32[]{:S(2)}, u32[]{:S(2)}) collective-permute-start(bf16[224,256]{1,0:T(8,128)(2,1)S(1)} %get-tuple-element.70), channel_id=1, source_target_pairs={{0,1},{1,0},{2,3},{3,2},{4,5},{5,4},{6,7},{7,6},{8,9},{9,8},{10,11... | collective-permute-start | bytes 344072 | tf_op jit(solution)/shard_map/ppermute | solution.py:219
  46.5 11.4 %collective-permute-start.21 = (bf16[224,256]{1,0:T(8,128)(2,1)S(1)}, bf16[224,256]{1,0:T(8,128)(2,1)S(1)}, u32[]{:S(2)}, u32[]{:S(2)}) collective-permute-start(bf16[224,256]{1,0:T(8,128)(2,1)S(1)} %get-tuple-element.71), channel_id=1, source_target_pairs={{0,2},{1,3},{2,0},{3,1},{4,6},{5,7},{6,4},{7,5},{8,10},{9,11},{10,... | collective-permute-start | bytes 344072 | tf_op jit(solution)/shard_map/ppermute | solution.py:219
  48.0 9.8 %collective-permute-start.22 = (bf16[224,256]{1,0:T(8,128)(2,1)S(1)}, bf16[224,256]{1,0:T(8,128)(2,1)S(1)}, u32[]{:S(2)}, u32[]{:S(2)}) collective-permute-start(bf16[224,256]{1,0:T(8,128)(2,1)S(1)} %get-tuple-element.72), channel_id=1, source_target_pairs={{0,3},{1,2},{2,1},{3,0},{4,7},{5,6},{6,5},{7,4},{8,11},{9,10},{10,... | collective-permute-start | bytes 344072 | tf_op jit(solution)/shard_map/ppermute | solution.py:219
  56.3 10.6 %collective-permute-start.25 = (f32[8,128]{1,0:T(8,128)S(1)}, f32[8,128]{1,0:T(8,128)S(1)}, u32[]{:S(2)}, u32[]{:S(2)}) collective-permute-start(f32[8,128]{1,0:T(8,128)S(1)} %get-tuple-element.78), channel_id=1, source_target_pairs={{0,16},{16,0},{1,17},{17,1},{2,18},{18,2},{3,19},{19,3},{4,20},{20... | collective-permute-start | bytes 12296 | tf_op jit(solution)/shard_map/ppermute | solution.py:218
